TPU v7x, 32 devices: a whole 2x2x4 slice. The times are simulated.
32 devices in a mesh: dp: 8 (over y, x, core), mp: 4 (over z).
Axes of the slice: x: 2, y: 2, z: 4, core: 2. Of those that a mesh axis runs over, the one named last changes fastest.
Arguments:
- activations: bfloat16 [8192, 1280], P(('dp', 'mp')), may hold values from -6 to 6
- cotangent: bfloat16 [8192, 1280], P(('dp', 'mp')), may hold values from -6 to 6
- doc_lengths: int32 [8, 8], P('dp'), may hold values from 1 to 512, 1024 in all within a row
- w_in: float32 [4, 1280, 1280], P(None, 'dp', 'mp'), may hold values from -0.15625 to 0.15625
- w_attn_out: float32 [1280, 1280], P('mp', 'dp'), may hold values from -1.25 to 1.25
- w_down: float32 [1280, 1280], P('mp', 'dp'), may hold values from -0.15625 to 0.15625
- gains: float32 [2, 1280], replicated, may hold values from 0.5 to 1.5
- scale_param: float32 [80], replicated, may hold values from 0.5 to 2.5
- mom_in: float32 [4, 1280, 1280], P(None, 'dp', 'mp'), may hold values from -3 to 3
- mom_out: float32 [2, 1280, 1280], P(None, 'mp', 'dp'), may hold values from -3 to 3
- mom_gain: float32 [2, 1280], replicated, may hold values from -6 to 6
- mom_scale: float32 [80], replicated, may hold values from -6 to 6
- error_buffer: float32 [8, 6, 1280, 1280], P('dp', None, 'mp'), may hold values from -1.5 to 1.5
- factors: float32 [6, 1280, 8], P(None, 'mp'), may hold values from -6 to 6
Outputs:
- output: bfloat16 [8192, 1280], P(('dp', 'mp'))
- grad_input: float32 [8192, 1280], P(('dp', 'mp'))
- grad_in: float32 [4, 1280, 1280], P(None, 'dp', 'mp')
- grad_out: float32 [2, 1280, 1280], P(None, 'mp', 'dp')
- grad_gain: float32 [2, 1280], replicated
- grad_scale: float32 [80], replicated
- new_in: float32 [4, 1280, 1280], P(None, 'dp', 'mp')
- new_out: float32 [2, 1280, 1280], P(None, 'mp', 'dp')
- new_gain: float32 [2, 1280], replicated
- new_scale: float32 [80], replicated
- mom_in_new: float32 [4, 1280, 1280], P(None, 'dp', 'mp')
- mom_out_new: float32 [2, 1280, 1280], P(None, 'mp', 'dp')
- mom_gain_new: float32 [2, 1280], replicated
- mom_scale_new: float32 [80], replicated
- error_new: float32 [8, 6, 1280, 1280], P('dp', None, 'mp')
- factors_new: float32 [6, 1280, 8], P(None, 'mp')
Inputs may be any that keep to these rules, and one draw needn't show every extreme that they name: `doc_lengths`: each row gives 8 document lengths that fill one sequence of 1024 tokens; in each row the longest is exactly 512.
All inputs are finite; a program needn't handle non-finite values.
Results may differ from a plain program's by a relative error of at most 0.014.
The roundings to bfloat16 on the way count: a program that leaves them out, or rounds other values in their place, can miss the bound.
Values may be sent and summed in bfloat16 or wider, within the bound.
A program may use at most 192 MiB of HBM per device.

v0:
```python
import math

import jax
import jax.numpy as jnp
from jax import lax
from jax.sharding import PartitionSpec as P

HD = 80


HIGHEST = lax.Precision.HIGHEST
EPSILON = 1e-06
SCALE_BASE = 1.442695041
MOMENTUM = 0.9
RATE = 0.1
MASKED_SCORE = -1e30


def rms_scale(values):
    return lax.rsqrt(jnp.mean(values * values, axis=-1, keepdims=True) + EPSILON)


def norm_back(grad_normed, unit, scale, gain):
    grad_gain = jnp.sum(grad_normed * unit, axis=0)
    grad_unit = grad_normed * gain
    grad_values = scale * (grad_unit - unit * jnp.mean(grad_unit * unit, axis=-1, keepdims=True))
    return (grad_gain, grad_values)


def silu_slope(gate):
    sigmoid = jax.nn.sigmoid(gate)
    return sigmoid * (1.0 + gate * (1.0 - sigmoid))


def segment_ids(lengths, count):
    ends = jnp.cumsum(lengths)
    position = jnp.arange(count, dtype=jnp.int32)
    return jnp.sum((position[:, None] >= ends[None, :]).astype(jnp.int32), axis=1)


def orthonormal(matrix):
    columns = []
    for index in range(matrix.shape[-1]):
        vector = matrix[..., index]
        for basis in columns:
            vector = vector - jnp.sum(basis * vector, axis=-1, keepdims=True) * basis
        vector = vector * lax.rsqrt(jnp.sum(vector * vector, axis=-1, keepdims=True) + 1e-12)
        columns.append(vector)
    return jnp.stack(columns, axis=-1)


def score_block(query, start, keys, segments):
    rows = query.shape[1]
    scores = jnp.einsum("hqd,hkd->hqk", query, keys, preferred_element_type=jnp.float32)
    query_pos = start + jnp.arange(rows, dtype=jnp.int32)
    key_pos = jnp.arange(keys.shape[1], dtype=jnp.int32)
    query_seg = lax.dynamic_slice_in_dim(segments, start, rows)
    allowed = (key_pos[None, :] <= query_pos[:, None]) & (segments[None, :] == query_seg[:, None])
    return jnp.where(allowed[None], scores, MASKED_SCORE)


def forward_block(query, start, keys, values, segments):
    masked = score_block(query, start, keys, segments)
    highest = jnp.max(masked, axis=-1, keepdims=True)
    raised = jnp.exp(masked - highest)
    total = jnp.sum(raised, axis=-1, keepdims=True)
    probability = (raised / total).astype(jnp.bfloat16)
    attended = jnp.einsum("hqk,hkd->hqd", probability, values, preferred_element_type=jnp.float32)
    return (attended.astype(jnp.bfloat16), highest + jnp.log(total))


def backward_block(query, start, grad_attended, log_total, keys, values, segments):
    masked = score_block(query, start, keys, segments)
    probability = jnp.exp(masked - log_total)
    grad_prob = jnp.einsum(
        "hqd,hkd->hqk", grad_attended, values, preferred_element_type=jnp.float32
    )
    inner = jnp.sum(probability * grad_prob, axis=-1, keepdims=True)
    grad_scores = (probability * (grad_prob - inner)).astype(jnp.bfloat16)
    grad_query = jnp.einsum("hqk,hkd->hqd", grad_scores, keys, preferred_element_type=jnp.float32)
    grad_keys = jnp.einsum("hqk,hqd->hkd", grad_scores, query, preferred_element_type=jnp.float32)
    grad_values = jnp.einsum(
        "hqk,hqd->hkd",
        probability.astype(jnp.bfloat16),
        grad_attended,
        preferred_element_type=jnp.float32,
    )
    return (grad_query, grad_keys, grad_values)


def on_device(
    activations,
    cotangent,
    doc_lengths,
    w_in,
    w_attn_out,
    w_down,
    gains,
    scale_param,
    mom_in,
    mom_out,
    mom_gain,
    mom_scale,
    error_buffer,
    factors,
):
    rows_tok = activations.shape[0]
    model_par = lax.axis_size("mp")
    data_par = lax.axis_size("dp")
    my_data = lax.axis_index("dp")
    count = rows_tok * model_par
    scaling = (rows_tok * model_par * data_par) ** (-0.5)
    columns = w_in.shape[2]
    local_heads = columns // HD
    block = min(512, count)
    block_count = count // block
    w_in_half, w_out_half, w_down_half = (
        lax.all_gather(w_in.astype(jnp.bfloat16), "dp", axis=1, tiled=True),
        lax.all_gather(w_attn_out.astype(jnp.bfloat16), "dp", axis=1, tiled=True),
        lax.all_gather(w_down.astype(jnp.bfloat16), "dp", axis=1, tiled=True),
    )
    w_qkv = w_in_half[:3]
    w_up = w_in_half[3]
    segments = segment_ids(doc_lengths[0], count)
    factor = SCALE_BASE / math.sqrt(HD) * jax.nn.softplus(scale_param)
    factor_cols = jnp.tile(factor, local_heads)

    def to_heads(table):
        return table.reshape(count, local_heads, HD).transpose(1, 0, 2)

    def from_heads(table):
        return table.transpose(1, 0, 2).reshape(count, columns)

    def to_blocks(table):
        return to_heads(table).reshape(local_heads, block_count, block, HD).transpose(1, 0, 2, 3)

    def from_blocks(table):
        return from_heads(table.transpose(1, 0, 2, 3).reshape(local_heads, count, HD))

    inputs = activations.astype(jnp.float32)
    scale_one = rms_scale(inputs)
    unit_one = inputs * scale_one
    normed = (unit_one * gains[0]).astype(jnp.bfloat16)
    normed_all = lax.all_gather(normed, "mp", axis=0, tiled=True)
    projected = jnp.einsum("sd,kdc->ksc", normed_all, w_qkv, preferred_element_type=jnp.float32)
    query_raw = projected[0]
    query = (query_raw * factor_cols).astype(jnp.bfloat16)
    key_heads = to_heads(projected[1].astype(jnp.bfloat16))
    value_heads = to_heads(projected[2].astype(jnp.bfloat16))
    query_blocks = to_blocks(query)
    starts = jnp.arange(block_count, dtype=jnp.int32) * block
    attended_blocks, log_total = lax.map(
        lambda item: forward_block(item[0], item[1], key_heads, value_heads, segments),
        (query_blocks, starts),
    )
    attended = from_blocks(attended_blocks)
    middle = inputs + lax.psum_scatter(
        jnp.dot(attended, w_out_half, preferred_element_type=jnp.float32),
        "mp",
        scatter_dimension=0,
        tiled=True,
    )
    scale_two = rms_scale(middle)
    unit_two = middle * scale_two
    normed_two = (unit_two * gains[1]).astype(jnp.bfloat16)
    normed_two_all = lax.all_gather(normed_two, "mp", axis=0, tiled=True)
    gate = jnp.dot(normed_two_all, w_up, preferred_element_type=jnp.float32)
    hidden = jax.nn.silu(gate).astype(jnp.bfloat16)
    result = middle + lax.psum_scatter(
        jnp.dot(hidden, w_down_half, preferred_element_type=jnp.float32).astype(jnp.bfloat16),
        "mp",
        scatter_dimension=0,
        tiled=True,
    ).astype(jnp.float32)
    cotangent_all = lax.all_gather(cotangent, "mp", axis=0, tiled=True)
    grad_hidden = jnp.dot(cotangent_all, w_down_half.T, preferred_element_type=jnp.float32)
    grad_down = jnp.dot(hidden.T, cotangent_all, preferred_element_type=jnp.float32)
    grad_gate = (grad_hidden * silu_slope(gate)).astype(jnp.bfloat16)
    grad_up = jnp.dot(normed_two_all.T, grad_gate, preferred_element_type=jnp.float32)
    grad_normed_two = lax.psum_scatter(
        jnp.dot(grad_gate, w_up.T, preferred_element_type=jnp.float32),
        "mp",
        scatter_dimension=0,
        tiled=True,
    )
    grad_gain_two, grad_middle = norm_back(grad_normed_two, unit_two, scale_two, gains[1])
    grad_middle = cotangent.astype(jnp.float32) + grad_middle
    branch_grad_all = lax.all_gather(grad_middle.astype(jnp.bfloat16), "mp", axis=0, tiled=True)
    grad_out_proj = jnp.dot(attended.T, branch_grad_all, preferred_element_type=jnp.float32)
    grad_attended = jnp.dot(
        branch_grad_all, w_out_half.T, preferred_element_type=jnp.float32
    ).astype(jnp.bfloat16)
    grad_blocks = to_blocks(grad_attended)

    def back_step(carry, item):
        query_block, start, grad_block, total_block = item
        grad_query, grad_keys, grad_values = backward_block(
            query_block, start, grad_block, total_block, key_heads, value_heads, segments
        )
        return ((carry[0] + grad_keys, carry[1] + grad_values), grad_query)

    zeros = jnp.zeros((local_heads, count, HD), jnp.float32)
    (grad_keys, grad_values), grad_query_blocks = lax.scan(
        back_step, (zeros, zeros), (query_blocks, starts, grad_blocks, log_total)
    )
    grad_query = from_blocks(grad_query_blocks)
    grad_factor_cols = jnp.sum(grad_query * query_raw, axis=0)
    grad_scale_local = (
        jnp.sum(grad_factor_cols.reshape(local_heads, HD), axis=0)
        * (SCALE_BASE / math.sqrt(HD))
        * jax.nn.sigmoid(scale_param)
    )
    grad_projected = jnp.stack(
        [grad_query * factor_cols, from_heads(grad_keys), from_heads(grad_values)]
    ).astype(jnp.bfloat16)
    grad_qkv = jnp.einsum(
        "sd,ksc->kdc", normed_all, grad_projected, preferred_element_type=jnp.float32
    )
    grad_normed = lax.psum_scatter(
        jnp.einsum("ksc,kdc->sd", grad_projected, w_qkv, preferred_element_type=jnp.float32),
        "mp",
        scatter_dimension=0,
        tiled=True,
    )
    grad_gain_one, grad_inputs = norm_back(grad_normed, unit_one, scale_one, gains[0])
    grad_input = grad_middle + grad_inputs
    local_in = scaling * jnp.concatenate([grad_qkv, grad_up[None]], axis=0)
    local_out = scaling * jnp.stack([grad_out_proj, grad_down])
    grad_in, grad_out = (
        lax.psum_scatter(local_in, "dp", scatter_dimension=1, tiled=True),
        lax.psum_scatter(local_out, "dp", scatter_dimension=2, tiled=True),
    )
    matrices = jnp.concatenate([local_in, jnp.swapaxes(local_out, 1, 2)], axis=0) + jnp.swapaxes(
        error_buffer[0], 1, 2
    )
    left_local = jnp.einsum("kdc,kcr->kdr", matrices, factors, precision=HIGHEST)
    gain_local = scaling * jnp.stack([grad_gain_one, grad_gain_two])
    left, grad_gain, grad_scale = lax.psum(
        (left_local, gain_local, scaling * grad_scale_local), ("dp", "mp")
    )
    basis = orthonormal(left)
    right = lax.psum(jnp.einsum("kdc,kdr->kcr", matrices, basis, precision=HIGHEST), "dp")
    approx = jnp.einsum("kdr,kcr->kdc", basis, right, precision=HIGHEST)
    error_new = jnp.swapaxes(matrices - approx, 1, 2)[None]
    own_rows = approx.shape[1] // data_par
    mine = lax.dynamic_slice_in_dim(approx, my_data * own_rows, own_rows, 1)
    mom_in_new = MOMENTUM * mom_in + mine[:4]
    new_in = w_in - RATE * mom_in_new
    mom_out_new = MOMENTUM * mom_out + jnp.swapaxes(mine[4:], 1, 2)
    new_out = jnp.stack([w_attn_out, w_down]) - RATE * mom_out_new
    mom_gain_new = MOMENTUM * mom_gain + grad_gain
    new_gain = gains - RATE * mom_gain_new
    mom_scale_new = MOMENTUM * mom_scale + grad_scale
    new_scale = scale_param - RATE * mom_scale_new
    return (
        result.astype(jnp.bfloat16),
        grad_input,
        grad_in,
        grad_out,
        grad_gain,
        grad_scale,
        new_in,
        new_out,
        new_gain,
        new_scale,
        mom_in_new,
        mom_out_new,
        mom_gain_new,
        mom_scale_new,
        error_new,
        right,
    )


def solution(mesh):
    return jax.shard_map(
        on_device,
        mesh=mesh,
        in_specs=(
            P(("dp", "mp"), None),
            P(("dp", "mp"), None),
            P("dp", None),
            P(None, "dp", "mp"),
            P("mp", "dp"),
            P("mp", "dp"),
            P(),
            P(),
            P(None, "dp", "mp"),
            P(None, "mp", "dp"),
            P(),
            P(),
            P("dp", None, "mp", None),
            P(None, "mp", None),
        ),
        out_specs=(
            P(("dp", "mp"), None),
            P(("dp", "mp"), None),
            P(None, "dp", "mp"),
            P(None, "mp", "dp"),
            P(),
            P(),
            P(None, "dp", "mp"),
            P(None, "mp", "dp"),
            P(),
            P(),
            P(None, "dp", "mp"),
            P(None, "mp", "dp"),
            P(),
            P(),
            P("dp", None, "mp", None),
            P(None, "mp", None),
        ),
        check_vma=False,
    )
```

profile of v0, /device:TPU:0, one launch (start us, length us, event | category | flops | bytes accessed | tf_op | source)
XLA Modules:
  0.0 1032.8 jit_solution(1922712841941297722)
XLA Ops:
  7.3 2.7 copy.574
  11.9 12.3 %all_gather.23 = bf16[320,1280]{0,1:T(8,128)(2,1)S(1)} all-gather(bf16[320,160]{0,1:T(8,128)(2,1)S(1)} %convert_element_type.79), channel_id=1, replica_groups=mesh['dp'=8,'mp'=4] {'dp'}, dimensions={1}, use_global_device_ids=true | all-gather | bytes 921600 | tf_op jit(solution)/shard_map/all_gather | solution.py:119
  24.2 24.6 %all-gather.8.cloned.1.call-done = bf16[4,1280,320]{2,0,1:T(4,128)(2,1)} async-done(((bf16[4,160,320]{2,0,1:T(4,128)(2,1)}), bf16[4,1280,320]{2,0,1:T(4,128)(2,1)}) %all-gather.8.cloned.1.call-update) | async-done | bytes 3276816 | tf_op jit(solution)/shard_map/all_gather | solution.py:118
  48.8 7.5 copy.233
  56.2 49.5 %all-gather.6.cloned.1.call-done = bf16[1024,1280]{1,0:T(8,128)(2,1)} async-done(((bf16[256,1280]{1,0:T(8,128)(2,1)}), bf16[1024,1280]{1,0:T(8,128)(2,1)}) %all-gather.6.cloned.1.call-update) | async-done | bytes 2621456 | tf_op jit(solution)/shard_map/all_gather | solution.py:144
  105.7 5.2 fusion.111
  114.9 22.2 %while.27 = (s32[]{:T(128)}, bf16[2,4,512,80]{2,3,1,0:T(8,128)(2,1)}, f32[2,4,512,1]{2,1,3,0:T(4,128)S(1)}, s32[2]{0:T(128)S(1)}, s32[1024]{0:T(1024)S(1)}, /*in...) while((s32[]{:T(128)}, ...), condition=%wide.region_6.7_spmd, body=%wide.region_3.6_spmd.sunk | while | flops 691698176 | bytes 34552044 | solution.py:152
  118.7 1.6 select_reduce_fusion.2
  120.3 2.3 fusion.162
  122.6 2.6 fusion.163
  129.8 1.6 select_reduce_fusion.2
  131.4 2.3 fusion.162
  133.6 2.6 fusion.163
  139.1 3.9 fusion.112
  143.1 92.7 %reduce-scatter.5.cloned.1.call-done = f32[256,1280]{1,0:T(8,128)} async-done(((f32[1024,1280]{1,0:T(8,128)}), f32[256,1280]{1,0:T(8,128)}) %reduce-scatter.5.cloned.1.call-update) | async-done | bytes 1310736 | tf_op jit(solution)/shard_map/reduce_scatter | solution.py:157
  235.8 1.7 multiply_reduce_fusion.3
  240.4 12.0 %all_gather.25 = bf16[320,1280]{0,1:T(8,128)(2,1)} all-gather(bf16[320,160]{0,1:T(8,128)(2,1)S(1)} %convert_element_type.82), channel_id=1, replica_groups=mesh['dp'=8,'mp'=4] {'dp'}, dimensions={1}, use_global_device_ids=true | all-gather | bytes 921600 | tf_op jit(solution)/shard_map/all_gather | solution.py:120
  252.4 5.1 slice.76
  257.5 4.8 copy.234
  262.4 31.8 %all-gather.10.cloned.1.call-done = bf16[1024,1280]{1,0:T(8,128)(2,1)} async-done(((bf16[256,1280]{1,0:T(8,128)(2,1)}), bf16[1024,1280]{1,0:T(8,128)(2,1)}) %all-gather.10.cloned.1.call-update) | async-done | bytes 2621456 | tf_op jit(solution)/shard_map/all_gather | solution.py:166
  294.2 4.0 fusion.59
  298.2 50.9 %all-gather.12.cloned.1.call-done = bf16[1024,1280]{1,0:T(8,128)(2,1)} async-done(((bf16[256,1280]{1,0:T(8,128)(2,1)}), bf16[1024,1280]{1,0:T(8,128)(2,1)}) %all-gather.12.cloned.1.call-update) | async-done | bytes 2621456 | tf_op jit(solution)/shard_map/all_gather | solution.py:175
  349.1 3.8 fusion.47
  353.8 3.9 fusion.57
  357.7 92.7 %reduce-scatter.9.cloned.1.call-done = f32[256,1280]{1,0:T(8,128)} async-done(((f32[1024,1280]{1,0:T(8,128)}), f32[256,1280]{1,0:T(8,128)}) %reduce-scatter.9.cloned.1.call-update) | async-done | bytes 1310736 | tf_op jit(solution)/shard_map/reduce_scatter | solution.py:180
  450.4 2.5 multiply_reduce_fusion.1
  454.9 4.3 convolution_bitcast_fusion.3
  459.2 2.4 convolution_bitcast_fusion.4
  461.6 48.6 %all-gather.14.cloned.1.call-done = bf16[1024,1280]{1,0:T(8,128)(2,1)} async-done(((bf16[256,1280]{1,0:T(8,128)(2,1)}), bf16[1024,1280]{1,0:T(8,128)(2,1)}) %all-gather.14.cloned.1.call-update) | async-done | bytes 2621456 | tf_op jit(solution)/shard_map/all_gather | solution.py:188
  510.2 3.9 convolution_convert_fusion.1
  514.0 3.3 reshape.1026
  517.4 2.0 copy.194
  519.4 33.6 %while.28 = (s32[]{:T(128)}, f32[4,1024,80]{1,2,0:T(8,128)S(1)}, f32[4,1024,80]{1,2,0:T(8,128)}, f32[2,4,512,80]{2,3,1,0:T(8,128)}, s32[2]{0:T(128)S(1)}, /*inde...) while((s32[]{:T(128)}, f32[4,1024,80]{1,2,0:T(8,128)S(1)}, ...), condition=%wide.region_14.15_spmd.clone, body=%wide.region_12.14_spmd.clone.sunk | while | flops 1705769472 | bytes 97851760 | solution.py:203
  524.6 2.5 fusion.175
  527.1 3.0 multiply_reduce_fusion.33
  530.1 2.1 multiply_convert_fusion.7
  541.4 2.5 fusion.175
  543.8 3.0 multiply_reduce_fusion.33
  546.9 2.1 multiply_convert_fusion.7
  557.1 2.7 convolution_bitcast_fusion.2
  562.8 3.5 copy-done.24
  566.4 2.2 fusion.105
  568.6 1.8 copy-done.2
  570.4 6.2 fusion.107
  576.6 9.6 copy.196
  586.2 7.5 copy.197
  595.2 6.4 convolution_bitcast_fusion.1
  607.2 2.7 copy.198
  611.1 4.5 convolution_convert_fusion
  617.2 83.5 %all-reduce.7.cloned.1.call-done = f32[6,1280,8]{1,2,0:T(8,128)} async-done(((f32[6,1280,8]{1,2,0:T(8,128)}), f32[6,1280,8]{1,2,0:T(8,128)}) %all-reduce.7.cloned.1.call-update) | async-done | bytes 245776 | tf_op jit(solution)/shard_map/psum | solution.py:238
  701.8 2.3 fusion.110
  708.1 1.8 subtract_multiply_fusion
  710.3 13.1 %fusion.106 = f32[6,320,8]{1,2,0:T(8,128)S(1)} fusion(f32[6,1280,8]{1,2,0:T(8,128)S(1)} %stack.50, f32[2,1280,320]{1,2,0:T(8,128)} %copy-done.2, f32[4,1280,320]{1,2,0:T(8,128)} %copy-done.1, f32[1,6,320,1280]{3,2,1,0:T(8,128)} %param.30), kind=kOutput, calls=%fused_computation.251 | convolution fusion | flops 240844800 | bytes 19968000 | tf_op jit(solution)/shard_map/kdc,kdr->kcr/dot_general | solution.py:242
  723.4 28.7 %psum.31 = f32[6,320,8]{1,2,0:T(8,128)S(1)} all-reduce(f32[6,320,8]{1,2,0:T(8,128)S(1)} %fusion.106), channel_id=1, replica_groups=mesh['dp'=8,'mp'=4] {'dp'}, use_global_device_ids=true, to_apply=%region_61.62 | all-reduce | flops 15360 | bytes 122880 | tf_op jit(solution)/shard_map/psum | solution.py:242
  752.1 7.9 fusion.113
  760.0 3.9 copy-done.3
  765.7 1.7 maximum_subtract_fusion
  770.8 14.6 %subtract_bitcast_fusion = f32[1,6,320,1280]{3,2,1,0:T(8,128)} fusion(f32[6,1280,320]{1,2,0:T(8,128)} %copy-done.3, f32[1,6,320,1280]{3,2,1,0:T(8,128)} %param.30, f32[2,1280,320]{1,2,0:T(8,128)} %copy-done.2, f32[4,1280,320]{1,2,0:T(8,128)} %copy-done.1), kind=kLoop, calls=%fused_computation.49 | loop fusion | flops 7372800 | bytes 39321600 | tf_op jit(solution)/shard_map/broadcast_in_dim | solution.py:244
  785.4 84.6 %all-reduce.9.cloned.1.call-done = (f32[4,1280,320]{2,0,1:T(4,128)}, f32[2,320,1280]{1,0,2:T(2,128)}) async-done(((f32[4,1280,320]{2,0,1:T(4,128)}, f32[2,320,1280]{1,0,2:T(2,128)}), (f32[4,1280,320]{2,0,1:T(4,128)}, f32[2,320,1280]{1,0,2:T(2,128)})) %all-reduce.9.cloned.1.call-update) | async-done | bytes 9830416
  874.6 91.5 %reduce-scatter.11.cloned.1.call-done = f32[256,1280]{1,0:T(8,128)} async-done(((f32[1024,1280]{1,0:T(8,128)}), f32[256,1280]{1,0:T(8,128)}) %reduce-scatter.11.cloned.1.call-update) | async-done | bytes 1310736 | tf_op jit(solution)/shard_map/reduce_scatter | solution.py:219
  966.1 1.8 fusion.53
  967.9 44.2 %all-reduce.2 = (f32[2,1280]{1,0:T(2,128)S(1)}, f32[80]{0:T(128)S(1)}) all-reduce(f32[2,1280]{1,0:T(2,128)S(1)} %maximum_multiply_fusion.2, f32[80]{0:T(128)S(1)} %fusion.101), channel_id=1, replica_groups=mesh['dp'=8,'mp'=4] {'dp','mp'}, use_global_device_ids=true, to_apply=%region_21.22 | all-reduce | flops 2640 | bytes 21120 | tf_op jit(solution)/shard_map/psum | solution.py:238
  1013.3 8.8 reduce-scatter.7.cloned.1.call-done
  1022.1 3.7 fusion.52
  (287 shorter events, 65.4 us)
Async XLA Ops:
  7.2 563.2 %copy-start = (f32[6,320,8]{1,2,0:T(8,128)S(1)}, f32[6,320,8]{1,2,0:T(8,128)}, u32[]{:S(2)}) copy-start(f32[6,320,8]{1,2,0:T(8,128)} %param.31) | copy-start | bytes 184324
  7.2 2.9 copy-start.46
  7.2 2.9 copy-start.10
  7.2 4.3 copy-start.64
  7.2 4.5 copy-start.30
  7.2 41.6 %all-gather.8.cloned.1.call-start = ((), (), s32[]{:S(2)}) async-start(), calls=%async_computation.5 | async-start | bytes 4423680 | tf_op jit(solution)/shard_map/all_gather | solution.py:118
  10.0 95.7 %all-gather.6.cloned.1.call-start = ((), (), s32[]{:S(2)}) async-start(), calls=%async_computation.4 | async-start | bytes 3276800 | tf_op jit(solution)/shard_map/all_gather | solution.py:144
  10.1 1.6 copy-start.44
  10.1 442.8 %copy-start.42 = (f32[1280]{0:T(1024)}, f32[1280]{0:T(1024)S(1)}, u32[]{:S(2)}) copy-start(f32[1280]{0:T(1024)S(1)} %get-tuple-element.346) | copy-start | bytes 15364
  10.1 14.0 %copy-start.57 = (f32[80]{0:T(128)S(1)}, f32[80]{0:T(128)}, u32[]{:S(2)}) copy-start(f32[80]{0:T(128)} %param.25) | copy-start | bytes 964
  11.5 224.3 %reduce-scatter.5.cloned.1.call-start = ((), (), s32[]{:S(2)}) async-start(), calls=%async_computation.6 | async-start | bytes 6553600 | tf_op jit(solution)/shard_map/reduce_scatter | solution.py:157
  24.2 114.1 %copy-start.22 = (bf16[320,1280]{0,1:T(8,128)(2,1)}, bf16[320,1280]{0,1:T(8,128)(2,1)S(1)}, u32[]{:S(2)}) copy-start(bf16[320,1280]{0,1:T(8,128)(2,1)S(1)} %all_gather.23) | copy-start | bytes 2457604
  120.3 2.3 copy-start.35
  131.3 2.3 copy-start.35
  143.1 151.1 %all-gather.10.cloned.1.call-start = ((), (), s32[]{:S(2)}) async-start(), calls=%async_computation.7 | async-start | bytes 3276800 | tf_op jit(solution)/shard_map/all_gather | solution.py:166
  237.5 215.4 %copy-start.7 = (f32[256,1280]{1,0:T(8,128)}, f32[256,1280]{1,0:T(8,128)S(1)}, u32[]{:S(2)}) copy-start(f32[256,1280]{1,0:T(8,128)S(1)} %get-tuple-element.417) | copy-start | bytes 3932164
  237.5 215.4 %copy-start.49 = (f32[256]{0:T(256)}, f32[256]{0:T(256)S(1)}, u32[]{:S(2)}) copy-start(f32[256]{0:T(256)S(1)} %add_rsqrt_fusion) | copy-start | bytes 3076
  238.8 110.4 %all-gather.12.cloned.1.call-start = ((), (), s32[]{:S(2)}) async-start(), calls=%async_computation.9 | async-start | bytes 3276800 | tf_op jit(solution)/shard_map/all_gather | solution.py:175
  239.4 211.0 %reduce-scatter.9.cloned.1.call-start = ((), (), s32[]{:S(2)}) async-start(), calls=%async_computation.10 | async-start | bytes 6553600 | tf_op jit(solution)/shard_map/reduce_scatter | solution.py:180
  349.1 4.6 copy-start.23
  357.7 152.5 %all-gather.14.cloned.1.call-start = ((), (), s32[]{:S(2)}) async-start(), calls=%async_computation.11 | async-start | bytes 3276800 | tf_op jit(solution)/shard_map/all_gather | solution.py:188
  450.4 3.0 copy-start.12
  450.4 3.0 copy-start.16
  454.8 246.0 %all-reduce.7.cloned.1.call-start = ((), (), s32[]{:S(2)}) async-start(), calls=%async_computation.13 | async-start | bytes 491520 | tf_op jit(solution)/shard_map/psum | solution.py:238
  454.9 4.3 copy-start.63
  454.9 4.3 copy-start.66
  527.1 3.0 copy-start.5
  543.8 3.0 copy-start.5
  553.0 1.7 copy-start.6
  554.7 2.4 copy-start.61
  557.1 2.7 copy-start.25
  559.8 1.9 copy-start.62
  559.8 10.5 %slice-start = ((s8[9830400]{0:T(1024)(128)(4,1)}), s8[4194304]{0:T(1024)(128)(4,1)S(1)}, s32[]{:S(2)}) async-start(s8[9830400]{0:T(1024)(128)(4,1)} %bitcast.498), calls=%async_computation.15 | async-start | bytes 8388608
  559.9 10.5 %slice-start.1 = ((s8[9830400]{0:T(1024)(128)(4,1)}), s8[4194304]{0:T(1024)(128)(4,1)S(1)}, s32[]{:S(2)}) async-start(s8[9830400]{0:T(1024)(128)(4,1)} %bitcast.498), calls=%async_computation.16 | async-start | bytes 8388608
  561.8 6.8 copy-start.1
  561.8 4.6 copy-start.24
  566.4 4.0 slice-start.2
  568.6 1.8 copy-start.2
  576.6 293.5 %all-reduce.9.cloned.1.call-start = ((), (), s32[]{:S(2)}) async-start(), calls=%async_computation.14 | async-start | bytes 23592960
  593.7 1.5 copy-start.40
  593.8 372.4 %reduce-scatter.11.cloned.1.call-start = ((), (), s32[]{:S(2)}) async-start(), calls=%async_computation.12 | async-start | bytes 6553600 | tf_op jit(solution)/shard_map/reduce_scatter | solution.py:219
  601.6 1.8 copy-start.32
  601.6 2.7 copy-start.21
  601.6 420.5 %reduce-scatter.7.cloned.1.call-start = ((), (), s32[]{:S(2)}) async-start(), calls=%async_computation.8 | async-start | bytes 3276800 | tf_op jit(solution)/shard_map/reduce_scatter | solution.py:169
  605.8 4.1 copy-start.65
  605.8 5.3 copy-start.29
  615.6 1.5 copy-start.58
  752.0 8.0 copy-start.41
  752.0 11.8 %copy-start.17 = (f32[4,160,320]{1,2,0:T(8,128)S(1)}, f32[4,160,320]{1,2,0:T(8,128)}, u32[]{:S(2)}) copy-start(f32[4,160,320]{1,2,0:T(8,128)} %copy.221) | copy-start | bytes 2457604
  752.1 11.8 %copy-start.18 = (f32[4,160,320]{1,2,0:T(8,128)S(1)}, f32[4,160,320]{1,2,0:T(8,128)}, u32[]{:S(2)}) copy-start(f32[4,160,320]{1,2,0:T(8,128)} %copy.198) | copy-start | bytes 2457604
  760.0 3.9 copy-start.3
  872.1 94.0 %copy-start.11 = (bf16[256,1280]{1,0:T(8,128)(2,1)S(1)}, bf16[256,1280]{1,0:T(8,128)(2,1)}, u32[]{:S(2)}) copy-start(bf16[256,1280]{1,0:T(8,128)(2,1)} %param.18) | copy-start | bytes 1966084
  872.1 94.0 %copy-start.45 = (f32[1280]{0:T(1024)S(1)}, f32[1280]{0:T(1024)}, u32[]{:S(2)}) copy-start(f32[1280]{0:T(1024)} %copy-done.44) | copy-start | bytes 15364
  872.1 94.0 %copy-start.52 = (f32[256]{0:T(256)S(1)}, f32[256]{0:T(256)}, u32[]{:S(2)}) copy-start(f32[256]{0:T(256)} %copy-done.51) | copy-start | bytes 3076
  873.5 138.6 %copy-start.59 = (f32[80]{0:T(128)S(1)}, f32[80]{0:T(128)}, u32[]{:S(2)}) copy-start(f32[80]{0:T(128)} %param.29) | copy-start | bytes 964
  873.5 139.2 %copy-start.47 = (f32[2,1280]{1,0:T(2,128)S(1)}, f32[2,1280]{1,0:T(2,128)}, u32[]{:S(2)}) copy-start(f32[2,1280]{1,0:T(2,128)} %param.24) | copy-start | bytes 30724
  873.5 139.1 %copy-start.53 = (f32[2,1280]{1,0:T(2,128)S(1)}, f32[2,1280]{1,0:T(2,128)}, u32[]{:S(2)}) copy-start(f32[2,1280]{1,0:T(2,128)} %param.28) | copy-start | bytes 30724
  873.5 148.6 %copy-start.8 = (f32[256,1280]{1,0:T(8,128)S(1)}, f32[256,1280]{1,0:T(8,128)}, u32[]{:S(2)}) copy-start(f32[256,1280]{1,0:T(8,128)} %copy-done.7) | copy-start | bytes 3932164
  873.6 148.6 %copy-start.13 = (f32[256,1280]{1,0:T(8,128)S(1)}, f32[256,1280]{1,0:T(8,128)}, u32[]{:S(2)}) copy-start(f32[256,1280]{1,0:T(8,128)} %reduce-scatter.9.cloned.1.call-done) | copy-start | bytes 3932164
  873.6 148.6 %copy-start.43 = (f32[1280]{0:T(1024)S(1)}, f32[1280]{0:T(1024)}, u32[]{:S(2)}) copy-start(f32[1280]{0:T(1024)} %copy-done.42) | copy-start | bytes 15364
  873.6 148.6 %copy-start.50 = (f32[256]{0:T(256)S(1)}, f32[256]{0:T(256)}, u32[]{:S(2)}) copy-start(f32[256]{0:T(256)} %copy-done.49) | copy-start | bytes 3076
  873.6 148.6 %copy-start.56 = (f32[256]{0:T(256)S(1)}, f32[256]{0:T(256)}, u32[]{:S(2)}) copy-start(f32[256]{0:T(256)} %copy-done.55) | copy-start | bytes 3076
  1012.1 13.7 %copy-start.54 = (f32[2,1280]{1,0:T(2,128)}, f32[2,1280]{1,0:T(2,128)S(1)}, u32[]{:S(2)}) copy-start(f32[2,1280]{1,0:T(2,128)S(1)} %get-tuple-element.386) | copy-start | bytes 30724
  1012.1 13.7 %copy-start.60 = (f32[80]{0:T(128)}, f32[80]{0:T(128)S(1)}, u32[]{:S(2)}) copy-start(f32[80]{0:T(128)S(1)} %get-tuple-element.387) | copy-start | bytes 964
  (24 other events, 25.9 us)
Sparse Core Ops, SparseCore 0:
  10.5 38.2 all-gather.7
  50.9 54.7 all-gather.5
  143.2 92.5 reduce-scatter.4
  238.9 55.2 all-gather.9
  295.6 53.5 all-gather.11
  357.8 92.5 reduce-scatter.8
  454.9 55.2 all-gather.13
  576.7 123.9 all-reduce.6
  704.5 165.4 all-reduce.8
  872.2 93.8 reduce-scatter.10
  968.4 53.6 reduce-scatter.6
where the time goes:
time: 1040 us; the launch traced here: 1030 us
  waiting for transfers between devices  660 us (63%)
  matrix products  100 us (10%)
  blocking collectives  97.2 us (9%)
  local copies, waits for them, and re-layouts  93.2 us (9%)
  other arithmetic  57.9 us (6%)
  between operations  15.8 us (2%)
    reduce_scatter x1, waiting for transfers between devices, on_device(): lax.psum_scatter(jnp.dot(attended, w_out_half, preferred_element_type=jnp...  92.7 us
    reduce_scatter x1, waiting for transfers between devices, on_device(): lax.psum_scatter(jnp.dot(grad_gate, w_up.T, preferred_element_type=jnp.fl...  92.7 us
    reduce_scatter x1, waiting for transfers between devices, on_device(): lax.psum_scatter(jnp.einsum('ksc,kdc->sd', grad_projected, w_qkv, preferr...  91.5 us
    unnamed x12, waiting for transfers between devices  85.3 us
    psum x1, waiting for transfers between devices, on_device(): lax.psum((left_local, gain_local, scaling * grad_scale_local), ('dp', 'mp'))  83.5 us
    unnamed x144, local copies, waits for them, and re-layouts  53.5 us
    all_gather x1, waiting for transfers between devices, on_device(): cotangent_all = lax.all_gather(cotangent, 'mp', axis=0, tiled=True)  50.9 us
    all_gather x1, waiting for transfers between devices, on_device(): normed_all = lax.all_gather(normed, 'mp', axis=0, tiled=True)  49.5 us
  transfers between devices with their start and end apart: 11, of which 11 were waited for; matrix products, arithmetic and copies ran while one was open for 12% of the time, Pallas kernels for 0%

commit v1 on v0

v1 whole, which is shorter than its diff:
```python
import functools
import math

import jax
import jax.numpy as jnp
from jax import lax
from jax.experimental import pallas as pl
from jax.experimental.pallas import tpu as pltpu
from jax.sharding import PartitionSpec as P

HD = 80
LANE = 128
HIGHEST = lax.Precision.HIGHEST
EPSILON = 1e-06
SCALE_BASE = 1.442695041
MOMENTUM = 0.9
RATE = 0.1
NEG = -1e30
F32 = jnp.float32
BF16 = jnp.bfloat16
MESH = pl.DeviceIdType.MESH
VMEM_LIMIT = 62 * 1024 * 1024


def nn(a, b):
    return jnp.dot(a, b, preferred_element_type=F32)


def nt(a, b):
    return lax.dot_general(a, b, (((1,), (1,)), ((), ())), preferred_element_type=F32)


def tn(a, b):
    return lax.dot_general(a, b, (((0,), (0,)), ((), ())), preferred_element_type=F32)


def spread(cols, heads):
    row = lax.broadcasted_iota(jnp.int32, (cols, heads * LANE), 0)
    col = lax.broadcasted_iota(jnp.int32, (cols, heads * LANE), 1)
    off = col & (LANE - 1)
    hit = (row == (col >> 7) * HD + off) & (off < HD)
    return jnp.where(hit, 1.0, 0.0).astype(BF16)


def block_rows(index, rows):
    return pl.ds(pl.multiple_of(index * rows, rows), rows)


def greet(peers):
    bar = pltpu.get_barrier_semaphore()
    for peer in peers:
        pl.semaphore_signal(bar, 1, device_id=peer, device_id_type=MESH)
    pl.semaphore_wait(bar, len(peers))


def line_peers(n, me):
    return [{"mp": lax.rem(me + off, n)} for off in range(1, n)]


class LineGather:
    def __init__(self, n, me, own, buf, ssem, rsem):
        self.n, self.me, self.own, self.buf = n, me, own, buf
        self.ssem, self.rsem = ssem, rsem

    def copy(self, slot, hop, way):
        src = self.own if hop == 0 else self.buf.at[slot]
        return pltpu.make_async_remote_copy(
            src_ref=src,
            dst_ref=self.buf.at[slot],
            send_sem=self.ssem.at[way, hop],
            recv_sem=self.rsem.at[slot],
            device_id={"mp": self.me + 1 - 2 * way},
            device_id_type=MESH,
        )

    def goes(self, hop, way):
        if way == 0:
            return (self.me - hop >= 0) & (self.me < self.n - 1)
        return (self.me + hop <= self.n - 1) & (self.me > 0)

    def slot(self, hop, way):
        return self.me - hop if way == 0 else self.me + hop

    def arrives(self, hop, way):
        return self.me - hop >= 0 if way == 0 else self.me + hop <= self.n - 1

    def send(self, hop, ways=(0, 1)):
        for way in ways:

            @pl.when(self.goes(hop, way))
            def _(way=way):
                self.copy(self.slot(hop, way), hop, way).start()

    def relay(self, hop):
        for way in (0, 1):

            @pl.when(self.arrives(hop, way))
            def _(way=way):
                slot = self.slot(hop, way)
                self.copy(slot, hop, way).wait_recv()

            if hop < self.n - 1:
                self.send(hop, (way,))

    def finish(self):
        for hop in range(self.n - 1):
            for way in (0, 1):

                @pl.when(self.goes(hop, way))
                def _(way=way, hop=hop):
                    self.copy(self.slot(hop, way), hop, way).wait_send()


def line_sems(n):
    return [pltpu.SemaphoreType.DMA((2, n)), pltpu.SemaphoreType.DMA((n,))]


def vmem(count):
    return [pl.BlockSpec(memory_space=pltpu.VMEM)] * count


def params(collective_id=None):
    return pltpu.CompilerParams(
        collective_id=collective_id,
        has_side_effects=collective_id is not None,
        vmem_limit_bytes=VMEM_LIMIT,
    )


def attend_kernel(
    dims, x_ref, w_ref, gain_ref, c_ref, st_ref,
    n1_ref, q_ref, k_ref, v_ref, lse_ref, oc_ref, of_ref,
    xbuf, wpad, mask, opad, zs, zr, as_, ar,
):
    n, rows, heads, span = dims
    me = lax.axis_index("mp")
    cols = w_ref.shape[2]
    greet(line_peers(n, me))
    gather = LineGather(n, me, x_ref, xbuf, zs, zr)
    gather.send(0)
    sel = spread(cols, heads)
    for m in range(3):
        wpad[m] = nn(w_ref[m], sel).astype(BF16)
    xbuf[me] = x_ref[...]

    def project(slot):
        x = xbuf[slot].astype(F32)
        scale = lax.rsqrt(jnp.mean(x * x, axis=-1, keepdims=True) + EPSILON)
        normed = (x * scale * gain_ref[...]).astype(BF16)
        n1_ref[slot] = normed
        at = block_rows(slot, rows)
        for m, ref in enumerate((q_ref, k_ref, v_ref)):
            out = nn(normed, wpad[m])
            if m == 0:
                out = out * c_ref[...]
            out = out.astype(BF16)
            for h in range(heads):
                ref[h, at, :] = out[:, h * LANE : (h + 1) * LANE]

    project(me)

    def arrivals(hop):
        def one(way, _):
            slot = me - hop + 2 * hop * way

            @pl.when((slot >= 0) & (slot < n))
            def _():
                project(slot)

            return 0

        lax.fori_loop(0, 2, one, 0)

    for hop in range(1, n):
        gather.relay(hop)
        arrivals(hop)

    def chunk(i, _):
        first = jnp.maximum(i - (span - 1), 0)
        at, keys = block_rows(i, rows), pl.ds(pl.multiple_of(first * rows, rows), span * rows)
        q_pos = i * rows + lax.broadcasted_iota(jnp.int32, mask.shape, 0)
        k_pos = first * rows + lax.broadcasted_iota(jnp.int32, mask.shape, 1)
        mask[...] = jnp.where((k_pos <= q_pos) & (k_pos >= st_ref[at, :]), 0.0, NEG)

        def head(h, _):
            scores = nt(q_ref[h, at, :], k_ref[h, keys, :]) + mask[...]
            top = jnp.max(scores, axis=-1, keepdims=True)
            raised = jnp.exp(scores - top)
            total = jnp.sum(raised, axis=-1, keepdims=True)
            prob = (raised * (1.0 / total)).astype(BF16)
            opad[h] = nn(prob, v_ref[h, keys, :]).astype(BF16)
            lse_ref[h, at, :] = top + jnp.log(total)
            return 0

        lax.fori_loop(0, heads, head, 0)
        wide = jnp.concatenate([opad[h] for h in range(heads)], axis=1)
        oc_ref[i] = nt(wide, sel).astype(BF16)

        @pl.when(i != me)
        def _():
            pltpu.make_async_remote_copy(
                src_ref=oc_ref.at[i], dst_ref=of_ref.at[me], send_sem=as_.at[i],
                recv_sem=ar.at[me], device_id={"mp": i}, device_id_type=MESH,
            ).start()

        @pl.when(i == me)
        def _():
            of_ref[me] = oc_ref[me]

        return 0

    lax.fori_loop(0, n, chunk, 0)
    gather.finish()
    for off in range(1, n):
        peer = lax.rem(me + off, n)
        copy = pltpu.make_async_remote_copy(
            src_ref=oc_ref.at[peer], dst_ref=of_ref.at[peer], send_sem=as_.at[peer],
            recv_sem=ar.at[peer], device_id={"mp": peer}, device_id_type=MESH,
        )
        copy.wait_send()
        copy.wait_recv()


def attend(dims, x, w, gain, c_row, starts):
    n, rows, heads, span = dims
    width, cols = x.shape[1], w.shape[2]
    count = n * rows
    head_out = jax.ShapeDtypeStruct((heads, count, LANE), BF16)
    return pl.pallas_call(
        functools.partial(attend_kernel, dims),
        out_shape=(
            jax.ShapeDtypeStruct((n, rows, width), BF16),
            head_out, head_out, head_out,
            jax.ShapeDtypeStruct((heads, count, 1), F32),
            jax.ShapeDtypeStruct((n, rows, cols), BF16),
            jax.ShapeDtypeStruct((n, rows, cols), BF16),
        ),
        in_specs=vmem(5),
        out_specs=vmem(7),
        scratch_shapes=[
            pltpu.VMEM((n, rows, width), BF16),
            pltpu.VMEM((3, width, heads * LANE), BF16),
            pltpu.VMEM((rows, span * rows), F32),
            pltpu.VMEM((heads, rows, LANE), BF16),
            *line_sems(n),
            pltpu.SemaphoreType.DMA((n,)),
            pltpu.SemaphoreType.DMA((n,)),
        ],
        compiler_params=params(1),
        name="attend",
    )(x, w, gain, c_row, starts)


def middle_kernel(
    dims, x_ref, g_ref, of_ref, w_ref, gain_ref,
    out_ref, dh_ref, n2_ref, g_all, dhb_ref, dgain_ref,
    h_ref, acc, dn2, gs, gr, ns, nr, ds, dr,
):
    n = dims[0]
    me = lax.axis_index("mp")
    greet(line_peers(n, me))
    gather_g = LineGather(n, me, g_ref, g_all, gs, gr)
    gather_n = LineGather(n, me, n2_ref.at[me], n2_ref, ns, nr)
    gather_d = LineGather(n, me, dhb_ref.at[me], dhb_ref, ds, dr)
    gather_g.send(0)
    g_all[me] = g_ref[...]
    h_ref[...] = x_ref[...].astype(F32)

    def project(j, _):
        h_ref[...] += nt(of_ref[j], w_ref[j, 0])
        return 0

    lax.fori_loop(0, n, project, 0)
    h = h_ref[...]
    scale = lax.rsqrt(jnp.mean(h * h, axis=-1, keepdims=True) + EPSILON)
    n2_ref[me] = (h * scale * gain_ref[...]).astype(BF16)
    gather_n.send(0)
    acc[...] = h_ref[...]
    dn2[...] = jnp.zeros_like(dn2)

    def hidden(j, _):
        gate = nn(n2_ref[me], w_ref[j, 1])
        sig = 1.0 / (1.0 + jnp.exp(-gate))
        acc[...] += nt((gate * sig).astype(BF16), w_ref[j, 2])
        dz = nn(g_ref[...], w_ref[j, 2])
        da = (dz * (sig * (1.0 + gate * (1.0 - sig)))).astype(BF16)
        dn2[...] += nt(da, w_ref[j, 1])
        return 0

    lax.fori_loop(0, n, hidden, 0)
    out_ref[...] = acc[...].astype(BF16)
    h = h_ref[...]
    scale = lax.rsqrt(jnp.mean(h * h, axis=-1, keepdims=True) + EPSILON)
    unit = h * scale
    grad = dn2[...]
    dgain_ref[...] = jnp.sum(grad * unit, axis=0, keepdims=True)
    du = grad * gain_ref[...]
    dh = g_ref[...].astype(F32) + scale * (du - unit * jnp.mean(du * unit, axis=-1, keepdims=True))
    dh_ref[...] = dh
    dhb_ref[me] = dh.astype(BF16)
    gather_d.send(0)
    for hop in range(1, n):
        gather_g.relay(hop)
        gather_n.relay(hop)
        gather_d.relay(hop)
    for gather in (gather_g, gather_n, gather_d):
        gather.finish()


def middle(dims, x, g, o_full, w_full, gain):
    n, rows = dims[:2]
    width = x.shape[1]
    every = jax.ShapeDtypeStruct((n, rows, width), BF16)
    return pl.pallas_call(
        functools.partial(middle_kernel, dims),
        out_shape=(
            jax.ShapeDtypeStruct((rows, width), BF16),
            jax.ShapeDtypeStruct((rows, width), F32),
            every, every, every,
            jax.ShapeDtypeStruct((1, width), F32),
        ),
        in_specs=vmem(5),
        out_specs=vmem(6),
        scratch_shapes=[pltpu.VMEM((rows, width), F32)] * 3 + line_sems(n) * 3,
        compiler_params=params(2),
        name="middle",
    )(x, g, o_full, w_full, gain)


def back_kernel(
    dims, q_ref, k_ref, v_ref, lse_ref, dhb_ref, w_ref, c_ref, st_ref,
    dx_ref, dc_ref,
    wpad, mask, do_ref, dq_ref, dk_ref, dv_ref,
):
    n, rows, heads, span = dims
    sel = spread(w_ref.shape[1], heads)
    wpad[...] = nn(w_ref[...], sel).astype(BF16)
    dk_ref[...] = jnp.zeros_like(dk_ref)
    dv_ref[...] = jnp.zeros_like(dv_ref)
    dc_ref[...] = jnp.zeros_like(dc_ref)

    def squeeze(ref, at):
        wide = jnp.concatenate([ref[h, at, :].astype(BF16) for h in range(heads)], axis=1)
        return nt(wide, sel).astype(BF16)

    def chunk(i, _):
        first = jnp.maximum(i - (span - 1), 0)
        at, keys = block_rows(i, rows), pl.ds(pl.multiple_of(first * rows, rows), span * rows)
        q_pos = i * rows + lax.broadcasted_iota(jnp.int32, mask.shape, 0)
        k_pos = first * rows + lax.broadcasted_iota(jnp.int32, mask.shape, 1)
        mask[...] = jnp.where((k_pos <= q_pos) & (k_pos >= st_ref[at, :]), 0.0, NEG)
        grad = nn(dhb_ref[i], wpad[...]).astype(BF16)
        for h in range(heads):
            do_ref[h] = grad[:, h * LANE : (h + 1) * LANE]

        def head(h, _):
            query = q_ref[h, at, :]
            scores = nt(query, k_ref[h, keys, :]) + mask[...]
            prob = jnp.exp(scores - lse_ref[h, at, :])
            dp = nt(do_ref[h], v_ref[h, keys, :])
            inner = jnp.sum(prob * dp, axis=-1, keepdims=True)
            ds = (prob * (dp - inner)).astype(BF16)
            dq = nn(ds, k_ref[h, keys, :])
            dk_ref[h, keys, :] += tn(ds, query)
            dv_ref[h, keys, :] += tn(prob.astype(BF16), do_ref[h])
            dc_ref[...] += jnp.sum(dq * query.astype(F32), axis=0, keepdims=True)
            dq_ref[h] = (dq * c_ref[:, :LANE]).astype(BF16)
            return 0

        lax.fori_loop(0, heads, head, 0)
        dx_ref[0, i] = squeeze(dq_ref, slice(None))
        return 0

    lax.fori_loop(0, n, chunk, 0)

    def close(i, _):
        at = block_rows(i, rows)
        dx_ref[1, i] = squeeze(dk_ref, at)
        dx_ref[2, i] = squeeze(dv_ref, at)
        return 0

    lax.fori_loop(0, n, close, 0)


def back(dims, q, k, v, lse, dhb, w_out, c_row, starts):
    n, rows, heads, span = dims
    cols, width = w_out.shape[1], w_out.shape[0]
    return pl.pallas_call(
        functools.partial(back_kernel, dims),
        out_shape=(
            jax.ShapeDtypeStruct((3, n, rows, cols), BF16),
            jax.ShapeDtypeStruct((1, LANE), F32),
        ),
        in_specs=vmem(8),
        out_specs=vmem(2),
        scratch_shapes=[
            pltpu.VMEM((width, heads * LANE), BF16),
            pltpu.VMEM((rows, span * rows), F32),
            pltpu.VMEM((heads, rows, LANE), BF16),
            pltpu.VMEM((heads, rows, LANE), BF16),
            pltpu.VMEM((heads, n * rows, LANE), F32),
            pltpu.VMEM((heads, n * rows, LANE), F32),
        ],
        compiler_params=params(),
        name="back",
    )(q, k, v, lse, dhb, w_out, c_row, starts)


def grads_kernel(
    dims, n1_ref, n2_ref, dhb_ref, g_ref, dx_ref, oc_ref, wqkv_ref, wup_ref, wdn_ref,
    x_ref, dh_ref, gain_ref,
    gt_ref, gb_ref, gin_ref, dgain_ref,
    z_ref, da_ref, sbuf, lbuf, rbuf, ss, ls, rs,
):
    n, rows, heads, span = dims
    me = lax.axis_index("mp")
    greet(line_peers(n, me))

    def own(i):
        total = nt(dx_ref[0, i], wqkv_ref[0])
        total += nt(dx_ref[1, i], wqkv_ref[1])
        return total + nt(dx_ref[2, i], wqkv_ref[2])

    def copy(i, way):
        buf, sem = (lbuf, ls) if way == 0 else (rbuf, rs)
        return pltpu.make_async_remote_copy(
            src_ref=sbuf.at[i], dst_ref=buf.at[i], send_sem=ss.at[i], recv_sem=sem.at[i],
            device_id={"mp": me + 1 - 2 * way}, device_id_type=MESH,
        )

    def step(t, way):
        i = n - 1 - t if way == 0 else t
        buf = lbuf if way == 0 else rbuf
        has = me > 0 if way == 0 else me < n - 1

        @pl.when(i > me if way == 0 else i < me)
        def _():
            mine = own(i)

            @pl.when(has)
            def _():
                copy(i, way).wait_recv()
                sbuf[i] = (mine + buf[i].astype(F32)).astype(BF16)

            @pl.when(jnp.logical_not(has))
            def _():
                sbuf[i] = mine.astype(BF16)

            copy(i, way).start()

    def hidden(i, _):
        gate = nn(n2_ref[i], wup_ref[...])
        sig = 1.0 / (1.0 + jnp.exp(-gate))
        z_ref[i] = (gate * sig).astype(BF16)
        dz = nn(g_ref[i], wdn_ref[...])
        da_ref[i] = (dz * (sig * (1.0 + gate * (1.0 - sig)))).astype(BF16)
        return 0

    def flat(value):
        return value.reshape(n * rows, value.shape[-1])

    def weight(m, a, b):
        left, right = flat(a), flat(b)
        gt_ref[m] = tn(right, left)
        gb_ref[m] = tn(left, right).astype(BF16)

    step(0, 0)
    step(0, 1)
    lax.fori_loop(0, n, hidden, 0)
    weight(3, n2_ref[...], da_ref[...])
    weight(5, g_ref[...], z_ref[...])
    weight(4, dhb_ref[...], oc_ref[...])
    for t in range(1, n - 1):
        step(t, 0)
        step(t, 1)

    def inputs(m, _):
        weight(m, n1_ref[...], dx_ref[m])
        return 0

    lax.fori_loop(0, 3, inputs, 0)
    gin_ref[...] = own(me)

    @pl.when(me > 0)
    def _():
        copy(me, 0).wait_recv()
        gin_ref[...] += lbuf[me].astype(F32)

    @pl.when(me < n - 1)
    def _():
        copy(me, 1).wait_recv()
        gin_ref[...] += rbuf[me].astype(F32)

    x = x_ref[...].astype(F32)
    scale = lax.rsqrt(jnp.mean(x * x, axis=-1, keepdims=True) + EPSILON)
    unit = x * scale
    grad = gin_ref[...]
    dgain_ref[...] = jnp.sum(grad * unit, axis=0, keepdims=True)
    du = grad * gain_ref[...]
    gin_ref[...] = dh_ref[...] + scale * (du - unit * jnp.mean(du * unit, axis=-1, keepdims=True))
    for i in range(n):

        @pl.when(me < i)
        def _(i=i):
            copy(i, 0).wait_send()

        @pl.when(me > i)
        def _(i=i):
            copy(i, 1).wait_send()


def grads(dims, n1, n2, dhb, g_all, dx, oc, wqkv, w_up, w_down, x, dh, gain):
    n, rows = dims[:2]
    width, cols = w_up.shape
    every = pltpu.VMEM((n, rows, width), BF16)
    return pl.pallas_call(
        functools.partial(grads_kernel, dims),
        out_shape=(
            jax.ShapeDtypeStruct((6, cols, width), F32),
            jax.ShapeDtypeStruct((6, width, cols), BF16),
            jax.ShapeDtypeStruct((rows, width), F32),
            jax.ShapeDtypeStruct((1, width), F32),
        ),
        in_specs=vmem(12),
        out_specs=vmem(4),
        scratch_shapes=[
            pltpu.VMEM((n, rows, cols), BF16),
            pltpu.VMEM((n, rows, cols), BF16),
            every, every, every,
            pltpu.SemaphoreType.DMA((n,)),
            pltpu.SemaphoreType.DMA((n,)),
            pltpu.SemaphoreType.DMA((n,)),
        ],
        compiler_params=params(3),
        name="grads",
    )(n1, n2, dhb, g_all, dx, oc, wqkv, w_up, w_down, x, dh, gain)


def orthonormal(matrix):
    columns = []
    for index in range(matrix.shape[-1]):
        vector = matrix[..., index]
        for basis in columns:
            vector = vector - jnp.sum(basis * vector, axis=-1, keepdims=True) * basis
        vector = vector * lax.rsqrt(jnp.sum(vector * vector, axis=-1, keepdims=True) + 1e-12)
        columns.append(vector)
    return jnp.stack(columns, axis=-1)


def on_device(
    activations, cotangent, doc_lengths, w_in, w_attn_out, w_down, gains, scale_param,
    mom_in, mom_out, mom_gain, mom_scale, error_buffer, factors,
):
    rows, width = activations.shape
    n = lax.axis_size("mp")
    data_par = lax.axis_size("dp")
    my_data, me = lax.axis_index("dp"), lax.axis_index("mp")
    count = rows * n
    scaling = (count * data_par) ** (-0.5)
    cols = w_in.shape[2]
    own_rows = w_in.shape[1]
    heads = cols // HD
    longest = count // 2
    span = min(n, -(-(longest - 1) // rows) + 1)
    dims = (n, rows, heads, span)

    shards = jnp.concatenate([w_in, w_attn_out.T[None], w_down.T[None]], axis=0).astype(BF16)
    wqkv = lax.all_gather(shards[:3], "dp", axis=1, tiled=True)
    tail = jnp.stack([shards[4], shards[3], shards[5]])
    w_full = lax.all_gather(lax.all_gather(tail, "mp", axis=0), "dp", axis=2, tiled=True)
    w_mine = lax.dynamic_index_in_dim(w_full, me, 0, keepdims=False)

    ends = jnp.cumsum(doc_lengths[0])
    position = jnp.arange(count, dtype=jnp.int32)[:, None]
    starts = jnp.max(jnp.where(ends[None, :] <= position, ends[None, :], 0), axis=1, keepdims=True)
    factor = SCALE_BASE / math.sqrt(HD) * jax.nn.softplus(scale_param)
    c_row = jnp.tile(jnp.pad(factor, (0, LANE - HD)), heads)[None]

    n1, q, k, v, lse, oc, o_full = attend(dims, activations, wqkv, gains[:1], c_row, starts)
    output, dh, n2, g_all, dhb, dgain2 = middle(dims, activations, cotangent, o_full, w_full, gains[1:])
    dx, dc = back(dims, q, k, v, lse, dhb, w_mine[0], c_row, starts)
    gt, gb, grad_input, dgain1 = grads(
        dims, n1, n2, dhb, g_all, dx, oc, wqkv, w_mine[1], w_mine[2], activations, dh, gains[:1]
    )

    grad_scale_local = dc[0, :HD] / factor * (SCALE_BASE / math.sqrt(HD)) * jax.nn.sigmoid(scale_param)
    parts = gb.reshape(6, data_par, own_rows, cols).transpose(1, 0, 2, 3)
    summed = scaling * lax.psum_scatter(parts, "dp", scatter_dimension=0).astype(F32)
    grad_in = summed[:4]
    grad_out = jnp.swapaxes(summed[4:], 1, 2)

    stored = scaling * gt + error_buffer[0]
    left_local = jnp.einsum("kcd,kcr->kdr", stored, factors, precision=HIGHEST)
    gain_local = scaling * jnp.concatenate([dgain1, dgain2])
    left, grad_gain, grad_scale = lax.psum(
        (left_local, gain_local, scaling * grad_scale_local), ("dp", "mp")
    )
    basis = orthonormal(left)
    right = lax.psum(jnp.einsum("kcd,kdr->kcr", stored, basis, precision=HIGHEST), "dp")
    error_new = (stored - jnp.einsum("kcr,kdr->kcd", right, basis, precision=HIGHEST))[None]
    mine_basis = lax.dynamic_slice_in_dim(basis, my_data * own_rows, own_rows, 1)
    mine = jnp.einsum("kdr,kcr->kdc", mine_basis, right, precision=HIGHEST)
    mom_in_new = MOMENTUM * mom_in + mine[:4]
    new_in = w_in - RATE * mom_in_new
    mom_out_new = MOMENTUM * mom_out + jnp.swapaxes(mine[4:], 1, 2)
    new_out = jnp.stack([w_attn_out, w_down]) - RATE * mom_out_new
    mom_gain_new = MOMENTUM * mom_gain + grad_gain
    new_gain = gains - RATE * mom_gain_new
    mom_scale_new = MOMENTUM * mom_scale + grad_scale
    new_scale = scale_param - RATE * mom_scale_new
    return (
        output, grad_input, grad_in, grad_out, grad_gain, grad_scale, new_in, new_out,
        new_gain, new_scale, mom_in_new, mom_out_new, mom_gain_new, mom_scale_new,
        error_new, right,
    )


def solution(mesh):
    tokens, shard = P(("dp", "mp"), None), P(None, "dp", "mp")
    return jax.shard_map(
        on_device,
        mesh=mesh,
        in_specs=(
            tokens, tokens, P("dp", None), shard, P("mp", "dp"), P("mp", "dp"), P(), P(),
            shard, P(None, "mp", "dp"), P(), P(), P("dp", None, "mp", None), P(None, "mp", None),
        ),
        out_specs=(
            tokens, tokens, shard, P(None, "mp", "dp"), P(), P(), shard, P(None, "mp", "dp"),
            P(), P(), shard, P(None, "mp", "dp"), P(), P(), P("dp", None, "mp", None),
            P(None, "mp", None),
        ),
        check_vma=False,
    )
```

time: 1040 us -> 632 us (0.61)
  waiting for transfers between devices: 660 us -> 150 us
  Pallas kernels: 0 us -> 309 us
  local copies, waits for them, and re-layouts: 93.2 us -> 20.1 us
  matrix products: 100 us -> 39.9 us
  other arithmetic: 57.9 us -> 18 us
  blocking collectives: 97.2 us -> 77 us
    pallas_call x0 -> x4, Pallas kernels: none -> 309 us  [the longest x1 138 us: middle(): pl.pallas_call(functools.partial(middle_kernel, dims), out_shape=(jax.Sha...]
    reduce_scatter x4 -> x1, waiting for transfers between devices: 286 us -> 0.01 us  [on_device(): lax.psum_scatter(parts, 'dp', scatter_dimension=0).astype(F32)]
    all_gather x5 -> x3, waiting for transfers between devices: 205 us -> 66.1 us  [the longest x1 37.3 us: on_device(): lax.all_gather(tail, 'mp', axis=0)]
    unnamed x12 -> x5, waiting for transfers between devices: 85.3 us -> 0.55 us
    dot_general x29 -> x4, matrix products: 100 us -> 39.9 us  [the longest x1 15.3 us: on_device(): jnp.einsum('kcr,kdr->kcd', right, basis, precision=HIGHEST)]
    unnamed x144 -> x42, local copies, waits for them, and re-layouts: 53.5 us -> 3.02 us
    all_gather x2 -> x0, blocking collectives: 24.3 us -> none  [the longest x1 12.3 us: on_device(): lax.all_gather(w_attn_out.astype(jnp.bfloat16), 'dp', axis=1, tiled=True)]
    mul x3 -> x0, local copies, waits for them, and re-layouts: 17.2 us -> none  [the longest x1 9.61 us: on_device(): local_in = scaling * jnp.concatenate([grad_qkv, grad_up[None]], axis=0)]
  transfers between devices with their start and end apart: 11 -> 5, of which waited for: 11 -> 3; matrix products, arithmetic and copies ran while one was open for 12% -> 8% of each run, Pallas kernels for 0% -> 13%
where the time goes in v1:
time: 632 us; the launch traced here: 628 us
  Pallas kernels  309 us (49%)
  waiting for transfers between devices  150 us (24%)
  blocking collectives  77 us (12%)
  matrix products  39.9 us (6%)
  local copies, waits for them, and re-layouts  20.1 us (3%)
  other arithmetic  18 us (3%)
  between operations  14.4 us (2%)
    pallas_call x1, Pallas kernels, middle(): pl.pallas_call(functools.partial(middle_kernel, dims), out_shape=(jax.Sha...  138 us
    psum x1, waiting for transfers between devices, on_device(): lax.psum((left_local, gain_local, scaling * grad_scale_local), ('dp', 'mp'))  83 us
    pallas_call x1, Pallas kernels, attend(): pl.pallas_call(functools.partial(attend_kernel, dims), out_shape=(jax.Sha...  80.2 us
    pallas_call x1, Pallas kernels, grads(): pl.pallas_call(functools.partial(grads_kernel, dims), out_shape=(jax.Shap...  64.4 us
    psum x1, blocking collectives, on_device(): lax.psum((left_local, gain_local, scaling * grad_scale_local), ('dp', 'mp'))  50.7 us
    all_gather x1, waiting for transfers between devices, on_device(): lax.all_gather(tail, 'mp', axis=0)  37.3 us
    all_gather x1, waiting for transfers between devices, on_device(): wqkv = lax.all_gather(shards[:3], 'dp', axis=1, tiled=True)  28.7 us
    pallas_call x1, Pallas kernels, back(): pl.pallas_call(functools.partial(back_kernel, dims), out_shape=(jax.Shape...  26.7 us
  transfers between devices with their start and end apart: 5, of which 3 were waited for; matrix products, arithmetic and copies ran while one was open for 8% of the time, Pallas kernels for 13%

profile of v1, /device:TPU:0, one launch (start us, length us, event | category | flops | bytes accessed | tf_op | source)
XLA Modules:
  0.0 628.3 jit_solution(18046610087969906220)
XLA Ops:
  7.2 1.3 convert.13
  8.5 1.1 convert_bitcast_fusion
  9.6 0.8 pad_maximum_fusion
  10.5 0.0 all-gather.5.cloned.1.call-start
  10.5 0.8 slice.96
  11.4 37.3 %all-gather.9.cloned.1.call-done = bf16[12,160,320]{2,1,0:T(8,128)(2,1)} async-done(((bf16[3,160,320]{2,1,0:T(8,128)(2,1)}), bf16[12,160,320]{2,1,0:T(8,128)(2,1)}) %all-gather.9.cloned.1.call-update) | async-done | bytes 1228816 | tf_op jit(solution)/shard_map/all_gather | solution.py:570
  48.8 0.8 reduce-window.8
  49.6 0.1 select_reduce_fusion
  49.7 1.0 copy.103.st_ref
  50.7 0.7 fusion.41
  51.4 1.4 fusion.47
  52.8 28.7 %all-gather.5.cloned.1.call-done.w_ref.wqkv_ref = bf16[3,1280,320]{2,1,0:T(8,128)(2,1)} async-done(((bf16[3,160,320]{2,1,0:T(8,128)(2,1)}), bf16[3,1280,320]{2,1,0:T(8,128)(2,1)}) %all-gather.5.cloned.1.call-update) | async-done | bytes 2457616 | tf_op jit(solution)/shard_map/all_gather | solution.py:568
  81.5 0.6 tile.2
  82.1 80.2 %attend.1 = (bf16[4,256,1280]{2,1,0:T(8,128)(2,1)}, bf16[4,1024,128]{2,1,0:T(8,128)(2,1)}, bf16[4,1024,128]{2,1,0:T(8,128)(2,1)}, bf16[4,1024,128]{2,1,0:T(8,128...) custom-call(bf16[256,1280]{1,0:T(8,128)(2,1)} %x_ref.5, ...), custom_call_target="tpu_custom_call" | custom-call | tf_op jit(solution)/shard_map/attend/pallas_call | solution.py:229
  162.4 137.8 %middle.1 = (bf16[256,1280]{1,0:T(8,128)(2,1)}, f32[256,1280]{1,0:T(8,128)}, bf16[4,256,1280]{2,1,0:T(8,128)(2,1)}, bf16[4,256,1280]{2,1,0:T(8,128)(2,1)}, bf16[...) custom-call(bf16[256,1280]{1,0:T(8,128)(2,1)} %x_ref.5, bf16[256,1280]{1,0:T(8,128)(2,1)} %g_ref.1, ...), custom_call_target="tpu_custom_call" | custom-call | tf_op jit(solution)/shard_map/middle/pallas_call | solution.py:314
  300.2 3.5 dynamic-slice_bitcast_fusion
  303.7 26.7 %back.1 = (bf16[3,4,256,320]{3,2,1,0:T(8,128)(2,1)}, f32[1,128]{1,0:T(1,128)}) custom-call(bf16[4,1024,128]{2,1,0:T(8,128)(2,1)} %get-tuple-element.41.q_ref, bf16[4,1024,128]{2,1,0:T(8,128)(2,1)} %get-tuple-element.42.k_ref, bf16[4,1024,128]{2,1,0:T(8,128)(2,1)} %get-tuple-element.43.v_ref, f32[4,1024,1]{2,1,0:T(8,128)} %get-tuple-element.44.lse_ref, ...), custom_call_target="tpu_custom_call" | custom-call | tf_op jit(solution)/shard_map/back/pallas_call | solution.py:388
  330.4 64.4 %grads.1 = (f32[6,320,1280]{2,1,0:T(8,128)}, bf16[6,1280,320]{2,1,0:T(8,128)(2,1)}, f32[256,1280]{1,0:T(8,128)}, f32[1,1280]{1,0:T(1,128)}) custom-call(bf16[4,256,1280]{2,1,0:T(8,128)(2,1)} %get-tuple-element.37.n1_ref, bf16[4,256,1280]{2,1,0:T(8,128)(2,1)} %get-tuple-element.38.n2_ref, bf16[4,256,1280]{2,1,0:T(8,128)(2,1)} %get-tuple-element.39.dhb_ref, ...), custom_call_target="tpu_custom_call" | custom-call | tf_op jit(solution)/shard_map/grads/pallas_call | solution.py:516
  394.8 6.6 %copy.494 = bf16[6,8,160,320]{3,2,0,1:T(8,128)(2,1)} copy(bf16[6,8,160,320]{3,2,1,0:T(8,128)(2,1)} %bitcast.364) | data formatting | bytes 9830400 | tf_op jit(solution)/shard_map/reshape | solution.py:587
  401.4 1.0 copy-done.2
  402.4 8.9 %fusion.44 = f32[6,1280,8]{1,2,0:T(8,128)} fusion(f32[6,320,8]{1,2,0:T(8,128)S(1)} %copy-done, f32[1,6,320,1280]{3,2,1,0:T(8,128)} %param.26, f32[6,320,1280]{2,1,0:T(8,128)S(1)} %copy-done.2), kind=kOutput, calls=%fused_computation.156 | convolution fusion | flops 240844800 | bytes 19968000 | tf_op jit(solution)/shard_map/kcd,kcr->kdr/dot_general | solution.py:593
  411.4 0.0 reduce-scatter.2.cloned.1.call-start
  411.5 0.5 reduce-scatter.2.cloned.1.call-update
  412.0 50.7 %all-reduce.1 = (f32[2,1280]{1,0:T(2,128)S(1)}, f32[80]{0:T(128)S(1)}) all-reduce(f32[2,1280]{1,0:T(2,128)S(1)} %maximum_multiply_fusion, f32[80]{0:T(128)S(1)} %fusion.42), channel_id=1, replica_groups=mesh['dp'=8,'mp'=4] {'dp','mp'}, use_global_device_ids=true, to_apply=%region_3.4 | all-reduce | flops 2640 | bytes 21120 | tf_op jit(solution)/shard_map/psum | solution.py:595
  462.7 0.5 multiply_subtract_fusion.22
  463.2 0.6 multiply_subtract_fusion.21
  463.8 83.0 %all-reduce.4.cloned.1.call-done = f32[6,1280,8]{1,2,0:T(8,128)} async-done(((f32[6,1280,8]{1,2,0:T(8,128)}), f32[6,1280,8]{1,2,0:T(8,128)}) %all-reduce.4.cloned.1.call-update) | async-done | bytes 245776 | tf_op jit(solution)/shard_map/psum | solution.py:595
  546.8 1.0 slice.100
  547.8 0.1 fusion.39
  547.9 2.4 fusion.46
  550.4 0.2 fusion.14
  550.6 0.3 fusion.37
  550.9 0.2 multiply_reduce_fusion.26
  551.1 0.3 multiply_reduce_fusion.6
  551.4 0.3 multiply_reduce_fusion.5
  551.6 0.2 multiply_reduce_fusion.11
  551.9 0.3 multiply_reduce_fusion.4
  552.2 0.2 multiply_reduce_fusion.18
  552.4 0.2 multiply_reduce_fusion.3
  552.6 0.2 multiply_reduce_fusion.13
  552.8 0.2 multiply_reduce_fusion.2
  553.0 0.2 multiply_reduce_fusion.7
  553.2 0.2 multiply_reduce_fusion.1
  553.4 0.2 multiply_reduce_fusion
  553.7 0.1 copy_subtract_fusion.3
  553.7 0.1 copy_multiply_fusion.13
  553.8 0.1 fusion.16
  553.9 0.1 copy_multiply_fusion.12
  554.0 0.1 fusion.11
  554.1 0.1 copy_multiply_fusion.11
  554.2 0.1 fusion.13
  554.3 1.8 subtract_multiply_fusion
  556.1 0.4 stack.11
  556.5 14.2 %fusion.43 = f32[6,320,8]{1,2,0:T(8,128)S(1)} fusion(f32[6,1280,8]{1,2,0:T(8,128)S(1)} %stack.11, f32[1,6,320,1280]{3,2,1,0:T(8,128)} %param.26, f32[6,320,1280]{2,1,0:T(8,128)} %get-tuple-element.53), kind=kOutput, calls=%fused_computation.155 | convolution fusion | flops 240844800 | bytes 19968000 | tf_op jit(solution)/shard_map/kcd,kdr->kcr/dot_general | solution.py:599
  570.8 26.4 %psum.31 = f32[6,320,8]{1,2,0:T(8,128)S(1)} all-reduce(f32[6,320,8]{1,2,0:T(8,128)S(1)} %fusion.43), channel_id=1, replica_groups=mesh['dp'=8,'mp'=4] {'dp'}, use_global_device_ids=true, to_apply=%region_42.43 | all-reduce | flops 15360 | bytes 122880 | tf_op jit(solution)/shard_map/psum | solution.py:599
  597.1 1.6 fusion.1
  598.7 1.1 maximum_subtract_fusion
  599.8 1.5 multiply_subtract_fusion
  601.3 15.3 %subtract_bitcast_fusion = f32[1,6,320,1280]{3,2,1,0:T(8,128)} fusion(f32[6,320,8]{1,2,0:T(8,128)S(1)} %psum.31, f32[6,1280,8]{1,2,0:T(8,128)S(1)} %stack.11, f32[1,6,320,1280]{3,2,1,0:T(8,128)} %param.26, f32[6,320,1280]{2,1,0:T(8,128)} %get-tuple-element.53), kind=kOutput, calls=%fused_computation.1 | convolution fusion | flops 243302400 | bytes 29798400 | tf_op jit(solution)/shard_map/kcr,kdr->kcd/dot_general | solution.py:600
  616.6 1.2 convert_multiply_fusion
  617.8 0.8 slice_bitcast_fusion.2
  618.6 1.0 slice_bitcast_fusion
  619.6 0.8 copy.498
  620.5 1.1 copy.499
  (60 shorter events, 0.4 us)
Async XLA Ops:
  7.2 394.2 %copy-start = (f32[6,320,8]{1,2,0:T(8,128)S(1)}, f32[6,320,8]{1,2,0:T(8,128)}, u32[]{:S(2)}) copy-start(f32[6,320,8]{1,2,0:T(8,128)} %param.27) | copy-start | bytes 184324
  7.2 41.5 %all-gather.9.cloned.1.call-start = ((), (), s32[]{:S(2)}) async-start(), calls=%async_computation.5 | async-start | bytes 1843200 | tf_op jit(solution)/shard_map/all_gather | solution.py:570
  10.5 71.0 %all-gather.5.cloned.1.call-start = ((), (), s32[]{:S(2)}) async-start(), calls=%async_computation.1 | async-start | bytes 3317760 | tf_op jit(solution)/shard_map/all_gather | solution.py:568
  11.3 151.0 %all-gather.7.cloned.1.call-start = ((), (), s32[]{:S(2)}) async-start(), calls=%async_computation.2 | async-start | bytes 13271040 | tf_op jit(solution)/shard_map/all_gather | solution.py:570
  48.7 498.1 %all-reduce.4.cloned.1.call-start = ((), (), s32[]{:S(2)}) async-start(), calls=%async_computation.4 | async-start | bytes 491520 | tf_op jit(solution)/shard_map/psum | solution.py:595
  394.7 7.6 %copy-start.2 = (f32[6,320,1280]{2,1,0:T(8,128)S(1)}, f32[6,320,1280]{2,1,0:T(8,128)}, u32[]{:S(2)}) copy-start(f32[6,320,1280]{2,1,0:T(8,128)} %get-tuple-element.53) | copy-start | bytes 29491204
  402.4 9.1 %copy-start.16 = (f32[80]{0:T(128)S(1)}, f32[80]{0:T(128)}, u32[]{:S(2)}) copy-start(f32[80]{0:T(128)} %param.21) | copy-start | bytes 964
  402.4 9.1 %copy-start.19 = (f32[1,128]{1,0:T(1,128)S(1)}, f32[1,128]{1,0:T(1,128)}, u32[]{:S(2)}) copy-start(f32[1,128]{1,0:T(1,128)} %get-tuple-element.52) | copy-start | bytes 1540
  402.4 9.6 %copy-start.14 = (f32[1,1280]{1,0:T(1,128)S(1)}, f32[1,1280]{1,0:T(1,128)}, u32[]{:S(2)}) copy-start(f32[1,1280]{1,0:T(1,128)} %get-tuple-element.51) | copy-start | bytes 15364
  402.4 9.6 %copy-start.15 = (f32[1,1280]{1,0:T(1,128)S(1)}, f32[1,1280]{1,0:T(1,128)}, u32[]{:S(2)}) copy-start(f32[1,1280]{1,0:T(1,128)} %get-tuple-element.50) | copy-start | bytes 15364
  402.4 60.3 %copy-start.17 = (f32[80]{0:T(128)S(1)}, f32[80]{0:T(128)}, u32[]{:S(2)}) copy-start(f32[80]{0:T(128)} %param.25) | copy-start | bytes 964
  402.4 60.8 %copy-start.11 = (f32[2,1280]{1,0:T(2,128)S(1)}, f32[2,1280]{1,0:T(2,128)}, u32[]{:S(2)}) copy-start(f32[2,1280]{1,0:T(2,128)} %param.20) | copy-start | bytes 30724
  402.4 60.8 %copy-start.12 = (f32[2,1280]{1,0:T(2,128)S(1)}, f32[2,1280]{1,0:T(2,128)}, u32[]{:S(2)}) copy-start(f32[2,1280]{1,0:T(2,128)} %param.24) | copy-start | bytes 30724
  411.4 205.2 %reduce-scatter.2.cloned.1.call-start = ((), (), s32[]{:S(2)}) async-start(), calls=%async_computation.3 | async-start | bytes 6635520 | tf_op jit(solution)/shard_map/reduce_scatter | solution.py:588
  462.7 108.0 %copy-start.13 = (f32[2,1280]{1,0:T(2,128)}, f32[2,1280]{1,0:T(2,128)S(1)}, u32[]{:S(2)}) copy-start(f32[2,1280]{1,0:T(2,128)S(1)} %get-tuple-element.146) | copy-start | bytes 30724
  462.7 108.1 %copy-start.18 = (f32[80]{0:T(128)}, f32[80]{0:T(128)S(1)}, u32[]{:S(2)}) copy-start(f32[80]{0:T(128)S(1)} %get-tuple-element.147) | copy-start | bytes 964
  556.5 42.2 %copy-start.6 = (f32[320,160]{0,1:T(8,128)S(1)}, f32[320,160]{0,1:T(8,128)}, u32[]{:S(2)}) copy-start(f32[320,160]{0,1:T(8,128)} %param.19) | copy-start | bytes 614404
  556.5 42.2 %copy-start.7 = (f32[320,160]{0,1:T(8,128)S(1)}, f32[320,160]{0,1:T(8,128)}, u32[]{:S(2)}) copy-start(f32[320,160]{0,1:T(8,128)} %param.18) | copy-start | bytes 614404
  556.5 42.2 %copy-start.10 = (f32[2,320,160]{1,2,0:T(8,128)S(1)}, f32[2,320,160]{1,2,0:T(8,128)}, u32[]{:S(2)}) copy-start(f32[2,320,160]{1,2,0:T(8,128)} %param.23) | copy-start | bytes 1228804
  556.5 43.3 %copy-start.3 = (f32[4,160,320]{2,1,0:T(8,128)S(1)}, f32[4,160,320]{2,1,0:T(8,128)}, u32[]{:S(2)}) copy-start(f32[4,160,320]{2,1,0:T(8,128)} %param.17) | copy-start | bytes 2457604
  556.5 43.3 %copy-start.5 = (f32[4,160,320]{2,1,0:T(8,128)S(1)}, f32[4,160,320]{2,1,0:T(8,128)}, u32[]{:S(2)}) copy-start(f32[4,160,320]{2,1,0:T(8,128)} %param.22) | copy-start | bytes 2457604
  597.1 19.4 %copy-start.8 = (f32[6,320,8]{1,2,0:T(8,128)}, f32[6,320,8]{1,2,0:T(8,128)S(1)}, u32[]{:S(2)}) copy-start(f32[6,320,8]{1,2,0:T(8,128)S(1)} %psum.31) | copy-start | bytes 184324
  601.3 18.4 %copy-start.9 = (bf16[256,1280]{1,0:T(8,128)(2,1)S(1)}, bf16[256,1280]{1,0:T(8,128)(2,1)}, u32[]{:S(2)}) copy-start(bf16[256,1280]{1,0:T(8,128)(2,1)} %get-tuple-element.142) | copy-start | bytes 1966084
  601.3 19.2 %copy-start.4 = (f32[256,1280]{1,0:T(8,128)S(1)}, f32[256,1280]{1,0:T(8,128)}, u32[]{:S(2)}) copy-start(f32[256,1280]{1,0:T(8,128)} %get-tuple-element.143) | copy-start | bytes 3932164
  601.3 20.3 %copy-start.1 = (f32[6,320,8]{1,2,0:T(8,128)S(1)}, f32[6,320,8]{1,2,0:T(8,128)}, u32[]{:S(2)}) copy-start(f32[6,320,8]{1,2,0:T(8,128)} %param.27) | copy-start | bytes 184324
Sparse Core Ops, SparseCore 0:
  10.6 38.0 all-gather.8
  51.2 30.3 all-gather.4
  83.4 68.6 all-gather.6
  411.5 135.2 all-reduce.3
  550.2 61.3 reduce-scatter.1

commit v2 on v1

--- a/solution.py
+++ b/solution.py
@@ -19,7 +19,7 @@
 F32 = jnp.float32
 BF16 = jnp.bfloat16
 MESH = pl.DeviceIdType.MESH
-VMEM_LIMIT = 62 * 1024 * 1024
+VMEM_LIMIT = 67_000_000
 
 
 def nn(a, b):
@@ -406,53 +406,278 @@
     )(q, k, v, lse, dhb, w_out, c_row, starts)
 
 
+def halves(value):
+    high = value.astype(BF16)
+    return high, (value - high.astype(F32)).astype(BF16)
+
+
+def dot_split(small, big, contract):
+    count = small.shape[0]
+    high, low = halves(small)
+    big_high, big_low = halves(big)
+    both = contract(jnp.concatenate([high.astype(F32), low.astype(F32)], axis=0).astype(BF16), big_high)
+    return both[:count] + both[count:] + contract(high, big_low)
+
+
+def plane(data_par):
+    half = data_par // 2
+    side = math.isqrt(half)
+    return (side, half // side) if side * side == half else (1, half)
+
+
+class PlaneScatter:
+    def __init__(self, n_data, gb, core, a1, b1, a2, b2, sems):
+        self.ys, self.xs = plane(n_data)
+        self.gb, self.core, self.a1, self.b1, self.a2, self.b2 = gb, core, a1, b1, a2, b2
+        (self.c_s, self.c_r, self.s1, self.ra1, self.rb1, self.s2, self.ra2, self.rb2) = sems
+        me = lax.axis_index("dp")
+        self.c = lax.rem(me, 2)
+        self.x = lax.rem(me // 2, self.xs)
+        self.y = me // (2 * self.xs)
+        self.half = gb.shape[0] // 2
+
+    def send(self, src, dst, ssem, rsem, y, x, c):
+        return pltpu.make_async_remote_copy(
+            src_ref=src, dst_ref=dst, send_sem=ssem, recv_sem=rsem,
+            device_id={"dp": (y * self.xs + x) * 2 + c}, device_id_type=MESH,
+        )
+
+    def copies_core(self):
+        other = 1 - self.c
+        src = self.gb.at[:, :, :, other]
+        return [self.send(src, self.core, self.c_s, self.c_r, self.y, self.x, other)]
+
+    def copies_one(self):
+        out, h = [], self.half
+        for o in range(1, self.xs):
+            to = lax.rem(self.x + o, self.xs)
+            src = self.core.at[:h, :, to]
+            out.append(self.send(src, self.a1.at[o - 1], self.s1.at[0, o], self.ra1.at[o], self.y, to, self.c))
+        for o in range(1, self.ys):
+            to = lax.rem(self.y + o, self.ys)
+            src = self.core.at[h:, to]
+            out.append(self.send(src, self.b1.at[o - 1], self.s1.at[1, o], self.rb1.at[o], to, self.x, self.c))
+        return out
+
+    def copies_two(self):
+        out, h = [], self.half
+        for o in range(1, self.ys):
+            to = lax.rem(self.y + o, self.ys)
+            src = self.core.at[:h, to, self.x]
+            out.append(self.send(src, self.a2.at[o - 1], self.s2.at[0, o], self.ra2.at[o], to, self.x, self.c))
+        for o in range(1, self.xs):
+            to = lax.rem(self.x + o, self.xs)
+            src = self.core.at[h:, self.y, to]
+            out.append(self.send(src, self.b2.at[o - 1], self.s2.at[1, o], self.rb2.at[o], self.y, to, self.c))
+        return out
+
+    def start(self, copies):
+        for copy in copies:
+            copy.start()
+
+    def arrive(self, copies):
+        for copy in copies:
+            copy.wait_recv()
+
+    def sum_core(self):
+        self.arrive(self.copies_core())
+
+        def one(i, _):
+            m, rest = i // (self.ys * self.xs), lax.rem(i, self.ys * self.xs)
+            y, x = rest // self.xs, lax.rem(rest, self.xs)
+            total = self.core[m, y, x].astype(F32) + self.gb[m, y, x, self.c].astype(F32)
+            self.core[m, y, x] = total.astype(BF16)
+            return 0
+
+        lax.fori_loop(0, self.gb.shape[0] * self.ys * self.xs, one, 0)
+
+    def sum_one(self):
+        self.arrive(self.copies_one())
+        h = self.half
+
+        def along_y(i, _):
+            m, y = i // self.ys, lax.rem(i, self.ys)
+            total = self.core[m, y, self.x].astype(F32)
+            for o in range(1, self.xs):
+                total += self.a1[o - 1, m, y].astype(F32)
+            self.core[m, y, self.x] = total.astype(BF16)
+            return 0
+
+        def along_x(i, _):
+            m, x = i // self.xs, lax.rem(i, self.xs)
+            total = self.core[h + m, self.y, x].astype(F32)
+            for o in range(1, self.ys):
+                total += self.b1[o - 1, m, x].astype(F32)
+            self.core[h + m, self.y, x] = total.astype(BF16)
+            return 0
+
+        lax.fori_loop(0, h * self.ys, along_y, 0)
+        lax.fori_loop(0, h * self.xs, along_x, 0)
+
+    def sum_two(self, out, factor):
+        self.arrive(self.copies_two())
+        h = self.half
+
+        def one(m, _):
+            total = self.core[m, self.y, self.x].astype(F32)
+            for o in range(1, self.ys):
+                total += self.a2[o - 1, m].astype(F32)
+            out[m] = factor * total
+            total = self.core[h + m, self.y, self.x].astype(F32)
+            for o in range(1, self.xs):
+                total += self.b2[o - 1, m].astype(F32)
+            out[h + m] = factor * total
+            return 0
+
+        lax.fori_loop(0, h, one, 0)
+
+    def finish(self):
+        for copy in self.copies_core() + self.copies_one() + self.copies_two():
+            copy.wait_send()
+
+    @staticmethod
+    def scratch(n_data, count, rows, cols):
+        ys, xs = plane(n_data)
+        h = count // 2
+        sem = pltpu.SemaphoreType.DMA
+        return [
+            pltpu.VMEM((count, ys, xs, 2, rows, cols), BF16),
+            pltpu.VMEM((count, ys, xs, rows, cols), BF16),
+            pltpu.VMEM((max(xs - 1, 1), h, ys, rows, cols), BF16),
+            pltpu.VMEM((max(ys - 1, 1), h, xs, rows, cols), BF16),
+            pltpu.VMEM((max(ys - 1, 1), h, rows, cols), BF16),
+            pltpu.VMEM((max(xs - 1, 1), h, rows, cols), BF16),
+            sem, sem, sem((2, max(xs, ys))), sem((xs,)), sem((ys,)),
+            sem((2, max(xs, ys))), sem((ys,)), sem((xs,)),
+        ]
+
+
+class Exchange:
+    def __init__(self, axis, size, src_of, dst, ssem, rsem):
+        self.axis, self.size, self.src_of, self.dst, self.ssem, self.rsem = axis, size, src_of, dst, ssem, rsem
+        self.me = lax.axis_index(axis)
+
+    def copy(self, peer, slot):
+        return pltpu.make_async_remote_copy(
+            src_ref=self.src_of(peer), dst_ref=self.dst.at[slot], send_sem=self.ssem.at[peer],
+            recv_sem=self.rsem.at[slot], device_id={self.axis: peer}, device_id_type=MESH,
+        )
+
+    def each(self, do):
+        def one(off, _):
+            do(lax.rem(self.me + off, self.size))
+            return 0
+
+        lax.fori_loop(1, self.size, one, 0)
+
+    def start(self):
+        self.each(lambda peer: self.copy(peer, self.me).start())
+
+    def arrive(self):
+        self.each(lambda peer: self.copy(peer, peer).wait_recv())
+
+    def finish(self):
+        self.each(lambda peer: self.copy(peer, peer).wait_send())
+
+
+def total_of(ref, size):
+    def one(i, total):
+        return total + ref[i]
+
+    return lax.fori_loop(1, size, one, ref[0])
+
+
 def grads_kernel(
-    dims, n1_ref, n2_ref, dhb_ref, g_ref, dx_ref, oc_ref, wqkv_ref, wup_ref, wdn_ref,
-    x_ref, dh_ref, gain_ref,
-    gt_ref, gb_ref, gin_ref, dgain_ref,
-    z_ref, da_ref, sbuf, lbuf, rbuf, ss, ls, rs,
+    dims, n_data, scaling, n1_ref, n2_ref, dhb_ref, g_ref, dx_ref, oc_ref, wqkv_ref, wup_ref, wdn_ref,
+    x_ref, dh_ref, gain_ref, dgain2_ref, dscale_ref, ft_ref, err_ref,
+    gsum_ref, gin_ref, m_out, basis_ref, right_ref, small_ref,
+    abuf, z_ref, da_ref, sbuf, lbuf, m_ref, lsend, lrecv, zrecv, lfull, rrecv, srecv, szrecv,
+    fs, ss, ls, es, ms, l_s, l_r, z_s, z_r, a_s, a_r, r_s, r_r, g_s, g_r, gz_s, gz_r, *plane_refs,
 ):
     n, rows, heads, span = dims
-    me = lax.axis_index("mp")
-    greet(line_peers(n, me))
-
-    def own(i):
+    me, mine = lax.axis_index("mp"), lax.axis_index("dp")
+    width, cols = wup_ref.shape
+    tiles = width // LANE
+
+    def load(m):
+        return pltpu.make_async_copy(err_ref.at[m], m_ref.at[m], es.at[m])
+
+    def save(m):
+        return pltpu.make_async_copy(m_ref.at[m], m_out.at[m], ms.at[m])
+
+    def fetch(k):
+        src = (n2_ref, g_ref, dhb_ref, n1_ref)[k]
+        return pltpu.make_async_copy(src, abuf.at[k % 2], fs.at[k])
+
+    fetch(0).start()
+    fetch(1).start()
+    for m in range(6):
+        load(m).start()
+    greet(line_peers(n, me) + [{"dp": lax.rem(mine + off, n_data)} for off in range(1, n_data)])
+    scatter = PlaneScatter(n_data, *plane_refs[:6], plane_refs[6:])
+    gb = plane_refs[0]
+    ex_left = Exchange("dp", n_data, lambda peer: lsend.at[peer], lrecv, l_s, l_r)
+    ex_line = Exchange("mp", n, lambda peer: zrecv.at[me], zrecv, z_s, z_r)
+    ex_all = Exchange("dp", n_data, lambda peer: lfull.at[mine], lfull, a_s, a_r)
+    ex_right = Exchange("dp", n_data, lambda peer: rrecv.at[mine], rrecv, r_s, r_r)
+    ex_small = Exchange("dp", n_data, lambda peer: srecv.at[mine], srecv, g_s, g_r)
+    ex_small_line = Exchange("mp", n, lambda peer: szrecv.at[me], szrecv, gz_s, gz_r)
+
+
+    def own(e, _):
+        i = jnp.where(lax.rem(e, 2) == 0, n - 1 - e // 2, e // 2)
         total = nt(dx_ref[0, i], wqkv_ref[0])
         total += nt(dx_ref[1, i], wqkv_ref[1])
-        return total + nt(dx_ref[2, i], wqkv_ref[2])
-
-    def copy(i, way):
-        buf, sem = (lbuf, ls) if way == 0 else (rbuf, rs)
+        total += nt(dx_ref[2, i], wqkv_ref[2])
+
+        @pl.when(i == me)
+        def _():
+            gin_ref[...] = total
+
+        @pl.when(i != me)
+        def _():
+            sbuf[i] = total.astype(BF16)
+
+        return 0
+
+    lax.fori_loop(0, n, own, 0)
+
+    def copy(i, way, here=False):
+        slot = i if way == 0 else jnp.where(i == (me if here else me - 1), n, i)
         return pltpu.make_async_remote_copy(
-            src_ref=sbuf.at[i], dst_ref=buf.at[i], send_sem=ss.at[i], recv_sem=sem.at[i],
+            src_ref=sbuf.at[i], dst_ref=lbuf.at[slot], send_sem=ss.at[i], recv_sem=ls.at[slot],
             device_id={"mp": me + 1 - 2 * way}, device_id_type=MESH,
         )
 
-    def step(t, way):
-        i = n - 1 - t if way == 0 else t
-        buf = lbuf if way == 0 else rbuf
-        has = me > 0 if way == 0 else me < n - 1
-
-        @pl.when(i > me if way == 0 else i < me)
+    def launch():
+        @pl.when(me == 0)
         def _():
-            mine = own(i)
-
-            @pl.when(has)
-            def _():
-                copy(i, way).wait_recv()
-                sbuf[i] = (mine + buf[i].astype(F32)).astype(BF16)
-
-            @pl.when(jnp.logical_not(has))
-            def _():
-                sbuf[i] = mine.astype(BF16)
-
-            copy(i, way).start()
+            for i in range(n - 1, 0, -1):
+                copy(i, 0).start()
+
+        @pl.when(me == n - 1)
+        def _():
+            for i in range(n - 1):
+                copy(i, 1).start()
+
+    def relay(r):
+        for way in (0, 1):
+            place = me if way == 0 else n - 1 - me
+            i = n - 1 - r + me if way == 0 else r - (n - 1 - me)
+
+            @pl.when((place >= 1) & (place <= r))
+            def _(i=i, way=way):
+                copy(i, way, True).wait_recv()
+                sbuf[i] = (sbuf[i].astype(F32) + lbuf[i].astype(F32)).astype(BF16)
+                copy(i, way).start()
+
+    launch()
 
     def hidden(i, _):
-        gate = nn(n2_ref[i], wup_ref[...])
+        gate = nn(abuf[0, i], wup_ref[...])
         sig = 1.0 / (1.0 + jnp.exp(-gate))
         z_ref[i] = (gate * sig).astype(BF16)
-        dz = nn(g_ref[i], wdn_ref[...])
+        dz = nn(abuf[1, i], wdn_ref[...])
         da_ref[i] = (dz * (sig * (1.0 + gate * (1.0 - sig)))).astype(BF16)
         return 0
 
@@ -461,25 +686,83 @@
 
     def weight(m, a, b):
         left, right = flat(a), flat(b)
-        gt_ref[m] = tn(right, left)
-        gb_ref[m] = tn(left, right).astype(BF16)
-
-    step(0, 0)
-    step(0, 1)
+        load(m).wait()
+        m_ref[m] = scaling * tn(right, left) + m_ref[m]
+        gb[m] = tn(left, right).reshape(gb.shape[1:]).astype(BF16)
+
+    def factor_rows(m):
+        rows_left = dot_split(ft_ref[m], m_ref[m], nn)
+        per = lsend.shape[1]
+        for t in range(tiles):
+            tile = m * tiles + t
+            lsend[tile // per, lax.rem(tile, per)] = rows_left[:, t * LANE : (t + 1) * LANE]
+
+    fetch(0).wait()
+    fetch(1).wait()
     lax.fori_loop(0, n, hidden, 0)
-    weight(3, n2_ref[...], da_ref[...])
-    weight(5, g_ref[...], z_ref[...])
-    weight(4, dhb_ref[...], oc_ref[...])
-    for t in range(1, n - 1):
-        step(t, 0)
-        step(t, 1)
+    weight(3, abuf[0], da_ref[...])
+    fetch(2).start()
+    weight(5, abuf[1], z_ref[...])
+    fetch(3).start()
+    fetch(2).wait()
+    weight(4, abuf[0], oc_ref[...])
+    relay(1)
+    fetch(3).wait()
 
     def inputs(m, _):
-        weight(m, n1_ref[...], dx_ref[m])
+        weight(m, abuf[1], dx_ref[m])
         return 0
 
     lax.fori_loop(0, 3, inputs, 0)
-    gin_ref[...] = own(me)
+    for tile in range(6 * tiles, lsend.shape[0] * lsend.shape[1]):
+        lsend[tile // lsend.shape[1], tile % lsend.shape[1]] = jnp.zeros((8, LANE), F32)
+
+    def left_rows(m, _):
+        factor_rows(m)
+        return 0
+
+    lax.fori_loop(0, 6, left_rows, 0)
+    lrecv[mine] = lsend[mine]
+    ex_left.start()
+    scatter.start(scatter.copies_core())
+    for m in range(6):
+        save(m).start()
+    ex_left.arrive()
+    zrecv[me] = total_of(lrecv, n_data)
+    ex_line.start()
+    for r in range(2, n - 1):
+        relay(r)
+    scatter.sum_core()
+    scatter.start(scatter.copies_one())
+    ex_line.arrive()
+    lfull[mine] = total_of(zrecv, n)
+    ex_all.start()
+    ex_all.arrive()
+
+    per = lfull.shape[1]
+    basis = jnp.stack(
+        [
+            jnp.concatenate([lfull[t // per, t % per] for t in range(m * tiles, (m + 1) * tiles)], axis=1)
+            for m in range(6)
+        ]
+    )
+    row = lax.broadcasted_iota(jnp.int32, (1, 8, 1), 1)
+    for index in range(8):
+        vector = basis[:, index : index + 1, :]
+        vector = vector * lax.rsqrt(jnp.sum(vector * vector, axis=-1, keepdims=True) + 1e-12)
+        onto = jnp.where(row > index, jnp.sum(basis * vector, axis=-1, keepdims=True), 0.0)
+        basis = jnp.where(row == index, vector, basis - onto * vector)
+    basis_ref[...] = basis
+
+    def right_rows(m, _):
+        rrecv[mine, m] = dot_split(basis_ref[m], m_ref[m], nt)
+        return 0
+
+    lax.fori_loop(0, 6, right_rows, 0)
+    ex_right.start()
+    scatter.sum_one()
+    scatter.start(scatter.copies_two())
+
 
     @pl.when(me > 0)
     def _():
@@ -488,16 +771,34 @@
 
     @pl.when(me < n - 1)
     def _():
-        copy(me, 1).wait_recv()
-        gin_ref[...] += rbuf[me].astype(F32)
+        copy(me, 1, True).wait_recv()
+        gin_ref[...] += lbuf[n].astype(F32)
 
     x = x_ref[...].astype(F32)
     scale = lax.rsqrt(jnp.mean(x * x, axis=-1, keepdims=True) + EPSILON)
     unit = x * scale
     grad = gin_ref[...]
-    dgain_ref[...] = jnp.sum(grad * unit, axis=0, keepdims=True)
+    dgain = jnp.sum(grad * unit, axis=0, keepdims=True)
+    srecv[mine] = jnp.zeros(srecv.shape[1:], F32)
+    for t in range(tiles):
+        at = slice(t * LANE, (t + 1) * LANE)
+        srecv[mine, t // 8, t % 8 : t % 8 + 1, :] = scaling * dgain[:, at]
+        t2 = tiles + t
+        srecv[mine, t2 // 8, t2 % 8 : t2 % 8 + 1, :] = scaling * dgain2_ref[:, at]
+    t3 = 2 * tiles
+    srecv[mine, t3 // 8, t3 % 8 : t3 % 8 + 1, :] = scaling * dscale_ref[...]
+    ex_small.start()
     du = grad * gain_ref[...]
     gin_ref[...] = dh_ref[...] + scale * (du - unit * jnp.mean(du * unit, axis=-1, keepdims=True))
+    ex_small.arrive()
+    szrecv[me] = total_of(srecv, n_data)
+    ex_small_line.start()
+    ex_right.arrive()
+    right_ref[...] = total_of(rrecv, n_data)
+    scatter.sum_two(gsum_ref, scaling)
+    ex_small_line.arrive()
+    small_ref[...] = total_of(szrecv, n)
+
     for i in range(n):
 
         @pl.when(me < i)
@@ -508,43 +809,80 @@
         def _(i=i):
             copy(i, 1).wait_send()
 
-
-def grads(dims, n1, n2, dhb, g_all, dx, oc, wqkv, w_up, w_down, x, dh, gain):
+    for exchange in (ex_left, ex_line, ex_all, ex_right, ex_small, ex_small_line):
+        exchange.finish()
+    scatter.finish()
+    for m in range(6):
+        save(m).wait()
+
+
+def grads(dims, scaling, n1, n2, dhb, g_all, dx, oc, wqkv, w_up, w_down, x, dh, gain, dgain2, dscale, ft, err):
     n, rows = dims[:2]
+    n_data = lax.axis_size("dp")
     width, cols = w_up.shape
+    own_rows = width // n_data
     every = pltpu.VMEM((n, rows, width), BF16)
+    sem = pltpu.SemaphoreType.DMA
+    per = -(-(6 * width // LANE) // n_data)
+    small = -(-(2 * width // LANE + 1) // 8)
+
+    def f32(*shape):
+        return pltpu.VMEM(shape, F32)
+
     return pl.pallas_call(
-        functools.partial(grads_kernel, dims),
+        functools.partial(grads_kernel, dims, n_data, scaling),
         out_shape=(
+            jax.ShapeDtypeStruct((6, own_rows, cols), F32),
+            jax.ShapeDtypeStruct((rows, width), F32),
             jax.ShapeDtypeStruct((6, cols, width), F32),
-            jax.ShapeDtypeStruct((6, width, cols), BF16),
-            jax.ShapeDtypeStruct((rows, width), F32),
-            jax.ShapeDtypeStruct((1, width), F32),
+            jax.ShapeDtypeStruct((6, 8, width), F32),
+            jax.ShapeDtypeStruct((6, 8, cols), F32),
+            jax.ShapeDtypeStruct((small, 8, LANE), F32),
         ),
-        in_specs=vmem(12),
-        out_specs=vmem(4),
+        in_specs=[pl.BlockSpec(memory_space=pl.ANY)] * 4 + vmem(11) + [pl.BlockSpec(memory_space=pl.ANY)],
+        out_specs=vmem(2) + [pl.BlockSpec(memory_space=pl.ANY)] + vmem(3),
         scratch_shapes=[
+            pltpu.VMEM((2, n, rows, width), BF16),
             pltpu.VMEM((n, rows, cols), BF16),
             pltpu.VMEM((n, rows, cols), BF16),
-            every, every, every,
-            pltpu.SemaphoreType.DMA((n,)),
-            pltpu.SemaphoreType.DMA((n,)),
-            pltpu.SemaphoreType.DMA((n,)),
+            every,
+            pltpu.VMEM((n + 1, rows, width), BF16),
+            f32(6, cols, width),
+            f32(n_data, per, 8, LANE), f32(n_data, per, 8, LANE), f32(n, per, 8, LANE),
+            f32(n_data, per, 8, LANE), f32(n_data, 6, 8, cols),
+            f32(n_data, small, 8, LANE), f32(n, small, 8, LANE),
+            sem((4,)), sem((n,)), sem((n + 1,)), sem((6,)), sem((6,)),
+            sem((n_data,)), sem((n_data,)), sem((n,)), sem((n,)), sem((n_data,)), sem((n_data,)),
+            sem((n_data,)), sem((n_data,)), sem((n_data,)), sem((n_data,)), sem((n,)), sem((n,)),
+            *PlaneScatter.scratch(n_data, 6, own_rows, cols),
         ],
         compiler_params=params(3),
         name="grads",
-    )(n1, n2, dhb, g_all, dx, oc, wqkv, w_up, w_down, x, dh, gain)
-
-
-def orthonormal(matrix):
-    columns = []
-    for index in range(matrix.shape[-1]):
-        vector = matrix[..., index]
-        for basis in columns:
-            vector = vector - jnp.sum(basis * vector, axis=-1, keepdims=True) * basis
-        vector = vector * lax.rsqrt(jnp.sum(vector * vector, axis=-1, keepdims=True) + 1e-12)
-        columns.append(vector)
-    return jnp.stack(columns, axis=-1)
+    )(n1, n2, dhb, g_all, dx, oc, wqkv, w_up, w_down, x, dh, gain, dgain2, dscale, ft, err)
+
+
+def close_kernel(m_ref, right_ref, basis_ref, out_ref):
+    right, basis = right_ref[0], basis_ref[0]
+    (rh, rl), (bh, bl) = halves(right), halves(basis)
+    left = jnp.concatenate([rh, rl, rh], axis=0)
+    out_ref[0] = m_ref[0] - tn(left, jnp.concatenate([bh, bh, bl], axis=0))
+
+
+def close(m, right, basis):
+    cols, width = m.shape[1:]
+
+    def spec(*shape):
+        return pl.BlockSpec((1, *shape), lambda i: (i, 0, 0))
+
+    return pl.pallas_call(
+        close_kernel,
+        grid=(6,),
+        out_shape=jax.ShapeDtypeStruct(m.shape, F32),
+        in_specs=[spec(cols, width), spec(8, cols), spec(8, width)],
+        out_specs=spec(cols, width),
+        compiler_params=params(),
+        name="close",
+    )(m, right, basis)
 
 
 def on_device(
@@ -579,27 +917,22 @@
     n1, q, k, v, lse, oc, o_full = attend(dims, activations, wqkv, gains[:1], c_row, starts)
     output, dh, n2, g_all, dhb, dgain2 = middle(dims, activations, cotangent, o_full, w_full, gains[1:])
     dx, dc = back(dims, q, k, v, lse, dhb, w_mine[0], c_row, starts)
-    gt, gb, grad_input, dgain1 = grads(
-        dims, n1, n2, dhb, g_all, dx, oc, wqkv, w_mine[1], w_mine[2], activations, dh, gains[:1]
+    grad_scale_local = dc[0, :HD] / factor * (SCALE_BASE / math.sqrt(HD)) * jax.nn.sigmoid(scale_param)
+    dscale = jnp.pad(grad_scale_local, (0, LANE - HD))[None]
+    summed, grad_input, stored, basis, right, small = grads(
+        dims, scaling, n1, n2, dhb, g_all, dx, oc, wqkv, w_mine[1], w_mine[2], activations, dh, gains[:1],
+        dgain2, dscale, jnp.swapaxes(factors, 1, 2), error_buffer[0],
     )
-
-    grad_scale_local = dc[0, :HD] / factor * (SCALE_BASE / math.sqrt(HD)) * jax.nn.sigmoid(scale_param)
-    parts = gb.reshape(6, data_par, own_rows, cols).transpose(1, 0, 2, 3)
-    summed = scaling * lax.psum_scatter(parts, "dp", scatter_dimension=0).astype(F32)
     grad_in = summed[:4]
     grad_out = jnp.swapaxes(summed[4:], 1, 2)
-
-    stored = scaling * gt + error_buffer[0]
-    left_local = jnp.einsum("kcd,kcr->kdr", stored, factors, precision=HIGHEST)
-    gain_local = scaling * jnp.concatenate([dgain1, dgain2])
-    left, grad_gain, grad_scale = lax.psum(
-        (left_local, gain_local, scaling * grad_scale_local), ("dp", "mp")
-    )
-    basis = orthonormal(left)
-    right = lax.psum(jnp.einsum("kcd,kdr->kcr", stored, basis, precision=HIGHEST), "dp")
-    error_new = (stored - jnp.einsum("kcr,kdr->kcd", right, basis, precision=HIGHEST))[None]
-    mine_basis = lax.dynamic_slice_in_dim(basis, my_data * own_rows, own_rows, 1)
-    mine = jnp.einsum("kdr,kcr->kdc", mine_basis, right, precision=HIGHEST)
+    error_new = close(stored, right, basis)[None]
+    tiles = width // LANE
+    small = small.reshape(-1, LANE)
+    grad_gain = small[: 2 * tiles].reshape(2, width)
+    grad_scale = small[2 * tiles, :HD]
+    mine_basis = lax.dynamic_slice_in_dim(basis, my_data * own_rows, own_rows, 2)
+    mine = jnp.einsum("krd,krc->kdc", mine_basis, right, precision=HIGHEST)
+    right = jnp.swapaxes(right, 1, 2)
     mom_in_new = MOMENTUM * mom_in + mine[:4]
     new_in = w_in - RATE * mom_in_new
     mom_out_new = MOMENTUM * mom_out + jnp.swapaxes(mine[4:], 1, 2)

time: 632 us -> 456 us (0.72)
  waiting for transfers between devices: 150 us -> 68.2 us
  blocking collectives: 77 us -> 0 us
  Pallas kernels: 309 us -> 348 us
  matrix products: 39.9 us -> 2.46 us
  other arithmetic: 18 us -> 9.37 us
  local copies, waits for them, and re-layouts: 20.1 us -> 13.7 us
    psum x1 -> x0, waiting for transfers between devices: 83 us -> none  [on_device(): lax.psum((left_local, gain_local, scaling * grad_scale_local), ('dp', 'mp'))]
    psum x2 -> x0, blocking collectives: 77 us -> none  [the longest x1 50.7 us: on_device(): lax.psum((left_local, gain_local, scaling * grad_scale_local), ('dp', 'mp'))]
    pallas_call x1 -> x2, Pallas kernels: 64.4 us -> 103 us  [the longest x1 93.5 us: grads(): pl.pallas_call(functools.partial(grads_kernel, dims, n_data, scaling), ou...]
    dot_general x4 -> x1, matrix products: 39.9 us -> 2.46 us  [on_device(): mine = jnp.einsum('krd,krc->kdc', mine_basis, right, precision=HIGHEST)]
    reshape x1, local copies, waits for them, and re-layouts: 6.63 us -> 0.01 us  [on_device(): grad_gain = small[:2 * tiles].reshape(2, width)]
  transfers between devices with their start and end apart: 5 -> 3, of which waited for: 3 -> 2; matrix products, arithmetic and copies ran while one was open for 8% -> 1% of each run, Pallas kernels for 13% -> 18%
where the time goes in v2:
time: 456 us
  Pallas kernels  348 us (76%)
  waiting for transfers between devices  68.2 us (15%)
  between operations  13.9 us (3%)
  local copies, waits for them, and re-layouts  13.7 us (3%)
  other arithmetic  9.37 us (2%)
    pallas_call x1, Pallas kernels, middle(): pl.pallas_call(functools.partial(middle_kernel, dims), out_shape=(jax.Sha...  138 us
    pallas_call x1, Pallas kernels, grads(): pl.pallas_call(functools.partial(grads_kernel, dims, n_data, scaling), ou...  93.5 us
    pallas_call x1, Pallas kernels, attend(): pl.pallas_call(functools.partial(attend_kernel, dims), out_shape=(jax.Sha...  80.2 us
    all_gather x1, waiting for transfers between devices, on_device(): lax.all_gather(tail, 'mp', axis=0)  37.3 us
    all_gather x1, waiting for transfers between devices, on_device(): wqkv = lax.all_gather(shards[:3], 'dp', axis=1, tiled=True)  30.8 us
    pallas_call x1, Pallas kernels, back(): pl.pallas_call(functools.partial(back_kernel, dims), out_shape=(jax.Shape...  26.4 us
    pallas_call x1, Pallas kernels, close(): pl.pallas_call(close_kernel, grid=(6,), out_shape=jax.ShapeDtypeStruct(m....  9.73 us
  transfers between devices with their start and end apart: 3, of which 2 were waited for; matrix products, arithmetic and copies ran while one was open for 1% of the time, Pallas kernels for 18%

profile of v2, /device:TPU:0, one launch (start us, length us, event | category | flops | bytes accessed | tf_op | source)
XLA Modules:
  0.0 455.6 jit_solution(12598169500671979298)
XLA Ops:
  7.2 0.0 all-gather.9.cloned.1.call-start
  7.2 1.3 convert.13
  8.5 0.0 copy-start.12
  8.5 0.0 copy-start.10
  8.5 0.0 copy-start.6
  8.5 1.1 convert_bitcast_fusion
  9.6 0.8 pad_maximum_fusion
  10.5 0.0 all-gather.9.cloned.1.call-update
  10.5 0.0 all-gather.5.cloned.1.call-start
  10.5 0.8 slice.64
  11.3 0.0 all-gather.5.cloned.1.call-update
  11.3 0.0 all-gather.7.cloned.1.call-start
  11.4 37.3 %all-gather.9.cloned.1.call-done = bf16[12,160,320]{2,1,0:T(8,128)(2,1)} async-done(((bf16[3,160,320]{2,1,0:T(8,128)(2,1)}), bf16[12,160,320]{2,1,0:T(8,128)(2,1)}) %all-gather.9.cloned.1.call-update) | async-done | bytes 1228816 | tf_op jit(solution)/shard_map/all_gather | solution.py:908
  48.7 0.0 all-gather.7.cloned.1.call-update
  48.7 0.0 copy-done.12
  48.7 0.2 reduce-window.8
  48.9 0.1 select_reduce_fusion
  49.0 1.0 copy.34.st_ref
  50.1 0.0 copy-done.10
  50.1 0.0 copy-done.6
  50.1 0.6 fusion.6
  50.7 30.8 %all-gather.5.cloned.1.call-done.w_ref.wqkv_ref = bf16[3,1280,320]{2,1,0:T(8,128)(2,1)} async-done(((bf16[3,160,320]{2,1,0:T(8,128)(2,1)}), bf16[3,1280,320]{2,1,0:T(8,128)(2,1)}) %all-gather.5.cloned.1.call-update) | async-done | bytes 2457616 | tf_op jit(solution)/shard_map/all_gather | solution.py:906
  81.5 0.6 tile.2
  82.1 80.2 %attend.1 = (bf16[4,256,1280]{2,1,0:T(8,128)(2,1)}, bf16[4,1024,128]{2,1,0:T(8,128)(2,1)}, bf16[4,1024,128]{2,1,0:T(8,128)(2,1)}, bf16[4,1024,128]{2,1,0:T(8,128...) custom-call(bf16[256,1280]{1,0:T(8,128)(2,1)} %x_ref.5, ...), custom_call_target="tpu_custom_call" | custom-call | tf_op jit(solution)/shard_map/attend/pallas_call | solution.py:229
  162.3 0.0 all-gather.7.cloned.1.call-done.w_ref
  162.4 137.9 %middle.1 = (bf16[256,1280]{1,0:T(8,128)(2,1)}, f32[256,1280]{1,0:T(8,128)}, bf16[4,256,1280]{2,1,0:T(8,128)(2,1)}, bf16[4,256,1280]{2,1,0:T(8,128)(2,1)}, bf16[...) custom-call(bf16[256,1280]{1,0:T(8,128)(2,1)} %x_ref.5, bf16[256,1280]{1,0:T(8,128)(2,1)} %g_ref.1, ...), custom_call_target="tpu_custom_call" | custom-call | tf_op jit(solution)/shard_map/middle/pallas_call | solution.py:314
  300.3 3.5 dynamic-slice_bitcast_fusion
  303.8 26.4 %back.1 = (bf16[3,4,256,320]{3,2,1,0:T(8,128)(2,1)}, f32[1,128]{1,0:T(1,128)}) custom-call(bf16[4,1024,128]{2,1,0:T(8,128)(2,1)} %get-tuple-element.43.q_ref, bf16[4,1024,128]{2,1,0:T(8,128)(2,1)} %get-tuple-element.44.k_ref, bf16[4,1024,128]{2,1,0:T(8,128)(2,1)} %get-tuple-element.45.v_ref, f32[4,1024,1]{2,1,0:T(8,128)} %get-tuple-element.46.lse_ref, ...), custom_call_target="tpu_custom_call" | custom-call | tf_op jit(solution)/shard_map/back/pallas_call | solution.py:388
  330.2 0.7 divide_multiply_fusion
  330.9 0.5 pad_bitcast_fusion.dscale_ref
  331.4 93.5 %grads.1 = (f32[6,160,320]{2,1,0:T(8,128)}, f32[256,1280]{1,0:T(8,128)}, f32[6,320,1280]{2,1,0:T(8,128)}, f32[6,8,1280]{2,1,0:T(8,128)}, f32[6,8,320]{2,1,0:T(8,128)}, /*index=5*/f32[3,8,128]{2,1,0:T(8,128)}) custom-call(bf16[4,256,1280]{2,1,0:T(8,128)(2,1)} %get-tuple-element.39.n1_ref, bf16[4,256,1280]{2,1,0:T(8,128)(2,1)} %get-tuple-element.40.n2_ref, ...), custom_call_target="tpu_custom_call" | custom-call | tf_op jit(solution)/shard_map/grads/pallas_call | solution.py:832
  424.9 2.2 slice.58
  427.2 1.8 slice_bitcast_fusion.1
  429.0 0.0 copy-start.8
  429.0 0.0 copy-start.11
  429.0 9.7 %close.1 = f32[6,320,1280]{2,1,0:T(8,128)} custom-call(f32[6,320,1280]{2,1,0:T(8,128)} %get-tuple-element.57.m_ref, f32[6,8,320]{2,1,0:T(8,128)} %get-tuple-element.56.right_ref, f32[6,8,1280]{2,1,0:T(8,128)} %get-tuple-element.55.basis_ref), custom_call_target="tpu_custom_call" | custom-call | tf_op jit(solution)/shard_map/close/pallas_call | solution.py:877
  438.7 2.5 fusion.1
  441.2 0.0 copy-done.8
  441.2 0.0 copy-done.11
  441.2 0.0 copy-start.7
  441.3 0.5 multiply_subtract_fusion.2
  441.8 0.0 copy-start.9
  441.8 0.0 copy-start.1
  441.8 0.0 copy-start.2
  441.8 0.0 copy-start.5
  441.8 3.0 multiply_subtract_fusion
  444.8 0.0 copy-done.7
  444.8 0.0 copy-done.9
  444.8 0.0 copy-start.4
  444.8 0.0 copy-start
  444.9 0.6 multiply_subtract_fusion.1
  445.5 0.0 copy-done.1
  445.5 0.0 copy-done.2
  445.5 0.0 copy-done.5
  445.5 1.1 maximum_subtract_fusion
  446.5 0.0 copy-start.3
  446.5 0.0 copy-done.4
  446.5 0.8 copy.39
  447.4 0.0 copy-done
  447.4 1.1 copy.40
  448.4 0.0 copy-done.3
  448.4 0.6 copy.41
  (4 shorter events, 0.0 us)
Async XLA Ops:
  7.2 41.5 %all-gather.9.cloned.1.call-start = ((), (), s32[]{:S(2)}) async-start(), calls=%async_computation.2 | async-start | bytes 1843200 | tf_op jit(solution)/shard_map/all_gather | solution.py:908
  8.5 40.3 %copy-start.12 = (s32[1,8]{1,0:T(1,128)S(1)}, s32[1,8]{1,0:T(1,128)}, u32[]{:S(2)}) copy-start(s32[1,8]{1,0:T(1,128)} %param.16) | copy-start | bytes 100
  8.5 41.5 %copy-start.10 = (f32[80]{0:T(128)S(1)}, f32[80]{0:T(128)}, u32[]{:S(2)}) copy-start(f32[80]{0:T(128)} %param.21) | copy-start | bytes 964
  8.5 41.5 %copy-start.6 = (f32[2,1280]{1,0:T(2,128)S(1)}, f32[2,1280]{1,0:T(2,128)}, u32[]{:S(2)}) copy-start(f32[2,1280]{1,0:T(2,128)} %param.20) | copy-start | bytes 30724
  10.5 71.0 %all-gather.5.cloned.1.call-start = ((), (), s32[]{:S(2)}) async-start(), calls=%async_computation | async-start | bytes 3317760 | tf_op jit(solution)/shard_map/all_gather | solution.py:906
  11.3 151.0 %all-gather.7.cloned.1.call-start = ((), (), s32[]{:S(2)}) async-start(), calls=%async_computation.1 | async-start | bytes 13271040 | tf_op jit(solution)/shard_map/all_gather | solution.py:908
  429.0 12.2 %copy-start.8 = (f32[3,8,128]{2,1,0:T(8,128)S(1)}, f32[3,8,128]{2,1,0:T(8,128)}, u32[]{:S(2)}) copy-start(f32[3,8,128]{2,1,0:T(8,128)} %get-tuple-element.54) | copy-start | bytes 36868
  429.0 12.2 %copy-start.11 = (f32[80]{0:T(128)S(1)}, f32[80]{0:T(128)}, u32[]{:S(2)}) copy-start(f32[80]{0:T(128)} %param.25) | copy-start | bytes 964
  441.2 3.6 copy-start.7
  441.8 3.1 copy-start.9
  441.8 3.7 copy-start.1
  441.8 3.7 copy-start.2
  441.8 3.7 copy-start.5
  444.8 1.7 copy-start.4
  444.8 2.5 copy-start
  446.5 1.9 copy-start.3
Sparse Core Ops, SparseCore 0:
  10.6 38.0 all-gather.8
  51.2 30.3 all-gather.4
  83.4 68.7 all-gather.6

commit v3 on v2

--- a/solution.py
+++ b/solution.py
@@ -58,14 +58,13 @@
 
 
 class LineGather:
-    def __init__(self, n, me, own, buf, ssem, rsem):
-        self.n, self.me, self.own, self.buf = n, me, own, buf
+    def __init__(self, n, me, source, buf, ssem, rsem):
+        self.n, self.me, self.source, self.buf = n, me, source, buf
         self.ssem, self.rsem = ssem, rsem
 
     def copy(self, slot, hop, way):
-        src = self.own if hop == 0 else self.buf.at[slot]
         return pltpu.make_async_remote_copy(
-            src_ref=src,
+            src_ref=self.source(hop, slot),
             dst_ref=self.buf.at[slot],
             send_sem=self.ssem.at[way, hop],
             recv_sem=self.rsem.at[slot],
@@ -91,24 +90,30 @@
             def _(way=way):
                 self.copy(self.slot(hop, way), hop, way).start()
 
+    def take(self, hop, ways=(0, 1)):
+        for way in ways:
+
+            @pl.when(self.arrives(hop, way))
+            def _(way=way):
+                self.copy(self.slot(hop, way), hop, way).wait_recv()
+
     def relay(self, hop):
         for way in (0, 1):
-
-            @pl.when(self.arrives(hop, way))
-            def _(way=way):
-                slot = self.slot(hop, way)
-                self.copy(slot, hop, way).wait_recv()
-
+            self.take(hop, (way,))
             if hop < self.n - 1:
                 self.send(hop, (way,))
 
-    def finish(self):
-        for hop in range(self.n - 1):
+    def finish(self, first=0, last=None):
+        for hop in range(first, self.n - 1 if last is None else last):
             for way in (0, 1):
 
                 @pl.when(self.goes(hop, way))
                 def _(way=way, hop=hop):
                     self.copy(self.slot(hop, way), hop, way).wait_send()
+
+
+def own_then(own, buf):
+    return lambda hop, slot: own if hop == 0 else buf.at[slot]
 
 
 def line_sems(n):
@@ -127,26 +132,143 @@
     )
 
 
-def attend_kernel(
-    dims, x_ref, w_ref, gain_ref, c_ref, st_ref,
-    n1_ref, q_ref, k_ref, v_ref, lse_ref, oc_ref, of_ref,
-    xbuf, wpad, mask, opad, zs, zr, as_, ar,
+def plane(data_par):
+    half = data_par // 2
+    side = math.isqrt(half)
+    return (side, half // side) if side * side == half else (1, half)
+
+
+class PlaneGather:
+    def __init__(self, n_data, buf, sems):
+        self.ys, self.xs = plane(n_data)
+        self.buf = buf
+        self.s1a, self.s1b, self.r1a, self.r1b, self.s2a, self.s2b, self.r2a, self.r2b, self.cs, self.cr = sems
+        me = lax.axis_index("dp")
+        self.c = lax.rem(me, 2)
+        self.x = lax.rem(me // 2, self.xs)
+        self.y = me // (2 * self.xs)
+
+    def move(self, src, dst, ssem, rsem, y, x, c):
+        return pltpu.make_async_remote_copy(
+            src_ref=src, dst_ref=dst, send_sem=ssem, recv_sem=rsem,
+            device_id={"dp": (y * self.xs + x) * 2 + c}, device_id_type=MESH,
+        )
+
+    def east(self, o):
+        return lax.rem(self.x + o + self.xs, self.xs)
+
+    def north(self, o):
+        return lax.rem(self.y + o + self.ys, self.ys)
+
+    def first(self, k, back=False):
+        out = []
+        for o in range(1, self.xs):
+            ref = self.buf.at[k, 0:2, self.y, self.east(-o) if back else self.x, self.c]
+            out.append(self.move(ref, ref, self.s1a.at[k, o], self.r1a.at[k, o], self.y, self.east(o), self.c))
+        for o in range(1, self.ys):
+            ref = self.buf.at[k, 2:3, self.north(-o) if back else self.y, self.x, self.c]
+            out.append(self.move(ref, ref, self.s1b.at[k, o], self.r1b.at[k, o], self.north(o), self.x, self.c))
+        return out
+
+    def second(self, k, back=False):
+        out = []
+        for o in range(1, self.ys):
+            ref = self.buf.at[k, 0:2, self.north(-o) if back else self.y, :, self.c]
+            out.append(self.move(ref, ref, self.s2a.at[k, o], self.r2a.at[k, o], self.north(o), self.x, self.c))
+        for o in range(1, self.xs):
+            ref = self.buf.at[k, 2:3, :, self.east(-o) if back else self.x, self.c]
+            out.append(self.move(ref, ref, self.s2b.at[k, o], self.r2b.at[k, o], self.y, self.east(o), self.c))
+        return out
+
+    def third(self, k, back=False):
+        ref = self.buf.at[k, :, :, :, 1 - self.c if back else self.c]
+        return [self.move(ref, ref, self.cs.at[k], self.cr.at[k], self.y, self.x, 1 - self.c)]
+
+    def stage(self, number, k):
+        stages = (self.first, self.second, self.third)
+        if number > 0:
+            for copy in stages[number - 1](k, True):
+                copy.wait_recv()
+        if number < 3:
+            for copy in stages[number](k):
+                copy.start()
+
+    def finish(self, k):
+        for stage in (self.first, self.second, self.third):
+            for copy in stage(k):
+                copy.wait_send()
+
+    @staticmethod
+    def sems(n_data, count):
+        ys, xs = plane(n_data)
+        sem = pltpu.SemaphoreType.DMA
+        xy = [sem((count, xs)), sem((count, ys))]
+        return xy + xy + xy[::-1] + xy[::-1] + [sem((count,)), sem((count,))]
+
+
+def near_hops(n):
+    return min(2, n - 1)
+
+
+def data_peers(n_data):
+    mine = lax.axis_index("dp")
+    return [{"dp": lax.rem(mine + off, n_data)} for off in range(1, n_data)]
+
+
+def front_kernel(
+    dims, n_data, x_ref, g_ref, w_ref, gain_ref, c_ref, st_ref,
+    n1_ref, q_ref, k_ref, v_ref, lse_ref, oc_ref, wq_out, wt_out, g_near, n2_near, out_ref, dh_ref, n2_ref, dhb_ref, dgain_ref,
+    xbuf, wf, wpad, mask, opad, of_ref, h_ref, acc, dn2, zs, zr, ws, wr, gs, gr, ns, nr, as_, ar, os_, *plane_sems,
 ):
     n, rows, heads, span = dims
+    hops_g = near_hops(n)
     me = lax.axis_index("mp")
     cols = w_ref.shape[2]
-    greet(line_peers(n, me))
-    gather = LineGather(n, me, x_ref, xbuf, zs, zr)
+    width = x_ref.shape[1]
+    greet(line_peers(n, me) + data_peers(n_data))
+    gather = LineGather(n, me, own_then(x_ref, xbuf), xbuf, zs, zr)
+    whole = PlaneGather(n_data, wf, plane_sems)
+
+    def place(k):
+        return wf.at[k, :, whole.y, whole.x, whole.c]
+
+    class Weights(LineGather):
+        def copy(self, slot, hop, way):
+            return pltpu.make_async_remote_copy(
+                src_ref=place(slot), dst_ref=place(slot), send_sem=self.ssem.at[way, hop],
+                recv_sem=self.rsem.at[slot], device_id={"mp": self.me + 1 - 2 * way}, device_id_type=MESH,
+            )
+
+    lines = Weights(n, me, None, None, ws, wr)
+    gather_g = LineGather(n, me, own_then(g_ref, g_near), g_near, gs, gr)
+    gather_n = LineGather(n, me, own_then(n2_ref, n2_near), n2_near, ns, nr)
     gather.send(0)
+    place(n)[...] = w_ref[0:3]
+    place(me)[...] = w_ref[3:6]
+    whole.stage(0, n)
+    lines.send(0)
+    whole.stage(0, me)
     sel = spread(cols, heads)
+    xbuf[me] = x_ref[...]
+
+    def matrix(k, m):
+        value = wf[k, m]
+        if value.shape[-2] % 16:
+            return value.astype(F32).reshape(width, cols).astype(BF16)
+        return value.reshape(width, cols)
+
+    whole.stage(1, n)
+    whole.stage(1, me)
+    whole.stage(2, n)
+    whole.stage(2, me)
+    whole.stage(3, n)
     for m in range(3):
-        wpad[m] = nn(w_ref[m], sel).astype(BF16)
-    xbuf[me] = x_ref[...]
+        wpad[m] = nn(matrix(n, m), sel).astype(BF16)
 
     def project(slot):
         x = xbuf[slot].astype(F32)
         scale = lax.rsqrt(jnp.mean(x * x, axis=-1, keepdims=True) + EPSILON)
-        normed = (x * scale * gain_ref[...]).astype(BF16)
+        normed = (x * scale * gain_ref[0:1]).astype(BF16)
         n1_ref[slot] = normed
         at = block_rows(slot, rows)
         for m, ref in enumerate((q_ref, k_ref, v_ref)):
@@ -159,21 +281,31 @@
 
     project(me)
 
-    def arrivals(hop):
+    def arrivals(hop, do):
         def one(way, _):
             slot = me - hop + 2 * hop * way
 
             @pl.when((slot >= 0) & (slot < n))
             def _():
-                project(slot)
+                do(slot)
 
             return 0
 
         lax.fori_loop(0, 2, one, 0)
+
+    def forward(stage, hop):
+        if 1 <= hop < n:
+            arrivals(hop, lambda slot: whole.stage(stage, slot))
 
     for hop in range(1, n):
         gather.relay(hop)
-        arrivals(hop)
+        if hop < n - 1:
+            lines.relay(hop)
+            forward(0, hop)
+        forward(1, hop - 1)
+        arrivals(hop, project)
+        forward(2, hop - 1)
+    gather_g.send(0)
 
     def chunk(i, _):
         first = jnp.maximum(i - (span - 1), 0)
@@ -207,84 +339,60 @@
         def _():
             of_ref[me] = oc_ref[me]
 
+        @pl.when(i == 0)
+        def _():
+            lines.relay(n - 1)
+            forward(0, n - 1)
+
+        @pl.when(i == n // 2)
+        def _():
+            forward(1, n - 1)
+
         return 0
 
     lax.fori_loop(0, n, chunk, 0)
-    gather.finish()
-    for off in range(1, n):
+    forward(2, n - 1)
+
+    def both(slot, _):
+        whole.stage(3, slot)
+        return 0
+
+    lax.fori_loop(0, n, both, 0)
+    keep_q = pltpu.make_async_copy(wf.at[n], wq_out, os_.at[0])
+    keep_t = pltpu.make_async_copy(wf.at[me], wt_out, os_.at[1])
+    keep_q.start()
+    keep_t.start()
+    for hop in range(1, hops_g):
+        gather_g.relay(hop)
+    h_ref[...] = x_ref[...].astype(F32) + nt(of_ref[me], matrix(me, 0))
+
+    def outward(off, _):
         peer = lax.rem(me + off, n)
         copy = pltpu.make_async_remote_copy(
             src_ref=oc_ref.at[peer], dst_ref=of_ref.at[peer], send_sem=as_.at[peer],
             recv_sem=ar.at[peer], device_id={"mp": peer}, device_id_type=MESH,
         )
+        copy.wait_recv()
+        h_ref[...] += nt(of_ref[peer], matrix(peer, 0))
         copy.wait_send()
-        copy.wait_recv()
-
-
-def attend(dims, x, w, gain, c_row, starts):
-    n, rows, heads, span = dims
-    width, cols = x.shape[1], w.shape[2]
-    count = n * rows
-    head_out = jax.ShapeDtypeStruct((heads, count, LANE), BF16)
-    return pl.pallas_call(
-        functools.partial(attend_kernel, dims),
-        out_shape=(
-            jax.ShapeDtypeStruct((n, rows, width), BF16),
-            head_out, head_out, head_out,
-            jax.ShapeDtypeStruct((heads, count, 1), F32),
-            jax.ShapeDtypeStruct((n, rows, cols), BF16),
-            jax.ShapeDtypeStruct((n, rows, cols), BF16),
-        ),
-        in_specs=vmem(5),
-        out_specs=vmem(7),
-        scratch_shapes=[
-            pltpu.VMEM((n, rows, width), BF16),
-            pltpu.VMEM((3, width, heads * LANE), BF16),
-            pltpu.VMEM((rows, span * rows), F32),
-            pltpu.VMEM((heads, rows, LANE), BF16),
-            *line_sems(n),
-            pltpu.SemaphoreType.DMA((n,)),
-            pltpu.SemaphoreType.DMA((n,)),
-        ],
-        compiler_params=params(1),
-        name="attend",
-    )(x, w, gain, c_row, starts)
-
-
-def middle_kernel(
-    dims, x_ref, g_ref, of_ref, w_ref, gain_ref,
-    out_ref, dh_ref, n2_ref, g_all, dhb_ref, dgain_ref,
-    h_ref, acc, dn2, gs, gr, ns, nr, ds, dr,
-):
-    n = dims[0]
-    me = lax.axis_index("mp")
-    greet(line_peers(n, me))
-    gather_g = LineGather(n, me, g_ref, g_all, gs, gr)
-    gather_n = LineGather(n, me, n2_ref.at[me], n2_ref, ns, nr)
-    gather_d = LineGather(n, me, dhb_ref.at[me], dhb_ref, ds, dr)
-    gather_g.send(0)
-    g_all[me] = g_ref[...]
-    h_ref[...] = x_ref[...].astype(F32)
-
-    def project(j, _):
-        h_ref[...] += nt(of_ref[j], w_ref[j, 0])
         return 0
 
-    lax.fori_loop(0, n, project, 0)
+    lax.fori_loop(1, n, outward, 0)
     h = h_ref[...]
     scale = lax.rsqrt(jnp.mean(h * h, axis=-1, keepdims=True) + EPSILON)
-    n2_ref[me] = (h * scale * gain_ref[...]).astype(BF16)
+    n2_ref[...] = (h * scale * gain_ref[1:2]).astype(BF16)
     gather_n.send(0)
-    acc[...] = h_ref[...]
+    acc[...] = h
     dn2[...] = jnp.zeros_like(dn2)
 
     def hidden(j, _):
-        gate = nn(n2_ref[me], w_ref[j, 1])
+        up, down = matrix(j, 1), matrix(j, 2)
+        gate = nn(n2_ref[...], up)
         sig = 1.0 / (1.0 + jnp.exp(-gate))
-        acc[...] += nt((gate * sig).astype(BF16), w_ref[j, 2])
-        dz = nn(g_ref[...], w_ref[j, 2])
+        acc[...] += nt((gate * sig).astype(BF16), down)
+        dz = nn(g_ref[...], down)
         da = (dz * (sig * (1.0 + gate * (1.0 - sig)))).astype(BF16)
-        dn2[...] += nt(da, w_ref[j, 1])
+        dn2[...] += nt(da, up)
         return 0
 
     lax.fori_loop(0, n, hidden, 0)
@@ -294,46 +402,86 @@
     unit = h * scale
     grad = dn2[...]
     dgain_ref[...] = jnp.sum(grad * unit, axis=0, keepdims=True)
-    du = grad * gain_ref[...]
+    du = grad * gain_ref[1:2]
     dh = g_ref[...].astype(F32) + scale * (du - unit * jnp.mean(du * unit, axis=-1, keepdims=True))
     dh_ref[...] = dh
-    dhb_ref[me] = dh.astype(BF16)
-    gather_d.send(0)
-    for hop in range(1, n):
-        gather_g.relay(hop)
-        gather_n.relay(hop)
-        gather_d.relay(hop)
-    for gather in (gather_g, gather_n, gather_d):
-        gather.finish()
-
-
-def middle(dims, x, g, o_full, w_full, gain):
-    n, rows = dims[:2]
+    dhb_ref[...] = dh.astype(BF16)
+    gather_g.take(hops_g)
+    gather_n.take(1)
+    gather_g.finish(0, hops_g)
+    gather_n.finish(0, 1)
+    gather.finish()
+    lines.finish()
+
+    def sent(k, _):
+        whole.finish(k)
+        return 0
+
+    lax.fori_loop(0, n + 1, sent, 0)
+    keep_q.wait()
+    keep_t.wait()
+
+
+def front(dims, x, g, shards, gains, c_row, starts):
+    n, rows, heads, span = dims
+    n_data = lax.axis_size("dp")
+    own_rows, cols = shards.shape[1:]
     width = x.shape[1]
-    every = jax.ShapeDtypeStruct((n, rows, width), BF16)
+    count = n * rows
+    ys, xs = plane(n_data)
+    head_out = jax.ShapeDtypeStruct((heads, count, LANE), BF16)
+    kept = jax.ShapeDtypeStruct((3, ys, xs, 2, own_rows, cols), BF16)
+    own = jax.ShapeDtypeStruct((rows, width), BF16)
+    sem = pltpu.SemaphoreType.DMA
     return pl.pallas_call(
-        functools.partial(middle_kernel, dims),
+        functools.partial(front_kernel, dims, n_data),
         out_shape=(
-            jax.ShapeDtypeStruct((rows, width), BF16),
+            jax.ShapeDtypeStruct((n, rows, width), BF16),
+            head_out, head_out, head_out,
+            jax.ShapeDtypeStruct((heads, count, 1), F32),
+            jax.ShapeDtypeStruct((n, rows, cols), BF16),
+            kept, kept,
+            jax.ShapeDtypeStruct((n, rows, width), BF16),
+            jax.ShapeDtypeStruct((n, rows, width), BF16),
+            own,
             jax.ShapeDtypeStruct((rows, width), F32),
-            every, every, every,
+            own, own,
             jax.ShapeDtypeStruct((1, width), F32),
         ),
-        in_specs=vmem(5),
-        out_specs=vmem(6),
-        scratch_shapes=[pltpu.VMEM((rows, width), F32)] * 3 + line_sems(n) * 3,
-        compiler_params=params(2),
-        name="middle",
-    )(x, g, o_full, w_full, gain)
+        in_specs=vmem(6),
+        out_specs=vmem(6) + [pl.BlockSpec(memory_space=pl.ANY)] * 4 + vmem(5),
+        scratch_shapes=[
+            pltpu.VMEM((n, rows, width), BF16),
+            pltpu.VMEM((n + 1, *kept.shape), BF16),
+            pltpu.VMEM((3, width, heads * LANE), BF16),
+            pltpu.VMEM((rows, span * rows), F32),
+            pltpu.VMEM((heads, rows, LANE), BF16),
+            pltpu.VMEM((n, rows, cols), BF16),
+            pltpu.VMEM((rows, width), F32), pltpu.VMEM((rows, width), F32), pltpu.VMEM((rows, width), F32),
+            *line_sems(n), *line_sems(n), *line_sems(n), *line_sems(n),
+            sem((n,)), sem((n,)), sem((2,)),
+            *PlaneGather.sems(n_data, n + 1),
+        ],
+        compiler_params=params(1),
+        name="front",
+    )(x, g, shards, gains, c_row, starts)
 
 
 def back_kernel(
-    dims, q_ref, k_ref, v_ref, lse_ref, dhb_ref, w_ref, c_ref, st_ref,
-    dx_ref, dc_ref,
-    wpad, mask, do_ref, dq_ref, dk_ref, dv_ref,
+    dims, q_ref, k_ref, v_ref, lse_ref, own_ref, c_ref, st_ref, w_hbm,
+    dx_ref, dc_ref, dhb_ref,
+    w_ref, wpad, mask, do_ref, dq_ref, dk_ref, dv_ref, zs, zr, w_sem,
 ):
     n, rows, heads, span = dims
+    me = lax.axis_index("mp")
+    take_w = pltpu.make_async_copy(w_hbm.at[0], w_ref, w_sem)
+    take_w.start()
+    greet(line_peers(n, me))
+    gather = LineGather(n, me, own_then(own_ref, dhb_ref), dhb_ref, zs, zr)
+    gather.send(0)
+    dhb_ref[me] = own_ref[...]
     sel = spread(w_ref.shape[1], heads)
+    take_w.wait()
     wpad[...] = nn(w_ref[...], sel).astype(BF16)
     dk_ref[...] = jnp.zeros_like(dk_ref)
     dv_ref[...] = jnp.zeros_like(dv_ref)
@@ -343,7 +491,7 @@
         wide = jnp.concatenate([ref[h, at, :].astype(BF16) for h in range(heads)], axis=1)
         return nt(wide, sel).astype(BF16)
 
-    def chunk(i, _):
+    def chunk(i):
         first = jnp.maximum(i - (span - 1), 0)
         at, keys = block_rows(i, rows), pl.ds(pl.multiple_of(first * rows, rows), span * rows)
         q_pos = i * rows + lax.broadcasted_iota(jnp.int32, mask.shape, 0)
@@ -369,9 +517,26 @@
 
         lax.fori_loop(0, heads, head, 0)
         dx_ref[0, i] = squeeze(dq_ref, slice(None))
+
+    def event(e, _):
+        hop, way = (e + 1) // 2, lax.rem(e + 1, 2)
+        i = me - hop + 2 * hop * way
+
+        @pl.when((way == 0) & (hop > 0))
+        def _():
+            for fixed in range(1, n):
+
+                @pl.when(hop == fixed)
+                def _(fixed=fixed):
+                    gather.relay(fixed)
+
+        @pl.when((i >= 0) & (i < n))
+        def _():
+            chunk(i)
+
         return 0
 
-    lax.fori_loop(0, n, chunk, 0)
+    lax.fori_loop(0, 2 * n - 1, event, 0)
 
     def close(i, _):
         at = block_rows(i, rows)
@@ -380,30 +545,35 @@
         return 0
 
     lax.fori_loop(0, n, close, 0)
-
-
-def back(dims, q, k, v, lse, dhb, w_out, c_row, starts):
+    gather.finish()
+
+
+def back(dims, q, k, v, lse, dhb, c_row, starts, w_tail):
     n, rows, heads, span = dims
-    cols, width = w_out.shape[1], w_out.shape[0]
+    width, cols = w_tail.shape[1:]
     return pl.pallas_call(
         functools.partial(back_kernel, dims),
         out_shape=(
             jax.ShapeDtypeStruct((3, n, rows, cols), BF16),
             jax.ShapeDtypeStruct((1, LANE), F32),
+            jax.ShapeDtypeStruct((n, rows, width), BF16),
         ),
-        in_specs=vmem(8),
-        out_specs=vmem(2),
+        in_specs=vmem(7) + [pl.BlockSpec(memory_space=pl.ANY)],
+        out_specs=vmem(3),
         scratch_shapes=[
+            pltpu.VMEM((width, cols), BF16),
             pltpu.VMEM((width, heads * LANE), BF16),
             pltpu.VMEM((rows, span * rows), F32),
             pltpu.VMEM((heads, rows, LANE), BF16),
             pltpu.VMEM((heads, rows, LANE), BF16),
             pltpu.VMEM((heads, n * rows, LANE), F32),
             pltpu.VMEM((heads, n * rows, LANE), F32),
+            *line_sems(n),
+            pltpu.SemaphoreType.DMA,
         ],
-        compiler_params=params(),
+        compiler_params=params(2),
         name="back",
-    )(q, k, v, lse, dhb, w_out, c_row, starts)
+    )(q, k, v, lse, dhb, c_row, starts, w_tail)
 
 
 def halves(value):
@@ -417,12 +587,6 @@
     big_high, big_low = halves(big)
     both = contract(jnp.concatenate([high.astype(F32), low.astype(F32)], axis=0).astype(BF16), big_high)
     return both[:count] + both[count:] + contract(high, big_low)
-
-
-def plane(data_par):
-    half = data_par // 2
-    side = math.isqrt(half)
-    return (side, half // side) if side * side == half else (1, half)
 
 
 class PlaneScatter:
@@ -514,22 +678,17 @@
         lax.fori_loop(0, h * self.ys, along_y, 0)
         lax.fori_loop(0, h * self.xs, along_x, 0)
 
-    def sum_two(self, out, factor):
+    def sum_two(self, put):
         self.arrive(self.copies_two())
-        h = self.half
-
-        def one(m, _):
+        for m in range(self.half):
             total = self.core[m, self.y, self.x].astype(F32)
             for o in range(1, self.ys):
                 total += self.a2[o - 1, m].astype(F32)
-            out[m] = factor * total
-            total = self.core[h + m, self.y, self.x].astype(F32)
+            put(m, total)
+            total = self.core[self.half + m, self.y, self.x].astype(F32)
             for o in range(1, self.xs):
                 total += self.b2[o - 1, m].astype(F32)
-            out[h + m] = factor * total
-            return 0
-
-        lax.fori_loop(0, h, one, 0)
+            put(self.half + m, total)
 
     def finish(self):
         for copy in self.copies_core() + self.copies_one() + self.copies_two():
@@ -587,17 +746,116 @@
     return lax.fori_loop(1, size, one, ref[0])
 
 
+FIRST, SECOND = (0, 1, 2, 4), (3, 5)
+
+
+class Factors:
+    def __init__(self, n, n_data, group, index, ft, m_ref, basis, right, refs):
+        self.group, self.index, self.ft, self.m, self.basis, self.right = group, index, ft, m_ref, basis, right
+        self.send, self.got, self.line, self.full, self.rgot = refs[:5]
+        l_s, l_r, z_s, z_r, a_s, a_r, r_s, r_r = refs[5:]
+        self.n, self.n_data = n, n_data
+        self.tiles = basis.shape[2] // LANE
+        self.per = self.send.shape[1]
+        self.mine, self.me = lax.axis_index("dp"), lax.axis_index("mp")
+        mine, me = self.mine, self.me
+        self.ex_left = Exchange("dp", n_data, lambda peer: self.send.at[peer], self.got, l_s, l_r)
+        self.ex_line = Exchange("mp", n, lambda peer: self.line.at[me], self.line, z_s, z_r)
+        self.ex_all = Exchange("dp", n_data, lambda peer: self.full.at[mine], self.full, a_s, a_r)
+        self.ex_right = Exchange("dp", n_data, lambda peer: self.rgot.at[mine], self.rgot, r_s, r_r)
+
+    def start(self):
+        size = len(self.group) * self.tiles
+        for tile in range(size, self.n_data * self.per):
+            self.send[tile // self.per, tile % self.per] = jnp.zeros((8, LANE), F32)
+
+        def rows_of(k, _):
+            m = self.index(k)
+            rows_left = dot_split(self.ft[m], self.m[m], nn)
+            for t in range(self.tiles):
+                tile = k * self.tiles + t
+                self.send[tile // self.per, lax.rem(tile, self.per)] = rows_left[:, t * LANE : (t + 1) * LANE]
+            return 0
+
+        lax.fori_loop(0, len(self.group), rows_of, 0)
+        self.got[self.mine] = self.send[self.mine]
+        self.ex_left.start()
+
+    def along_line(self):
+        self.ex_left.arrive()
+        self.line[self.me] = total_of(self.got, self.n_data)
+        self.ex_line.start()
+
+    def spread_out(self):
+        self.ex_line.arrive()
+        self.full[self.mine] = total_of(self.line, self.n)
+        self.ex_all.start()
+
+    def orthonormal(self):
+        self.ex_all.arrive()
+        tiles, per = self.tiles, self.per
+        basis = jnp.stack(
+            [
+                jnp.concatenate([self.full[t // per, t % per] for t in range(k * tiles, (k + 1) * tiles)], axis=1)
+                for k in range(len(self.group))
+            ]
+        )
+        row = lax.broadcasted_iota(jnp.int32, (1, 8, 1), 1)
+        for index in range(8):
+            vector = basis[:, index : index + 1, :]
+            vector = vector * lax.rsqrt(jnp.sum(vector * vector, axis=-1, keepdims=True) + 1e-12)
+            onto = jnp.where(row > index, jnp.sum(basis * vector, axis=-1, keepdims=True), 0.0)
+            basis = jnp.where(row == index, vector, basis - onto * vector)
+        for k, m in enumerate(self.group):
+            self.basis[m] = basis[k]
+
+        def rows_of(k, _):
+            m = self.index(k)
+            self.rgot[self.mine, k] = dot_split(self.basis[m], self.m[m], nt)
+            return 0
+
+        lax.fori_loop(0, len(self.group), rows_of, 0)
+        self.ex_right.start()
+
+    def close(self):
+        self.ex_right.arrive()
+        total = total_of(self.rgot, self.n_data)
+        for k, m in enumerate(self.group):
+            self.right[m] = total[k]
+
+    def finish(self):
+        for exchange in (self.ex_left, self.ex_line, self.ex_all, self.ex_right):
+            exchange.finish()
+
+    @staticmethod
+    def scratch(n, n_data, count, width, cols):
+        sem = pltpu.SemaphoreType.DMA
+        per = -(-(count * width // LANE) // n_data)
+        tiles = (per, 8, LANE)
+        return [
+            pltpu.VMEM((n_data, *tiles), F32), pltpu.VMEM((n_data, *tiles), F32),
+            pltpu.VMEM((n, *tiles), F32), pltpu.VMEM((n_data, *tiles), F32),
+            pltpu.VMEM((n_data, count, 8, cols), F32),
+            sem((n_data,)), sem((n_data,)), sem((n,)), sem((n,)),
+            sem((n_data,)), sem((n_data,)), sem((n_data,)), sem((n_data,)),
+        ]
+
+
 def grads_kernel(
-    dims, n_data, scaling, n1_ref, n2_ref, dhb_ref, g_ref, dx_ref, oc_ref, wqkv_ref, wup_ref, wdn_ref,
-    x_ref, dh_ref, gain_ref, dgain2_ref, dscale_ref, ft_ref, err_ref,
-    gsum_ref, gin_ref, m_out, basis_ref, right_ref, small_ref,
-    abuf, z_ref, da_ref, sbuf, lbuf, m_ref, lsend, lrecv, zrecv, lfull, rrecv, srecv, szrecv,
-    fs, ss, ls, es, ms, l_s, l_r, z_s, z_r, a_s, a_r, r_s, r_r, g_s, g_r, gz_s, gz_r, *plane_refs,
+    dims, n_data, scaling, n1_ref, n2_ref, n2_near, dhb_ref, g_ref, g_near, dx_hbm, oc_hbm, wqkv_hbm, wtail_hbm,
+    err_ref, x_ref, dh_ref, gain_ref, dgain2_ref, dscale_ref, ft_ref,
+    gin_sum, gout_sum, gin_ref, basis_ref, right_ref, small_ref, m_out, n2_far, g_far,
+    abuf, dx_ref, wbuf, sbuf, lbuf, m_ref, srecv, szrecv,
+    fs, ns_, nr_, gs_, gr_, gts, gtr, nts, ntr, ss, ls, es, ms, g_s, g_r, gz_s, gz_r, *refs,
 ):
     n, rows, heads, span = dims
+    hops_g = near_hops(n)
     me, mine = lax.axis_index("mp"), lax.axis_index("dp")
-    width, cols = wup_ref.shape
+    width, cols = wbuf.shape[1:]
     tiles = width // LANE
+    sizes = (14, 14, 13, 13)
+    cuts = [sum(sizes[:k]) for k in range(5)]
+    parts = [refs[cuts[k] : cuts[k + 1]] for k in range(4)]
 
     def load(m):
         return pltpu.make_async_copy(err_ref.at[m], m_ref.at[m], es.at[m])
@@ -605,30 +863,65 @@
     def save(m):
         return pltpu.make_async_copy(m_ref.at[m], m_out.at[m], ms.at[m])
 
-    def fetch(k):
-        src = (n2_ref, g_ref, dhb_ref, n1_ref)[k]
-        return pltpu.make_async_copy(src, abuf.at[k % 2], fs.at[k])
-
-    fetch(0).start()
-    fetch(1).start()
+    take_dx = pltpu.make_async_copy(dx_hbm, dx_ref, fs.at[0])
+    take_oc = pltpu.make_async_copy(oc_hbm, dx_ref.at[2], fs.at[1])
+    take_qkv = pltpu.make_async_copy(wqkv_hbm, wbuf, fs.at[2])
+    take_tail = pltpu.make_async_copy(wtail_hbm, wbuf, fs.at[3])
+    take_dhb = pltpu.make_async_copy(dhb_ref, abuf.at[0], fs.at[4])
+    take_n1 = pltpu.make_async_copy(n1_ref, abuf.at[1], fs.at[5])
+    take_dx.start()
+    take_qkv.start()
+    take_n1.start()
     for m in range(6):
         load(m).start()
-    greet(line_peers(n, me) + [{"dp": lax.rem(mine + off, n_data)} for off in range(1, n_data)])
-    scatter = PlaneScatter(n_data, *plane_refs[:6], plane_refs[6:])
-    gb = plane_refs[0]
-    ex_left = Exchange("dp", n_data, lambda peer: lsend.at[peer], lrecv, l_s, l_r)
-    ex_line = Exchange("mp", n, lambda peer: zrecv.at[me], zrecv, z_s, z_r)
-    ex_all = Exchange("dp", n_data, lambda peer: lfull.at[mine], lfull, a_s, a_r)
-    ex_right = Exchange("dp", n_data, lambda peer: rrecv.at[mine], rrecv, r_s, r_r)
+    take_dhb.start()
+    greet(line_peers(n, me) + data_peers(n_data))
+    scatter_1 = PlaneScatter(n_data, *parts[0][:6], parts[0][6:])
+    scatter_2 = PlaneScatter(n_data, *parts[1][:6], parts[1][6:])
+    chain_1 = Factors(n, n_data, FIRST, lambda k: k + k // 3, ft_ref, m_ref, basis_ref, right_ref, parts[2])
+    chain_2 = Factors(n, n_data, SECOND, lambda k: 3 + 2 * k, ft_ref, m_ref, basis_ref, right_ref, parts[3])
+    gb_1, gb_2 = parts[0][0], parts[1][0]
     ex_small = Exchange("dp", n_data, lambda peer: srecv.at[mine], srecv, g_s, g_r)
     ex_small_line = Exchange("mp", n, lambda peer: szrecv.at[me], szrecv, gz_s, gz_r)
 
+    def follow(own, near, far, hops):
+        def source(hop, slot):
+            return own if hop == 0 else near.at[slot] if hop <= hops else far.at[slot]
+
+        return source
+
+    gather_n = LineGather(n, me, follow(n2_ref, n2_near, n2_far, 1), n2_far, nts, ntr)
+    gather_g = LineGather(n, me, follow(g_ref, g_near, g_far, hops_g), g_far, gts, gtr)
+
+    def bring(step):
+        for gather, hops in ((gather_g, hops_g), (gather_n, 1)):
+            hop = hops + step
+            if step == 0 and hop < n - 1:
+                gather.send(hop)
+            elif step > 0 and hop <= n - 1:
+                gather.relay(hop)
+
+    bring(0)
+
+    def pieces(own, near, far, hops, slot_of, sems, do):
+        for i in range(n):
+            away = jnp.maximum(i - me, me - i)
+            for src, hit in ((own, away == 0), (near.at[i], (away >= 1) & (away <= hops)), (far.at[i], away > hops)):
+
+                @pl.when(hit)
+                def _(src=src, i=i):
+                    do(pltpu.make_async_copy(src, abuf.at[slot_of, i], sems.at[i]))
+
+    def take_inputs(do):
+        pieces(n2_ref, n2_near, n2_far, 1, 0, ns_, do)
+        pieces(g_ref, g_near, g_far, hops_g, 1, gs_, do)
+
 
     def own(e, _):
         i = jnp.where(lax.rem(e, 2) == 0, n - 1 - e // 2, e // 2)
-        total = nt(dx_ref[0, i], wqkv_ref[0])
-        total += nt(dx_ref[1, i], wqkv_ref[1])
-        total += nt(dx_ref[2, i], wqkv_ref[2])
+        total = nt(dx_ref[0, i], wbuf[0])
+        total += nt(dx_ref[1, i], wbuf[1])
+        total += nt(dx_ref[2, i], wbuf[2])
 
         @pl.when(i == me)
         def _():
@@ -640,7 +933,10 @@
 
         return 0
 
+    take_dx.wait()
+    take_qkv.wait()
     lax.fori_loop(0, n, own, 0)
+    take_tail.start()
 
     def copy(i, way, here=False):
         slot = i if way == 0 else jnp.where(i == (me if here else me - 1), n, i)
@@ -674,94 +970,61 @@
     launch()
 
     def hidden(i, _):
-        gate = nn(abuf[0, i], wup_ref[...])
+        gate = nn(abuf[0, i], wbuf[1])
         sig = 1.0 / (1.0 + jnp.exp(-gate))
-        z_ref[i] = (gate * sig).astype(BF16)
-        dz = nn(abuf[1, i], wdn_ref[...])
-        da_ref[i] = (dz * (sig * (1.0 + gate * (1.0 - sig)))).astype(BF16)
+        dx_ref[0, i] = (gate * sig).astype(BF16)
+        dz = nn(abuf[1, i], wbuf[2])
+        dx_ref[1, i] = (dz * (sig * (1.0 + gate * (1.0 - sig)))).astype(BF16)
         return 0
 
     def flat(value):
         return value.reshape(n * rows, value.shape[-1])
 
-    def weight(m, a, b):
+    def weight(m, gb, k, a, b):
         left, right = flat(a), flat(b)
         load(m).wait()
         m_ref[m] = scaling * tn(right, left) + m_ref[m]
-        gb[m] = tn(left, right).reshape(gb.shape[1:]).astype(BF16)
-
-    def factor_rows(m):
-        rows_left = dot_split(ft_ref[m], m_ref[m], nn)
-        per = lsend.shape[1]
-        for t in range(tiles):
-            tile = m * tiles + t
-            lsend[tile // per, lax.rem(tile, per)] = rows_left[:, t * LANE : (t + 1) * LANE]
-
-    fetch(0).wait()
-    fetch(1).wait()
+        gb[k] = tn(left, right).reshape(gb.shape[1:]).astype(BF16)
+
+    def inputs(m, _):
+        weight(m, gb_1, m, abuf[1], dx_ref[m])
+        return 0
+
+    take_n1.wait()
+    lax.fori_loop(0, 3, inputs, 0)
+    take_oc.start()
+    bring(1)
+    take_dhb.wait()
+    take_oc.wait()
+    weight(4, gb_1, 3, abuf[0], dx_ref[2])
+    chain_1.start()
+    scatter_1.start(scatter_1.copies_core())
+    relay(1)
+    chain_1.along_line()
+    scatter_1.sum_core()
+    scatter_1.start(scatter_1.copies_one())
+    chain_1.spread_out()
+    chain_1.orthonormal()
+    for r in range(2, n - 1):
+        relay(r)
+        bring(r)
+    bring(n - 1)
+    take_inputs(lambda c: c.start())
+    scatter_1.sum_one()
+    scatter_1.start(scatter_1.copies_two())
+    take_tail.wait()
+    take_inputs(lambda c: c.wait())
     lax.fori_loop(0, n, hidden, 0)
-    weight(3, abuf[0], da_ref[...])
-    fetch(2).start()
-    weight(5, abuf[1], z_ref[...])
-    fetch(3).start()
-    fetch(2).wait()
-    weight(4, abuf[0], oc_ref[...])
-    relay(1)
-    fetch(3).wait()
-
-    def inputs(m, _):
-        weight(m, abuf[1], dx_ref[m])
+
+    def late(k, _):
+        weight(3 + 2 * k, gb_2, k, abuf[k], dx_ref[1 - k])
         return 0
 
-    lax.fori_loop(0, 3, inputs, 0)
-    for tile in range(6 * tiles, lsend.shape[0] * lsend.shape[1]):
-        lsend[tile // lsend.shape[1], tile % lsend.shape[1]] = jnp.zeros((8, LANE), F32)
-
-    def left_rows(m, _):
-        factor_rows(m)
-        return 0
-
-    lax.fori_loop(0, 6, left_rows, 0)
-    lrecv[mine] = lsend[mine]
-    ex_left.start()
-    scatter.start(scatter.copies_core())
+    lax.fori_loop(0, 2, late, 0)
+    chain_2.start()
+    scatter_2.start(scatter_2.copies_core())
     for m in range(6):
         save(m).start()
-    ex_left.arrive()
-    zrecv[me] = total_of(lrecv, n_data)
-    ex_line.start()
-    for r in range(2, n - 1):
-        relay(r)
-    scatter.sum_core()
-    scatter.start(scatter.copies_one())
-    ex_line.arrive()
-    lfull[mine] = total_of(zrecv, n)
-    ex_all.start()
-    ex_all.arrive()
-
-    per = lfull.shape[1]
-    basis = jnp.stack(
-        [
-            jnp.concatenate([lfull[t // per, t % per] for t in range(m * tiles, (m + 1) * tiles)], axis=1)
-            for m in range(6)
-        ]
-    )
-    row = lax.broadcasted_iota(jnp.int32, (1, 8, 1), 1)
-    for index in range(8):
-        vector = basis[:, index : index + 1, :]
-        vector = vector * lax.rsqrt(jnp.sum(vector * vector, axis=-1, keepdims=True) + 1e-12)
-        onto = jnp.where(row > index, jnp.sum(basis * vector, axis=-1, keepdims=True), 0.0)
-        basis = jnp.where(row == index, vector, basis - onto * vector)
-    basis_ref[...] = basis
-
-    def right_rows(m, _):
-        rrecv[mine, m] = dot_split(basis_ref[m], m_ref[m], nt)
-        return 0
-
-    lax.fori_loop(0, 6, right_rows, 0)
-    ex_right.start()
-    scatter.sum_one()
-    scatter.start(scatter.copies_two())
 
 
     @pl.when(me > 0)
@@ -774,6 +1037,7 @@
         copy(me, 1, True).wait_recv()
         gin_ref[...] += lbuf[n].astype(F32)
 
+    chain_2.along_line()
     x = x_ref[...].astype(F32)
     scale = lax.rsqrt(jnp.mean(x * x, axis=-1, keepdims=True) + EPSILON)
     unit = x * scale
@@ -788,16 +1052,33 @@
     t3 = 2 * tiles
     srecv[mine, t3 // 8, t3 % 8 : t3 % 8 + 1, :] = scaling * dscale_ref[...]
     ex_small.start()
+    scatter_2.sum_core()
+    scatter_2.start(scatter_2.copies_one())
+    chain_2.spread_out()
     du = grad * gain_ref[...]
     gin_ref[...] = dh_ref[...] + scale * (du - unit * jnp.mean(du * unit, axis=-1, keepdims=True))
     ex_small.arrive()
     szrecv[me] = total_of(srecv, n_data)
     ex_small_line.start()
-    ex_right.arrive()
-    right_ref[...] = total_of(rrecv, n_data)
-    scatter.sum_two(gsum_ref, scaling)
+    chain_2.orthonormal()
+
+    def put_1(k, value):
+        if k < 3:
+            gin_sum[k] = scaling * value
+        else:
+            gout_sum[0] = scaling * value
+
+    def put_2(k, value):
+        (gout_sum if k else gin_sum)[1 if k else 3] = scaling * value
+
+    scatter_1.sum_two(put_1)
+    chain_1.close()
+    scatter_2.sum_one()
+    scatter_2.start(scatter_2.copies_two())
     ex_small_line.arrive()
     small_ref[...] = total_of(szrecv, n)
+    chain_2.close()
+    scatter_2.sum_two(put_2)
 
     for i in range(n):
 
@@ -809,56 +1090,61 @@
         def _(i=i):
             copy(i, 1).wait_send()
 
-    for exchange in (ex_left, ex_line, ex_all, ex_right, ex_small, ex_small_line):
-        exchange.finish()
-    scatter.finish()
+    chain_1.finish()
+    chain_2.finish()
+    ex_small.finish()
+    ex_small_line.finish()
+    scatter_1.finish()
+    scatter_2.finish()
+    gather_g.finish(hops_g)
+    gather_n.finish(1)
     for m in range(6):
         save(m).wait()
 
 
-def grads(dims, scaling, n1, n2, dhb, g_all, dx, oc, wqkv, w_up, w_down, x, dh, gain, dgain2, dscale, ft, err):
+def grads(dims, scaling, hbm, x, dh, gain, dgain2, dscale, ft):
     n, rows = dims[:2]
     n_data = lax.axis_size("dp")
-    width, cols = w_up.shape
+    width, cols = hbm[-2].shape[1:]
     own_rows = width // n_data
-    every = pltpu.VMEM((n, rows, width), BF16)
     sem = pltpu.SemaphoreType.DMA
-    per = -(-(6 * width // LANE) // n_data)
     small = -(-(2 * width // LANE + 1) // 8)
+    far = jax.ShapeDtypeStruct((n, rows, width), BF16)
 
     def f32(*shape):
         return pltpu.VMEM(shape, F32)
+
+    def out(*shape):
+        return jax.ShapeDtypeStruct(shape, F32)
 
     return pl.pallas_call(
         functools.partial(grads_kernel, dims, n_data, scaling),
         out_shape=(
-            jax.ShapeDtypeStruct((6, own_rows, cols), F32),
-            jax.ShapeDtypeStruct((rows, width), F32),
-            jax.ShapeDtypeStruct((6, cols, width), F32),
-            jax.ShapeDtypeStruct((6, 8, width), F32),
-            jax.ShapeDtypeStruct((6, 8, cols), F32),
-            jax.ShapeDtypeStruct((small, 8, LANE), F32),
+            out(4, own_rows, cols), out(2, own_rows, cols), out(rows, width),
+            out(6, 8, width), out(6, 8, cols), out(small, 8, LANE),
+            out(6, cols, width), far, far,
         ),
-        in_specs=[pl.BlockSpec(memory_space=pl.ANY)] * 4 + vmem(11) + [pl.BlockSpec(memory_space=pl.ANY)],
-        out_specs=vmem(2) + [pl.BlockSpec(memory_space=pl.ANY)] + vmem(3),
+        in_specs=[pl.BlockSpec(memory_space=pl.ANY)] * len(hbm) + vmem(6),
+        out_specs=vmem(6) + [pl.BlockSpec(memory_space=pl.ANY)] * 3,
         scratch_shapes=[
             pltpu.VMEM((2, n, rows, width), BF16),
-            pltpu.VMEM((n, rows, cols), BF16),
-            pltpu.VMEM((n, rows, cols), BF16),
-            every,
+            pltpu.VMEM((3, n, rows, cols), BF16),
+            pltpu.VMEM((3, width, cols), BF16),
+            pltpu.VMEM((n, rows, width), BF16),
             pltpu.VMEM((n + 1, rows, width), BF16),
             f32(6, cols, width),
-            f32(n_data, per, 8, LANE), f32(n_data, per, 8, LANE), f32(n, per, 8, LANE),
-            f32(n_data, per, 8, LANE), f32(n_data, 6, 8, cols),
             f32(n_data, small, 8, LANE), f32(n, small, 8, LANE),
-            sem((4,)), sem((n,)), sem((n + 1,)), sem((6,)), sem((6,)),
-            sem((n_data,)), sem((n_data,)), sem((n,)), sem((n,)), sem((n_data,)), sem((n_data,)),
-            sem((n_data,)), sem((n_data,)), sem((n_data,)), sem((n_data,)), sem((n,)), sem((n,)),
-            *PlaneScatter.scratch(n_data, 6, own_rows, cols),
+            sem((6,)), sem((n,)), sem((n,)), sem((n,)), sem((n,)),
+            *line_sems(n), *line_sems(n), sem((n,)), sem((n + 1,)), sem((6,)), sem((6,)),
+            sem((n_data,)), sem((n_data,)), sem((n,)), sem((n,)),
+            *PlaneScatter.scratch(n_data, 4, own_rows, cols),
+            *PlaneScatter.scratch(n_data, 2, own_rows, cols),
+            *Factors.scratch(n, n_data, 4, width, cols),
+            *Factors.scratch(n, n_data, 2, width, cols),
         ],
         compiler_params=params(3),
         name="grads",
-    )(n1, n2, dhb, g_all, dx, oc, wqkv, w_up, w_down, x, dh, gain, dgain2, dscale, ft, err)
+    )(*hbm, x, dh, gain, dgain2, dscale, ft)[:7]
 
 
 def close_kernel(m_ref, right_ref, basis_ref, out_ref):
@@ -892,7 +1178,7 @@
     rows, width = activations.shape
     n = lax.axis_size("mp")
     data_par = lax.axis_size("dp")
-    my_data, me = lax.axis_index("dp"), lax.axis_index("mp")
+    my_data = lax.axis_index("dp")
     count = rows * n
     scaling = (count * data_par) ** (-0.5)
     cols = w_in.shape[2]
@@ -902,29 +1188,25 @@
     span = min(n, -(-(longest - 1) // rows) + 1)
     dims = (n, rows, heads, span)
 
-    shards = jnp.concatenate([w_in, w_attn_out.T[None], w_down.T[None]], axis=0).astype(BF16)
-    wqkv = lax.all_gather(shards[:3], "dp", axis=1, tiled=True)
-    tail = jnp.stack([shards[4], shards[3], shards[5]])
-    w_full = lax.all_gather(lax.all_gather(tail, "mp", axis=0), "dp", axis=2, tiled=True)
-    w_mine = lax.dynamic_index_in_dim(w_full, me, 0, keepdims=False)
-
+    shards = jnp.concatenate([w_in[:3], w_attn_out.T[None], w_in[3:], w_down.T[None]], axis=0).astype(BF16)
     ends = jnp.cumsum(doc_lengths[0])
     position = jnp.arange(count, dtype=jnp.int32)[:, None]
     starts = jnp.max(jnp.where(ends[None, :] <= position, ends[None, :], 0), axis=1, keepdims=True)
     factor = SCALE_BASE / math.sqrt(HD) * jax.nn.softplus(scale_param)
     c_row = jnp.tile(jnp.pad(factor, (0, LANE - HD)), heads)[None]
 
-    n1, q, k, v, lse, oc, o_full = attend(dims, activations, wqkv, gains[:1], c_row, starts)
-    output, dh, n2, g_all, dhb, dgain2 = middle(dims, activations, cotangent, o_full, w_full, gains[1:])
-    dx, dc = back(dims, q, k, v, lse, dhb, w_mine[0], c_row, starts)
+    n1, q, k, v, lse, oc, wqkv, w_tail, g_near, n2_near, output, dh, n2, dhb, dgain2 = front(
+        dims, activations, cotangent, shards, gains, c_row, starts
+    )
+    wqkv, w_tail = wqkv.reshape(3, width, cols), w_tail.reshape(3, width, cols)
+    dx, dc, dhb = back(dims, q, k, v, lse, dhb, c_row, starts, w_tail)
     grad_scale_local = dc[0, :HD] / factor * (SCALE_BASE / math.sqrt(HD)) * jax.nn.sigmoid(scale_param)
     dscale = jnp.pad(grad_scale_local, (0, LANE - HD))[None]
-    summed, grad_input, stored, basis, right, small = grads(
-        dims, scaling, n1, n2, dhb, g_all, dx, oc, wqkv, w_mine[1], w_mine[2], activations, dh, gains[:1],
-        dgain2, dscale, jnp.swapaxes(factors, 1, 2), error_buffer[0],
+    hbm = (n1, n2, n2_near, dhb, cotangent, g_near, dx, oc, wqkv, w_tail, error_buffer[0])
+    grad_in, out_sum, grad_input, basis, right, small, stored = grads(
+        dims, scaling, hbm, activations, dh, gains[:1], dgain2, dscale, jnp.swapaxes(factors, 1, 2)
     )
-    grad_in = summed[:4]
-    grad_out = jnp.swapaxes(summed[4:], 1, 2)
+    grad_out = jnp.swapaxes(out_sum, 1, 2)
     error_new = close(stored, right, basis)[None]
     tiles = width // LANE
     small = small.reshape(-1, LANE)

time: 456 us -> 350 us (0.77)
  waiting for transfers between devices: 68.2 us -> 0 us
  Pallas kernels: 348 us -> 326 us
  between operations: 13.9 us -> 0.8 us
    all_gather x3 -> x0, waiting for transfers between devices: 68.2 us -> none  [the longest x1 37.3 us: on_device(): lax.all_gather(tail, 'mp', axis=0)]
    pallas_call x2 -> x1, Pallas kernels: 218 us -> 153 us  [front(): pl.pallas_call(functools.partial(front_kernel, dims, n_data), out_shape=(...]
    pallas_call x1, Pallas kernels: 26.4 us -> 59.2 us  [back(): pl.pallas_call(functools.partial(back_kernel, dims), out_shape=(jax.Shape...]
    pallas_call x1, Pallas kernels: 93.5 us -> 104 us  [grads(): pl.pallas_call(functools.partial(grads_kernel, dims, n_data, scaling), ou...]
  transfers between devices with their start and end apart: 3 -> 0, of which waited for: 2 -> 0; matrix products, arithmetic and copies ran while one was open for 1% -> 0% of each run, Pallas kernels for 18% -> 0%
where the time goes in v3:
time: 350 us
  Pallas kernels  326 us (93%)
  local copies, waits for them, and re-layouts  10.5 us (3%)
  other arithmetic  10.2 us (3%)
    pallas_call x1, Pallas kernels, front(): pl.pallas_call(functools.partial(front_kernel, dims, n_data), out_shape=(...  153 us
    pallas_call x1, Pallas kernels, grads(): pl.pallas_call(functools.partial(grads_kernel, dims, n_data, scaling), ou...  104 us
    pallas_call x1, Pallas kernels, back(): pl.pallas_call(functools.partial(back_kernel, dims), out_shape=(jax.Shape...  59.2 us
    pallas_call x1, Pallas kernels, close(): pl.pallas_call(close_kernel, grid=(6,), out_shape=jax.ShapeDtypeStruct(m....  9.7 us

profile of v3, /device:TPU:0, one launch (start us, length us, event | category | flops | bytes accessed | tf_op | source)
XLA Modules:
  0.0 349.7 jit_solution(13269596466305706773)
XLA Ops:
  0.6 0.0 copy-start.9
  0.7 0.0 copy-start.11
  0.7 1.1 convert_bitcast_fusion
  1.8 1.3 convert.16
  3.1 1.0 pad_maximum_fusion.w_ref
  4.1 0.0 copy-done.9
  4.2 0.6 tile.2
  4.8 0.0 copy-done.11
  4.8 0.2 reduce-window.8
  4.9 0.1 select_reduce_fusion
  5.0 1.0 copy.32.st_ref
  6.1 152.8 %front.1 = (bf16[4,256,1280]{2,1,0:T(8,128)(2,1)}, bf16[4,1024,128]{2,1,0:T(8,128)(2,1)}, bf16[4,1024,128]{2,1,0:T(8,128)(2,1)}, bf16[4,1024,128]{2,1,0:T(8,128)...) custom-call(bf16[256,1280]{1,0:T(8,128)(2,1)} %x_ref.3, ...), custom_call_target="tpu_custom_call" | custom-call | tf_op jit(solution)/shard_map/front/pallas_call | solution.py:436
  158.9 0.0 copy-start.6
  158.9 59.2 %back.1 = (bf16[3,4,256,320]{3,2,1,0:T(8,128)(2,1)}, f32[1,128]{1,0:T(1,128)}, bf16[4,256,1280]{2,1,0:T(8,128)(2,1)}) custom-call(bf16[4,1024,128]{2,1,0:T(8,128)(2,1)} %get-tuple-element.45.q_ref, bf16[4,1024,128]{2,1,0:T(8,128)(2,1)} %get-tuple-element.46.k_ref, bf16[4,1024,128]{2,1,0:T(8,128)(2,1)} %get-tuple-element.47.v_ref, ...), custom_call_target="tpu_custom_call" | custom-call | tf_op jit(solution)/shard_map/back/pallas_call | solution.py:554
  218.2 0.0 copy-done.6
  218.2 0.6 slice.28.gain_ref
  218.8 0.6 divide_multiply_fusion
  219.4 0.5 pad_bitcast_fusion.dscale_ref
  219.9 0.0 copy-start.10
  219.9 103.9 %grads.1 = (f32[4,160,320]{2,1,0:T(8,128)}, f32[2,160,320]{2,1,0:T(8,128)}, f32[256,1280]{1,0:T(8,128)}, f32[6,8,1280]{2,1,0:T(8,128)}, f32[6,8,320]{2,1,0:T(8,1...) custom-call(bf16[4,256,1280]{2,1,0:T(8,128)(2,1)} %get-tuple-element, ...), custom_call_target="tpu_custom_call" | custom-call | tf_op jit(solution)/shard_map/grads/pallas_call | solution.py:1120
  323.9 0.7 reshape.74
  324.6 0.0 copy-done.10
  324.6 0.0 copy-start.7
  324.6 1.2 multiply_subtract_fusion.2
  325.8 2.5 fusion.1
  328.3 0.0 copy-start.1
  328.3 0.0 copy-start.2
  328.3 0.0 copy-start.4
  328.3 0.0 copy-start.8
  328.4 3.1 multiply_subtract_fusion
  331.4 0.0 copy-done.1
  331.4 0.0 copy-done.2
  331.4 0.0 copy-done.4
  331.4 1.0 maximum_subtract_fusion
  332.5 0.0 copy-done.7
  332.5 0.0 copy-done.8
  332.5 0.6 multiply_subtract_fusion.1
  333.1 9.7 %close.1 = f32[6,320,1280]{2,1,0:T(8,128)} custom-call(f32[6,320,1280]{2,1,0:T(8,128)} %get-tuple-element.65.m_ref, f32[6,8,320]{2,1,0:T(8,128)} %get-tuple-element.64.right_ref, f32[6,8,1280]{2,1,0:T(8,128)} %get-tuple-element.63.basis_ref), custom_call_target="tpu_custom_call" | custom-call | tf_op jit(solution)/shard_map/close/pallas_call | solution.py:1163
  342.8 0.0 copy-start
  342.8 2.0 copy.39
  344.9 0.0 copy-start.5
  344.9 0.0 copy-start.3
  344.9 2.5 copy.40
  347.4 0.0 copy-done
  347.4 0.9 copy.41
  348.3 0.0 copy-done.5
  348.3 0.8 copy.42
  349.1 0.0 copy-done.3
  349.1 0.6 copy.43
  (4 shorter events, 0.1 us)
Async XLA Ops:
  0.6 3.5 %copy-start.9 = (f32[80]{0:T(128)S(1)}, f32[80]{0:T(128)}, u32[]{:S(2)}) copy-start(f32[80]{0:T(128)} %param.21) | copy-start | bytes 964
  0.7 4.1 %copy-start.11 = (s32[1,8]{1,0:T(1,128)S(1)}, s32[1,8]{1,0:T(1,128)}, u32[]{:S(2)}) copy-start(s32[1,8]{1,0:T(1,128)} %param.16) | copy-start | bytes 100
  158.9 59.3 %copy-start.6 = (f32[2,1280]{1,0:T(2,128)S(1)}, f32[2,1280]{1,0:T(2,128)}, u32[]{:S(2)}) copy-start(f32[2,1280]{1,0:T(2,128)} %gain_ref.1) | copy-start | bytes 30724
  219.9 104.7 %copy-start.10 = (f32[80]{0:T(128)S(1)}, f32[80]{0:T(128)}, u32[]{:S(2)}) copy-start(f32[80]{0:T(128)} %param.25) | copy-start | bytes 964
  324.6 7.9 %copy-start.7 = (f32[2,1280]{1,0:T(2,128)}, f32[2,1280]{1,0:T(2,128)S(1)}, u32[]{:S(2)}) copy-start(f32[2,1280]{1,0:T(2,128)S(1)} %reshape.74) | copy-start | bytes 30724
  328.3 3.1 copy-start.1
  328.3 3.1 copy-start.2
  328.3 3.1 copy-start.4
  328.3 4.1 %copy-start.8 = (f32[2,1280]{1,0:T(2,128)S(1)}, f32[2,1280]{1,0:T(2,128)}, u32[]{:S(2)}) copy-start(f32[2,1280]{1,0:T(2,128)} %param.24) | copy-start | bytes 30724
  342.8 4.6 %copy-start = (f32[4,160,320]{2,1,0:T(8,128)S(1)}, f32[4,160,320]{2,1,0:T(8,128)}, u32[]{:S(2)}) copy-start(f32[4,160,320]{2,1,0:T(8,128)} %get-tuple-element.95) | copy-start | bytes 2457604
  344.9 3.5 copy-start.5
  344.9 4.2 %copy-start.3 = (f32[6,8,320]{2,1,0:T(8,128)S(1)}, f32[6,8,320]{2,1,0:T(8,128)}, u32[]{:S(2)}) copy-start(f32[6,8,320]{2,1,0:T(8,128)} %get-tuple-element.64.right_ref) | copy-start | bytes 184324

commit v4 on v3

--- a/solution.py
+++ b/solution.py
@@ -90,6 +90,15 @@
             def _(way=way):
                 self.copy(self.slot(hop, way), hop, way).start()
 
+    def send_toward(self, hop, middle):
+        low = self.me < self.n // 2
+        for way in (0, 1):
+            toward = low if way == 0 else jnp.logical_not(low)
+
+            @pl.when(self.goes(hop, way) & (toward if middle else jnp.logical_not(toward)))
+            def _(way=way):
+                self.copy(self.slot(hop, way), hop, way).start()
+
     def take(self, hop, ways=(0, 1)):
         for way in ways:
 
@@ -216,14 +225,13 @@
 
 
 def front_kernel(
-    dims, n_data, x_ref, g_ref, w_ref, gain_ref, c_ref, st_ref,
-    n1_ref, q_ref, k_ref, v_ref, lse_ref, oc_ref, wq_out, wt_out, g_near, n2_near, out_ref, dh_ref, n2_ref, dhb_ref, dgain_ref,
-    xbuf, wf, wpad, mask, opad, of_ref, h_ref, acc, dn2, zs, zr, ws, wr, gs, gr, ns, nr, as_, ar, os_, *plane_sems,
+    dims, n_data, x_ref, g_ref, win_ref, wo_ref, wd_ref, gain_ref, c_ref, st_ref,
+    n1_out, q_out, k_out, v_out, lse_out, oc_out, wq_out, wt_out, g_near, n2_near, out_ref, dh_ref, n2_ref, dhb_ref, dgain_ref,
+    n1_ref, q_ref, k_ref, v_ref, lse_ref, oc_ref, xbuf, wf, wpad, mask, opad, of_ref, h_ref, acc, dn2, zs, zr, ws, wr, gs, gr, ns, nr, as_, ar, os_, ko, *plane_sems,
 ):
     n, rows, heads, span = dims
-    hops_g = near_hops(n)
     me = lax.axis_index("mp")
-    cols = w_ref.shape[2]
+    cols = win_ref.shape[2]
     width = x_ref.shape[1]
     greet(line_peers(n, me) + data_peers(n_data))
     gather = LineGather(n, me, own_then(x_ref, xbuf), xbuf, zs, zr)
@@ -242,14 +250,18 @@
     lines = Weights(n, me, None, None, ws, wr)
     gather_g = LineGather(n, me, own_then(g_ref, g_near), g_near, gs, gr)
     gather_n = LineGather(n, me, own_then(n2_ref, n2_near), n2_near, ns, nr)
+    for k in range(3):
+        place(n)[k] = win_ref[k].astype(BF16)
+    place(me)[0] = wo_ref[...].astype(BF16)
+    place(me)[1] = win_ref[3].astype(BF16)
+    place(me)[2] = wd_ref[...].astype(BF16)
+    lines.send(0)
     gather.send(0)
-    place(n)[...] = w_ref[0:3]
-    place(me)[...] = w_ref[3:6]
     whole.stage(0, n)
-    lines.send(0)
-    whole.stage(0, me)
     sel = spread(cols, heads)
     xbuf[me] = x_ref[...]
+    k_ref[...] = jnp.zeros_like(k_ref)
+    v_ref[...] = jnp.zeros_like(v_ref)
 
     def matrix(k, m):
         value = wf[k, m]
@@ -257,19 +269,49 @@
             return value.astype(F32).reshape(width, cols).astype(BF16)
         return value.reshape(width, cols)
 
+    def arrivals(hop, do):
+        def one(way, _):
+            slot = me - hop + 2 * hop * way
+
+            @pl.when((slot >= 0) & (slot < n))
+            def _():
+                do(slot)
+
+            return 0
+
+        lax.fori_loop(0, 2, one, 0)
+
+    def forward(stage, hop):
+        if 1 <= hop < n:
+            arrivals(hop, lambda slot: whole.stage(stage, slot))
+
     whole.stage(1, n)
+    whole.stage(0, me)
+    whole.stage(2, n)
+    whole.stage(3, n)
+    lines.relay(1)
+    gather.relay(1)
+    forward(0, 1)
     whole.stage(1, me)
-    whole.stage(2, n)
-    whole.stage(2, me)
-    whole.stage(3, n)
     for m in range(3):
         wpad[m] = nn(matrix(n, m), sel).astype(BF16)
+
+    def keep_n1(slot):
+        return pltpu.make_async_copy(n1_ref.at[slot], n1_out.at[slot], ko.at[slot])
+
+    kept = [
+        pltpu.make_async_copy(src, dst, ko.at[n + k])
+        for k, (src, dst) in enumerate(
+            ((q_ref, q_out), (k_ref, k_out), (v_ref, v_out), (lse_ref, lse_out), (oc_ref, oc_out))
+        )
+    ]
 
     def project(slot):
         x = xbuf[slot].astype(F32)
         scale = lax.rsqrt(jnp.mean(x * x, axis=-1, keepdims=True) + EPSILON)
         normed = (x * scale * gain_ref[0:1]).astype(BF16)
         n1_ref[slot] = normed
+        keep_n1(slot).start()
         at = block_rows(slot, rows)
         for m, ref in enumerate((q_ref, k_ref, v_ref)):
             out = nn(normed, wpad[m])
@@ -281,33 +323,7 @@
 
     project(me)
 
-    def arrivals(hop, do):
-        def one(way, _):
-            slot = me - hop + 2 * hop * way
-
-            @pl.when((slot >= 0) & (slot < n))
-            def _():
-                do(slot)
-
-            return 0
-
-        lax.fori_loop(0, 2, one, 0)
-
-    def forward(stage, hop):
-        if 1 <= hop < n:
-            arrivals(hop, lambda slot: whole.stage(stage, slot))
-
-    for hop in range(1, n):
-        gather.relay(hop)
-        if hop < n - 1:
-            lines.relay(hop)
-            forward(0, hop)
-        forward(1, hop - 1)
-        arrivals(hop, project)
-        forward(2, hop - 1)
-    gather_g.send(0)
-
-    def chunk(i, _):
+    def chunk(i):
         first = jnp.maximum(i - (span - 1), 0)
         at, keys = block_rows(i, rows), pl.ds(pl.multiple_of(first * rows, rows), span * rows)
         q_pos = i * rows + lax.broadcasted_iota(jnp.int32, mask.shape, 0)
@@ -339,19 +355,44 @@
         def _():
             of_ref[me] = oc_ref[me]
 
-        @pl.when(i == 0)
-        def _():
-            lines.relay(n - 1)
-            forward(0, n - 1)
-
-        @pl.when(i == n // 2)
-        def _():
-            forward(1, n - 1)
-
-        return 0
-
-    lax.fori_loop(0, n, chunk, 0)
+    def ready(hop):
+        def one(e, _):
+            i = n - 1 - e
+            low = jnp.maximum(i - (span - 1), 0)
+            far = jnp.maximum(jnp.maximum(i - me, me - i), jnp.maximum(me - low, low - me))
+
+            @pl.when((far <= 1) if hop == 1 else (far == hop))
+            def _():
+                chunk(i)
+
+            return 0
+
+        lax.fori_loop(0, n, one, 0)
+
+    arrivals(1, project)
+    ready(1)
+    whole.stage(2, me)
+    for hop in range(2, n):
+        lines.relay(hop)
+        forward(0, hop)
+        forward(1, hop - 1)
+        if hop == n - 1:
+            forward(1, hop)
+            forward(2, hop - 1)
+        gather.relay(hop)
+        if hop == 2:
+            gather_g.send_toward(0, True)
+        arrivals(hop, project)
+        if hop == n - 1:
+            for copy in kept[:3]:
+                copy.start()
+        ready(hop)
+        if hop < n - 1:
+            forward(2, hop - 1)
+    gather_g.send_toward(0, False)
     forward(2, n - 1)
+    for copy in kept[3:]:
+        copy.start()
 
     def both(slot, _):
         whole.stage(3, slot)
@@ -362,8 +403,6 @@
     keep_t = pltpu.make_async_copy(wf.at[me], wt_out, os_.at[1])
     keep_q.start()
     keep_t.start()
-    for hop in range(1, hops_g):
-        gather_g.relay(hop)
     h_ref[...] = x_ref[...].astype(F32) + nt(of_ref[me], matrix(me, 0))
 
     def outward(off, _):
@@ -406,9 +445,9 @@
     dh = g_ref[...].astype(F32) + scale * (du - unit * jnp.mean(du * unit, axis=-1, keepdims=True))
     dh_ref[...] = dh
     dhb_ref[...] = dh.astype(BF16)
-    gather_g.take(hops_g)
+    gather_g.take(1)
     gather_n.take(1)
-    gather_g.finish(0, hops_g)
+    gather_g.finish(0, 1)
     gather_n.finish(0, 1)
     gather.finish()
     lines.finish()
@@ -420,12 +459,16 @@
     lax.fori_loop(0, n + 1, sent, 0)
     keep_q.wait()
     keep_t.wait()
-
-
-def front(dims, x, g, shards, gains, c_row, starts):
+    for copy in kept:
+        copy.wait()
+    for slot in range(n):
+        keep_n1(slot).wait()
+
+
+def front(dims, x, g, w_in, w_out, w_down, gains, c_row, starts):
     n, rows, heads, span = dims
     n_data = lax.axis_size("dp")
-    own_rows, cols = shards.shape[1:]
+    own_rows, cols = w_in.shape[1:]
     width = x.shape[1]
     count = n * rows
     ys, xs = plane(n_data)
@@ -448,9 +491,13 @@
             own, own,
             jax.ShapeDtypeStruct((1, width), F32),
         ),
-        in_specs=vmem(6),
-        out_specs=vmem(6) + [pl.BlockSpec(memory_space=pl.ANY)] * 4 + vmem(5),
+        in_specs=vmem(8),
+        out_specs=[pl.BlockSpec(memory_space=pl.ANY)] * 10 + vmem(5),
         scratch_shapes=[
+            pltpu.VMEM((n, rows, width), BF16),
+            *[pltpu.VMEM((heads, count, LANE), BF16)] * 3,
+            pltpu.VMEM((heads, count, 1), F32),
+            pltpu.VMEM((n, rows, cols), BF16),
             pltpu.VMEM((n, rows, width), BF16),
             pltpu.VMEM((n + 1, *kept.shape), BF16),
             pltpu.VMEM((3, width, heads * LANE), BF16),
@@ -459,29 +506,37 @@
             pltpu.VMEM((n, rows, cols), BF16),
             pltpu.VMEM((rows, width), F32), pltpu.VMEM((rows, width), F32), pltpu.VMEM((rows, width), F32),
             *line_sems(n), *line_sems(n), *line_sems(n), *line_sems(n),
-            sem((n,)), sem((n,)), sem((2,)),
+            sem((n,)), sem((n,)), sem((2,)), sem((n + 5,)),
             *PlaneGather.sems(n_data, n + 1),
         ],
         compiler_params=params(1),
         name="front",
-    )(x, g, shards, gains, c_row, starts)
+    )(x, g, w_in, w_out, w_down, gains, c_row, starts)
 
 
 def back_kernel(
-    dims, q_ref, k_ref, v_ref, lse_ref, own_ref, c_ref, st_ref, w_hbm,
-    dx_ref, dc_ref, dhb_ref,
-    w_ref, wpad, mask, do_ref, dq_ref, dk_ref, dv_ref, zs, zr, w_sem,
+    dims, own_ref, c_ref, st_ref, q_hbm, k_hbm, v_hbm, lse_hbm, w_hbm, g_near,
+    dx_ref, dc_ref, dhb_out, g_mid,
+    q_ref, k_ref, v_ref, lse_ref, dhb_ref, w_ref, wpad, mask, do_ref, dq_ref, dk_ref, dv_ref, zs, zr, gs, gr, w_sem, ko,
 ):
     n, rows, heads, span = dims
     me = lax.axis_index("mp")
-    take_w = pltpu.make_async_copy(w_hbm.at[0], w_ref, w_sem)
-    take_w.start()
+    takes = [
+        pltpu.make_async_copy(src, dst, w_sem.at[k])
+        for k, (src, dst) in enumerate(
+            ((w_hbm.at[0], w_ref), (q_hbm, q_ref), (k_hbm, k_ref), (v_hbm, v_ref), (lse_hbm, lse_ref))
+        )
+    ]
+    for copy in takes:
+        copy.start()
     greet(line_peers(n, me))
     gather = LineGather(n, me, own_then(own_ref, dhb_ref), dhb_ref, zs, zr)
     gather.send(0)
+    gather_g = LineGather(n, me, lambda hop, slot: g_near.at[slot], g_mid, gs, gr)
     dhb_ref[me] = own_ref[...]
     sel = spread(w_ref.shape[1], heads)
-    take_w.wait()
+    for copy in takes:
+        copy.wait()
     wpad[...] = nn(w_ref[...], sel).astype(BF16)
     dk_ref[...] = jnp.zeros_like(dk_ref)
     dv_ref[...] = jnp.zeros_like(dv_ref)
@@ -491,7 +546,11 @@
         wide = jnp.concatenate([ref[h, at, :].astype(BF16) for h in range(heads)], axis=1)
         return nt(wide, sel).astype(BF16)
 
+    def keep(i):
+        return pltpu.make_async_copy(dhb_ref.at[i], dhb_out.at[i], ko.at[i])
+
     def chunk(i):
+        keep(i).start()
         first = jnp.maximum(i - (span - 1), 0)
         at, keys = block_rows(i, rows), pl.ds(pl.multiple_of(first * rows, rows), span * rows)
         q_pos = i * rows + lax.broadcasted_iota(jnp.int32, mask.shape, 0)
@@ -537,6 +596,8 @@
         return 0
 
     lax.fori_loop(0, 2 * n - 1, event, 0)
+    if n > 2:
+        gather_g.send(1)
 
     def close(i, _):
         at = block_rows(i, rows)
@@ -546,21 +607,32 @@
 
     lax.fori_loop(0, n, close, 0)
     gather.finish()
-
-
-def back(dims, q, k, v, lse, dhb, c_row, starts, w_tail):
+    if n > 2:
+        gather_g.take(2)
+        gather_g.finish(1, 2)
+    for i in range(n):
+        keep(i).wait()
+
+
+def back(dims, q, k, v, lse, dhb, c_row, starts, w_tail, g_near):
     n, rows, heads, span = dims
     width, cols = w_tail.shape[1:]
+    every = jax.ShapeDtypeStruct((n, rows, width), BF16)
+    sem = pltpu.SemaphoreType.DMA
+    anywhere = pl.BlockSpec(memory_space=pl.ANY)
     return pl.pallas_call(
         functools.partial(back_kernel, dims),
         out_shape=(
             jax.ShapeDtypeStruct((3, n, rows, cols), BF16),
             jax.ShapeDtypeStruct((1, LANE), F32),
-            jax.ShapeDtypeStruct((n, rows, width), BF16),
+            every, every,
         ),
-        in_specs=vmem(7) + [pl.BlockSpec(memory_space=pl.ANY)],
-        out_specs=vmem(3),
+        in_specs=vmem(3) + [anywhere] * 6,
+        out_specs=vmem(2) + [anywhere] * 2,
         scratch_shapes=[
+            *[pltpu.VMEM((heads, n * rows, LANE), BF16)] * 3,
+            pltpu.VMEM((heads, n * rows, 1), F32),
+            pltpu.VMEM((n, rows, width), BF16),
             pltpu.VMEM((width, cols), BF16),
             pltpu.VMEM((width, heads * LANE), BF16),
             pltpu.VMEM((rows, span * rows), F32),
@@ -568,12 +640,12 @@
             pltpu.VMEM((heads, rows, LANE), BF16),
             pltpu.VMEM((heads, n * rows, LANE), F32),
             pltpu.VMEM((heads, n * rows, LANE), F32),
-            *line_sems(n),
-            pltpu.SemaphoreType.DMA,
+            *line_sems(n), *line_sems(n),
+            sem((5,)), sem((n,)),
         ],
         compiler_params=params(2),
         name="back",
-    )(q, k, v, lse, dhb, c_row, starts, w_tail)
+    )(dhb, c_row, starts, q, k, v, lse, w_tail, g_near)
 
 
 def halves(value):
@@ -842,7 +914,7 @@
 
 
 def grads_kernel(
-    dims, n_data, scaling, n1_ref, n2_ref, n2_near, dhb_ref, g_ref, g_near, dx_hbm, oc_hbm, wqkv_hbm, wtail_hbm,
+    dims, n_data, scaling, n1_ref, n2_ref, n2_near, dhb_ref, g_ref, g_near, g_mid, dx_hbm, oc_hbm, wqkv_hbm, wtail_hbm,
     err_ref, x_ref, dh_ref, gain_ref, dgain2_ref, dscale_ref, ft_ref,
     gin_sum, gout_sum, gin_ref, basis_ref, right_ref, small_ref, m_out, n2_far, g_far,
     abuf, dx_ref, wbuf, sbuf, lbuf, m_ref, srecv, szrecv,
@@ -884,37 +956,41 @@
     ex_small = Exchange("dp", n_data, lambda peer: srecv.at[mine], srecv, g_s, g_r)
     ex_small_line = Exchange("mp", n, lambda peer: szrecv.at[me], szrecv, gz_s, gz_r)
 
-    def follow(own, near, far, hops):
-        def source(hop, slot):
-            return own if hop == 0 else near.at[slot] if hop <= hops else far.at[slot]
-
-        return source
-
-    gather_n = LineGather(n, me, follow(n2_ref, n2_near, n2_far, 1), n2_far, nts, ntr)
-    gather_g = LineGather(n, me, follow(g_ref, g_near, g_far, hops_g), g_far, gts, gtr)
-
-    def bring(step):
-        for gather, hops in ((gather_g, hops_g), (gather_n, 1)):
-            hop = hops + step
-            if step == 0 and hop < n - 1:
-                gather.send(hop)
-            elif step > 0 and hop <= n - 1:
-                gather.relay(hop)
-
-    bring(0)
-
-    def pieces(own, near, far, hops, slot_of, sems, do):
+    def follow(near, far, hops):
+        return lambda hop, slot: near.at[slot] if hop <= hops else far.at[slot]
+
+    gather_n = LineGather(n, me, follow(n2_near, n2_far, 1), n2_far, nts, ntr)
+    gather_g = LineGather(n, me, follow(g_mid, g_far, hops_g), g_far, gts, gtr)
+
+    def bring(step, which):
+        gather, hops = ((gather_n, 1), (gather_g, hops_g))[which]
+        hop = hops + step
+        if step == 0 and hop < n - 1:
+            gather.send(hop)
+        elif step > 0 and hop < n - 1:
+            gather.relay(hop)
+
+    bring(0, 0)
+
+    def away(i):
+        return jnp.maximum(i - me, me - i)
+
+    def take_inputs(far, do):
         for i in range(n):
-            away = jnp.maximum(i - me, me - i)
-            for src, hit in ((own, away == 0), (near.at[i], (away >= 1) & (away <= hops)), (far.at[i], away > hops)):
+            d = away(i)
+            if far:
+                cases = ((0, n2_far, d > 1), (1, g_mid, d == 2), (1, g_far, d > 2))
+            else:
+                cases = ((0, n2_near, d == 1), (1, g_near, d == 1))
+            for k, src, hit in cases:
 
                 @pl.when(hit)
-                def _(src=src, i=i):
-                    do(pltpu.make_async_copy(src, abuf.at[slot_of, i], sems.at[i]))
-
-    def take_inputs(do):
-        pieces(n2_ref, n2_near, n2_far, 1, 0, ns_, do)
-        pieces(g_ref, g_near, g_far, hops_g, 1, gs_, do)
+                def _(k=k, src=src, i=i):
+                    do(pltpu.make_async_copy(src.at[i], abuf.at[k, i], (ns_, gs_)[k].at[i]))
+
+        if not far:
+            do(pltpu.make_async_copy(n2_ref, abuf.at[0, me], ns_.at[me]))
+            do(pltpu.make_async_copy(g_ref, abuf.at[1, me], gs_.at[me]))
 
 
     def own(e, _):
@@ -968,14 +1044,24 @@
                 copy(i, way).start()
 
     launch()
-
-    def hidden(i, _):
+    bring(0, 1)
+
+    def hidden(i):
         gate = nn(abuf[0, i], wbuf[1])
         sig = 1.0 / (1.0 + jnp.exp(-gate))
         dx_ref[0, i] = (gate * sig).astype(BF16)
         dz = nn(abuf[1, i], wbuf[2])
         dx_ref[1, i] = (dz * (sig * (1.0 + gate * (1.0 - sig)))).astype(BF16)
-        return 0
+
+    def hiddens(far):
+        def one(i, _):
+            @pl.when((away(i) > 1) if far else (away(i) <= 1))
+            def _():
+                hidden(i)
+
+            return 0
+
+        lax.fori_loop(0, n, one, 0)
 
     def flat(value):
         return value.reshape(n * rows, value.shape[-1])
@@ -993,28 +1079,32 @@
     take_n1.wait()
     lax.fori_loop(0, 3, inputs, 0)
     take_oc.start()
-    bring(1)
     take_dhb.wait()
     take_oc.wait()
     weight(4, gb_1, 3, abuf[0], dx_ref[2])
     chain_1.start()
     scatter_1.start(scatter_1.copies_core())
+    take_inputs(False, lambda c: c.start())
+    bring(1, 0)
+    bring(1, 1)
     relay(1)
     chain_1.along_line()
     scatter_1.sum_core()
     scatter_1.start(scatter_1.copies_one())
-    chain_1.spread_out()
-    chain_1.orthonormal()
+    take_tail.wait()
+    take_inputs(False, lambda c: c.wait())
+    hiddens(False)
     for r in range(2, n - 1):
         relay(r)
-        bring(r)
-    bring(n - 1)
-    take_inputs(lambda c: c.start())
+        bring(r, 0)
+        bring(r, 1)
+    gather_n.take(n - 1)
+    gather_g.take(n - 1)
+    take_inputs(True, lambda c: c.start())
     scatter_1.sum_one()
     scatter_1.start(scatter_1.copies_two())
-    take_tail.wait()
-    take_inputs(lambda c: c.wait())
-    lax.fori_loop(0, n, hidden, 0)
+    take_inputs(True, lambda c: c.wait())
+    hiddens(True)
 
     def late(k, _):
         weight(3 + 2 * k, gb_2, k, abuf[k], dx_ref[1 - k])
@@ -1025,6 +1115,7 @@
     scatter_2.start(scatter_2.copies_core())
     for m in range(6):
         save(m).start()
+    chain_1.spread_out()
 
 
     @pl.when(me > 0)
@@ -1055,8 +1146,9 @@
     scatter_2.sum_core()
     scatter_2.start(scatter_2.copies_one())
     chain_2.spread_out()
-    du = grad * gain_ref[...]
+    du = grad * gain_ref[0:1]
     gin_ref[...] = dh_ref[...] + scale * (du - unit * jnp.mean(du * unit, axis=-1, keepdims=True))
+    chain_1.orthonormal()
     ex_small.arrive()
     szrecv[me] = total_of(srecv, n_data)
     ex_small_line.start()
@@ -1147,28 +1239,73 @@
     )(*hbm, x, dh, gain, dgain2, dscale, ft)[:7]
 
 
-def close_kernel(m_ref, right_ref, basis_ref, out_ref):
-    right, basis = right_ref[0], basis_ref[0]
-    (rh, rl), (bh, bl) = halves(right), halves(basis)
-    left = jnp.concatenate([rh, rl, rh], axis=0)
-    out_ref[0] = m_ref[0] - tn(left, jnp.concatenate([bh, bh, bl], axis=0))
-
-
-def close(m, right, basis):
+def outer(a, b):
+    (ah, al), (bh, bl) = halves(a), halves(b)
+    left = jnp.concatenate([ah.astype(F32), al.astype(F32), ah.astype(F32)], axis=0).astype(BF16)
+    right = jnp.concatenate([bh.astype(F32), bh.astype(F32), bl.astype(F32)], axis=0).astype(BF16)
+    return tn(left, right)
+
+
+def close_kernel(
+    m_ref, right_ref, basis_ref, mine_ref, mom_in_ref, w_in_ref, mom_out_ref, w_out_ref, w_down_ref,
+    gin_ref, out_ref, gw_ref, gw2_ref,
+    err_ref, new_in_ref, mom_in_new_ref, new_out_ref, mom_out_new_ref, gin_out, out_out, gw_out, gw2_out,
+):
+    k = pl.program_id(0)
+    right, mine = right_ref[0], mine_ref[0]
+    err_ref[0] = m_ref[0] - outer(right, basis_ref[0])
+    gin_out[...] = gin_ref[...]
+    out_out[...] = out_ref[...]
+    gw_out[...] = gw_ref[...]
+    gw2_out[...] = gw2_ref[...]
+    step = outer(mine, right)
+
+    @pl.when(k < 4)
+    def _():
+        moment = MOMENTUM * mom_in_ref[0] + step
+        mom_in_new_ref[0] = moment
+        new_in_ref[0] = w_in_ref[0] - RATE * moment
+
+    for index, ref in ((4, w_out_ref), (5, w_down_ref)):
+
+        @pl.when(k == index)
+        def _(ref=ref):
+            moment = MOMENTUM * mom_out_ref[0] + step
+            mom_out_new_ref[0] = moment
+            new_out_ref[0] = ref[...] - RATE * moment
+
+
+def close(m, right, basis, mine, mom_in, w_in, mom_out, w_out, w_down, grad_input, output, grad_in, grad_out):
     cols, width = m.shape[1:]
+    own_rows = w_in.shape[1]
+    quarter = grad_input.shape[0] // 4
 
     def spec(*shape):
         return pl.BlockSpec((1, *shape), lambda i: (i, 0, 0))
+
+    into = pl.BlockSpec((1, own_rows, cols), lambda i: (jnp.minimum(i, 3), 0, 0))
+    out = pl.BlockSpec((1, own_rows, cols), lambda i: (jnp.maximum(i - 4, 0), 0, 0))
+    whole = pl.BlockSpec((own_rows, cols), lambda i: (0, 0))
+    part = pl.BlockSpec((quarter, width), lambda i: (jnp.minimum(i, 3), 0))
+
+    def like(x):
+        return jax.ShapeDtypeStruct(x.shape, x.dtype)
 
     return pl.pallas_call(
         close_kernel,
         grid=(6,),
-        out_shape=jax.ShapeDtypeStruct(m.shape, F32),
-        in_specs=[spec(cols, width), spec(8, cols), spec(8, width)],
-        out_specs=spec(cols, width),
+        out_shape=(
+            like(m), like(w_in), like(mom_in), like(mom_out), like(mom_out),
+            like(grad_input), like(output), like(grad_in), like(grad_out),
+        ),
+        in_specs=[
+            spec(cols, width), spec(8, cols), spec(8, width), spec(8, own_rows), into, into, out,
+            whole, whole, part, part, into, out,
+        ],
+        out_specs=[spec(cols, width), into, into, out, out, part, part, into, out],
         compiler_params=params(),
         name="close",
-    )(m, right, basis)
+    )(m, right, basis, mine, mom_in, w_in, mom_out, w_out, w_down, grad_input, output, grad_in, grad_out)
 
 
 def on_device(
@@ -1188,7 +1325,6 @@
     span = min(n, -(-(longest - 1) // rows) + 1)
     dims = (n, rows, heads, span)
 
-    shards = jnp.concatenate([w_in[:3], w_attn_out.T[None], w_in[3:], w_down.T[None]], axis=0).astype(BF16)
     ends = jnp.cumsum(doc_lengths[0])
     position = jnp.arange(count, dtype=jnp.int32)[:, None]
     starts = jnp.max(jnp.where(ends[None, :] <= position, ends[None, :], 0), axis=1, keepdims=True)
@@ -1196,29 +1332,27 @@
     c_row = jnp.tile(jnp.pad(factor, (0, LANE - HD)), heads)[None]
 
     n1, q, k, v, lse, oc, wqkv, w_tail, g_near, n2_near, output, dh, n2, dhb, dgain2 = front(
-        dims, activations, cotangent, shards, gains, c_row, starts
+        dims, activations, cotangent, w_in, w_attn_out.T, w_down.T, gains, c_row, starts
     )
     wqkv, w_tail = wqkv.reshape(3, width, cols), w_tail.reshape(3, width, cols)
-    dx, dc, dhb = back(dims, q, k, v, lse, dhb, c_row, starts, w_tail)
-    grad_scale_local = dc[0, :HD] / factor * (SCALE_BASE / math.sqrt(HD)) * jax.nn.sigmoid(scale_param)
-    dscale = jnp.pad(grad_scale_local, (0, LANE - HD))[None]
-    hbm = (n1, n2, n2_near, dhb, cotangent, g_near, dx, oc, wqkv, w_tail, error_buffer[0])
+    dx, dc, dhb, g_mid = back(dims, q, k, v, lse, dhb, c_row, starts, w_tail, g_near)
+    hbm = (n1, n2, n2_near, dhb, cotangent, g_near, g_mid, dx, oc, wqkv, w_tail, error_buffer[0])
     grad_in, out_sum, grad_input, basis, right, small, stored = grads(
-        dims, scaling, hbm, activations, dh, gains[:1], dgain2, dscale, jnp.swapaxes(factors, 1, 2)
+        dims, scaling, hbm, activations, dh, gains, dgain2, dc, jnp.swapaxes(factors, 1, 2)
     )
-    grad_out = jnp.swapaxes(out_sum, 1, 2)
-    error_new = close(stored, right, basis)[None]
+    mine = lax.dynamic_slice_in_dim(basis, my_data * own_rows, own_rows, 2)
+    error_new, new_in, mom_in_new, new_out, mom_out_new, grad_input, output, grad_in, grad_out = close(
+        stored, right, basis, mine, mom_in, w_in, jnp.swapaxes(mom_out, 1, 2), w_attn_out.T, w_down.T,
+        grad_input, output, grad_in, out_sum,
+    )
+    error_new = error_new[None]
+    new_out, mom_out_new, grad_out = (jnp.swapaxes(x, 1, 2) for x in (new_out, mom_out_new, grad_out))
     tiles = width // LANE
     small = small.reshape(-1, LANE)
     grad_gain = small[: 2 * tiles].reshape(2, width)
-    grad_scale = small[2 * tiles, :HD]
-    mine_basis = lax.dynamic_slice_in_dim(basis, my_data * own_rows, own_rows, 2)
-    mine = jnp.einsum("krd,krc->kdc", mine_basis, right, precision=HIGHEST)
+    slope = (SCALE_BASE / math.sqrt(HD)) * jax.nn.sigmoid(scale_param) / factor
+    grad_scale = small[2 * tiles, :HD] * slope
     right = jnp.swapaxes(right, 1, 2)
-    mom_in_new = MOMENTUM * mom_in + mine[:4]
-    new_in = w_in - RATE * mom_in_new
-    mom_out_new = MOMENTUM * mom_out + jnp.swapaxes(mine[4:], 1, 2)
-    new_out = jnp.stack([w_attn_out, w_down]) - RATE * mom_out_new
     mom_gain_new = MOMENTUM * mom_gain + grad_gain
     new_gain = gains - RATE * mom_gain_new
     mom_scale_new = MOMENTUM * mom_scale + grad_scale

time: 350 us -> 294 us (0.84)
  Pallas kernels: 326 us -> 284 us
  other arithmetic: 10.2 us -> 3.41 us
  local copies, waits for them, and re-layouts: 10.5 us -> 4.77 us
    pallas_call x1, Pallas kernels: 153 us -> 122 us  [front(): pl.pallas_call(functools.partial(front_kernel, dims, n_data), out_shape=(...]
    pallas_call x1, Pallas kernels: 104 us -> 85.3 us  [grads(): pl.pallas_call(functools.partial(grads_kernel, dims, n_data, scaling), ou...]
    unnamed x29 -> x11, local copies, waits for them, and re-layouts: 6.98 us -> 1.54 us
    pallas_call x1, Pallas kernels: 59.2 us -> 63.6 us  [back(): pl.pallas_call(functools.partial(back_kernel, dims), out_shape=(jax.Shape...]
    sub x2 -> x0, other arithmetic: 4.11 us -> none  [the longest x1 3.06 us: on_device(): new_in = w_in - RATE * mom_in_new]
    pallas_call x1, Pallas kernels: 9.7 us -> 13.6 us  [close(): pl.pallas_call(close_kernel, grid=(6,), out_shape=(like(m), like(w_in), l...]
where the time goes in v4:
time: 294 us; the launch traced here: 293 us
  Pallas kernels  284 us (97%)
  local copies, waits for them, and re-layouts  4.77 us (2%)
  other arithmetic  3.41 us (1%)
    pallas_call x1, Pallas kernels, front(): pl.pallas_call(functools.partial(front_kernel, dims, n_data), out_shape=(...  122 us
    pallas_call x1, Pallas kernels, grads(): pl.pallas_call(functools.partial(grads_kernel, dims, n_data, scaling), ou...  85.3 us
    pallas_call x1, Pallas kernels, back(): pl.pallas_call(functools.partial(back_kernel, dims), out_shape=(jax.Shape...  63.6 us
    pallas_call x1, Pallas kernels, close(): pl.pallas_call(close_kernel, grid=(6,), out_shape=(like(m), like(w_in), l...  13.6 us

profile of v4, /device:TPU:0, one launch (start us, length us, event | category | flops | bytes accessed | tf_op | source)
XLA Modules:
  0.0 293.4 jit_solution(13457608922198337605)
XLA Ops:
  0.6 0.8 reduce-window.8
  1.5 0.1 select_reduce_fusion
  1.6 1.0 copy.32.st_ref
  2.6 0.7 fusion
  3.3 0.6 tile.2
  3.9 122.0 %front.1 = (bf16[4,256,1280]{2,1,0:T(8,128)(2,1)}, bf16[4,1024,128]{2,1,0:T(8,128)(2,1)}, bf16[4,1024,128]{2,1,0:T(8,128)(2,1)}, bf16[4,1024,128]{2,1,0:T(8,128)...) custom-call(bf16[256,1280]{1,0:T(8,128)(2,1)} %x_ref.3, ...), custom_call_target="tpu_custom_call" | custom-call | tf_op jit(solution)/shard_map/front/pallas_call | solution.py:479
  125.9 63.6 %back.1 = (bf16[3,4,256,320]{3,2,1,0:T(8,128)(2,1)}, f32[1,128]{1,0:T(1,128)}, bf16[4,256,1280]{2,1,0:T(8,128)(2,1)}, bf16[4,256,1280]{2,1,0:T(8,128)(2,1)}) custom-call(bf16[256,1280]{1,0:T(8,128)(2,1)} %get-tuple-element.54.own_ref, f32[1,512]{1,0:T(1,128)} %bitcast.35, s32[1024,1]{1,0:T(8,128)} %copy.32.st_ref, ...), custom_call_target="tpu_custom_call" | custom-call | tf_op jit(solution)/shard_map/back/pallas_call | solution.py:623
  189.5 85.3 %grads.1 = (f32[4,160,320]{2,1,0:T(8,128)}, f32[2,160,320]{2,1,0:T(8,128)}, f32[256,1280]{1,0:T(8,128)}, f32[6,8,1280]{2,1,0:T(8,128)}, f32[6,8,320]{2,1,0:T(8,1...) custom-call(bf16[4,256,1280]{2,1,0:T(8,128)(2,1)} %get-tuple-element, ...), custom_call_target="tpu_custom_call" | custom-call | tf_op jit(solution)/shard_map/grads/pallas_call | solution.py:1212
  274.8 1.6 constant_dynamic-slice_fusion.mine_ref
  276.4 0.0 copy-start.2
  276.4 0.0 copy-start
  276.4 0.0 copy-start.3
  276.4 0.0 copy-start.4
  276.4 13.6 %close.1 = (f32[6,320,1280]{2,1,0:T(8,128)}, f32[4,160,320]{2,1,0:T(8,128)}, f32[4,160,320]{2,1,0:T(8,128)}, f32[2,160,320]{2,1,0:T(8,128)}, f32[2,160,320]{2,1,...) custom-call(f32[6,320,1280]{2,1,0:T(8,128)} %get-tuple-element.69.m_, ...), custom_call_target="tpu_custom_call" | custom-call | tf_op jit(solution)/shard_map/close/pallas_call | solution.py:1294
  290.0 0.0 copy-done.2
  290.0 0.0 copy-done
  290.0 0.0 copy-done.3
  290.0 0.0 copy-start.1
  290.0 0.6 multiply_subtract_fusion
  290.7 0.0 copy-done.4
  290.7 1.2 multiply_subtract_fusion.1
  291.9 1.5 copy.35
  293.4 0.0 copy-done.1
  (2 shorter events, 0.0 us)
Async XLA Ops:
  276.4 13.6 %copy-start.2 = (f32[3,8,128]{2,1,0:T(8,128)S(1)}, f32[3,8,128]{2,1,0:T(8,128)}, u32[]{:S(2)}) copy-start(f32[3,8,128]{2,1,0:T(8,128)} %get-tuple-element.80) | copy-start | bytes 36868
  276.4 13.6 %copy-start = (f32[2,1280]{1,0:T(2,128)S(1)}, f32[2,1280]{1,0:T(2,128)}, u32[]{:S(2)}) copy-start(f32[2,1280]{1,0:T(2,128)} %gain_ref.3) | copy-start | bytes 30724
  276.4 13.6 %copy-start.3 = (f32[2,1280]{1,0:T(2,128)S(1)}, f32[2,1280]{1,0:T(2,128)}, u32[]{:S(2)}) copy-start(f32[2,1280]{1,0:T(2,128)} %param.24) | copy-start | bytes 30724
  276.4 14.3 %copy-start.4 = (f32[80]{0:T(128)S(1)}, f32[80]{0:T(128)}, u32[]{:S(2)}) copy-start(f32[80]{0:T(128)} %param.21) | copy-start | bytes 964
  290.0 3.4 %copy-start.1 = (f32[2,1280]{1,0:T(2,128)}, f32[2,1280]{1,0:T(2,128)S(1)}, u32[]{:S(2)}) copy-start(f32[2,1280]{1,0:T(2,128)S(1)} %reshape.74) | copy-start | bytes 30724
